TPU v7x, 128 devices: a whole 4x4x4 slice. The times are simulated.
128 devices in a mesh: rows: 16 (over x, y_lo, core), dim: 8 (over y_hi, z).
Axes of the slice: x: 4, y: 4 (y_hi: 2, y_lo: 2; y = y_hi * 2 + y_lo), z: 4, core: 2. Of those that a mesh axis runs over, the one named last changes fastest.
Arguments:
- entity_table: float32 [524288, 512], P(('rows', 'dim')), may hold values from -2.5 to 2.5
- relations: float32 [822, 512], replicated, may hold values from -6 to 6
- thresholds: float32 [64], replicated, may hold values from 0.2 to 2
- head_ids: int32 [2048], replicated, may hold values from 0 to 524287
- rel_ids: int32 [2048], replicated, may hold values from 0 to 821
- thr_idx: int32 [2048], replicated, may hold values from 0 to 63
Outputs:
- serving_table: float32 [524288, 512], P('rows', 'dim')
- fraction: float32 [2048], P(('rows', 'dim'))
All inputs are finite; a program needn't handle non-finite values.
Results may differ from a plain program's by a relative error of at most 0.0011.
Values sent between devices are 32-bit elements; how exact they have to be, the bound alone decides.
No kernel may reach another device: no remote copies, remote signals or barrier semaphores. Data moves between devices by JAX's collectives and lax.ppermute only.
A program may use at most 128 MiB of HBM per device.

v0:
```python
import jax
import jax.numpy as jnp
from jax import lax
from jax.sharding import PartitionSpec as P

sharpness = 2.0


def cut_along(value, dim, length):
    lengths = value.shape
    parts = value.reshape(*lengths[:dim], length, lengths[dim] // length, *lengths[dim + 1 :])
    return jnp.moveaxis(parts, dim, 0)


def cut_rows(length, count):
    lap = length // count
    if lap >= 8:
        lap -= lap % 8
    return [lap * k for k in range(1, count)]


def joined_along(parts, dim):
    lengths = list(parts.shape[1:])
    lengths[dim] *= parts.shape[0]
    return jnp.moveaxis(parts, 0, dim).reshape(lengths)


def several_exchanges(value, axis, pieces, split_dim, concat_dim):
    parts = cut_along(value, split_dim, lax.axis_size(axis))
    cut = max(range(1, max(2, parts.ndim - 1)), key=lambda d: parts.shape[d])
    outs = []
    for slab in jnp.split(parts, cut_rows(parts.shape[cut], pieces), axis=cut):
        if slab.size:
            outs.append(lax.all_to_all(slab, axis, split_axis=0, concat_axis=0, tiled=True))
    return joined_along(jnp.concatenate(outs, axis=cut), concat_dim)


def pick_rows(table, head_ids, start):
    count = table.shape[0]
    local = head_ids - start
    owned = (local >= 0) & (local < count)
    picked = jnp.take(table, jnp.clip(local, 0, count - 1), axis=0)
    return jnp.where(owned[:, None], picked, jnp.zeros_like(picked))


def shards(entity_table, relations, thresholds, head_ids, rel_ids, thr_idx):
    local_rows = entity_table.shape[0]
    width = entity_table.shape[1]
    total_ents = local_rows * lax.axis_size("rows") * lax.axis_size("dim")
    serving = several_exchanges(entity_table, "dim", 2, 1, 0)
    start = (lax.axis_index("rows") * lax.axis_size("dim") + lax.axis_index("dim")) * local_rows
    partial_value = pick_rows(entity_table, head_ids, start)
    head_vecs = lax.psum(partial_value, ("rows", "dim"))
    query = (head_vecs * jnp.take(relations, rel_ids, axis=0)).astype(jnp.bfloat16)
    ent_low = entity_table.astype(jnp.bfloat16)
    level = jnp.take(thresholds, thr_idx)
    queries = query.shape[0]
    query_blocks = query.reshape(queries // 512, 512, width)
    level_blocks = level.reshape(queries // 512, 512)

    def score_block(pair):
        rows_q, rows_level = pair
        score = jnp.dot(rows_q, ent_low.T, preferred_element_type=jnp.float32)
        soft = jax.nn.sigmoid(sharpness * (score - rows_level[:, None]))
        return jnp.sum(soft, axis=1) * (1.0 / total_ents)

    partial_share = lax.map(score_block, (query_blocks, level_blocks)).reshape(queries)
    fraction = lax.psum_scatter(partial_share, ("rows", "dim"), scatter_dimension=0, tiled=True)
    return (serving, fraction)


def solution(mesh):
    placed = (P(("rows", "dim"), None), P(), P(), P(), P(), P())
    return jax.shard_map(
        shards,
        mesh=mesh,
        in_specs=placed,
        out_specs=(P("rows", "dim"), P(("rows", "dim"))),
        check_vma=False,
    )
```

profile of v0, /device:TPU:1, one launch (start us, length us, event | category | flops | bytes accessed | tf_op | source)
XLA Modules:
  0.0 349.4 jit_solution(9521090022698641144)
XLA Ops:
  7.2 9.0 %copy.12 = f32[4096,512]{0,1:T(8,128)} copy(f32[4096,512]{1,0:T(8,128)} %param.8) | data formatting | bytes 16777216 | tf_op args[0]
  16.2 7.9 %fusion.6 = (f32[8,2048,64]{1,2,0:T(8,128)}, f32[8,2048,64]{1,2,0:T(8,128)}) fusion(f32[8,4096,64]{1,2,0:T(8,128)} %bitcast.87), kind=kLoop, calls=%fused_computation.21 | loop fusion | bytes 16777216 | tf_op jit(solution)/shard_map/split | solution.py:32
  24.1 8.6 %all-to-all-start = ((f32[8,2048,64]{1,2,0:T(8,128)}), f32[8,2048,64]{1,2,0:T(8,128)}, u32[]{:S(2)}, u32[]{:S(2)}) async-start(f32[8,2048,64]{1,2,0:T(8,128)} %get-tuple-element.40), calls=%async_computation | async-start | bytes 8388608 | tf_op jit(solution)/shard_map/all_to_all | solution.py:34
  32.8 12.9 %gather_fusion = f32[2048,512]{1,0:T(8,128)} fusion(f32[4096,512]{1,0:T(8,128)} %param.8, s32[2048]{0:T(1024)S(1)} %fusion.5), kind=kCustom, calls=%fused_computation | custom fusion | bytes 8396800 | tf_op jit(solution)/shard_map/jit(_take)/gather | solution.py:42
  45.7 4.0 %select_select_fusion = f32[2048,512]{1,0:T(8,128)} fusion(f32[2048,512]{1,0:T(8,128)} %gather_fusion, pred[2048]{0:T(1024)(128)(4,1)S(1)} %get-tuple-element.43, pred[2048]{0:T(1024)(128)(4,1)S(1)} %get-tuple-element.42), kind=kLoop, calls=%fused_computation.11 | loop fusion | flops 2097152 | bytes 8392704 | tf_op jit(solution)/shard_map/jit(_where)/select_n | solution.py:43
  49.7 5.9 %convert_element_type.7 = bf16[4096,512]{1,0:T(8,128)(2,1)} convert(f32[4096,512]{1,0:T(8,128)} %param.8) | non-fusion elementwise | flops 2097152 | bytes 12582912 | tf_op jit(solution)/shard_map/convert_element_type | solution.py:55
  55.5 0.7 fusion.10
  56.2 0.7 fusion.8
  57.0 0.7 fusion.7
  57.7 0.7 fusion.9
  58.4 39.7 %select_select_fusion.1 = f32[2048]{0:T(1024)S(1)} fusion(s32[2048]{0:T(1024)S(1)} %copy-done.5, f32[]{:T(128)} %bitcast.7, f32[]{:T(128)} %bitcast.8, f32[]{:T(128)} %bitcast.9, f32[]{:T(128)} %bitcast.10, f32[]{:T(128)} %bitcast.11, f32[]{:T(128)} %bitcast.12, f32[]{:T(128)} %bitcast.13, f32[]{:T(128)} %bitcast.14, f32[]{:T(128)} %bitcast.15, f32[]{:T(128)} %bitcast.16, ...), kind=kLoop, calls=%fused_computation.15 | loop fusion | flops 272384 | bytes 16640 | tf_op jit(solution)/shard_map/jit(_take)/select_n | solution.py:56
  98.2 8.9 %gather_fusion.1 = f32[2048,512]{1,0:T(8,128)} fusion(f32[822,512]{1,0:T(8,128)S(1)} %copy-done, s32[2048]{0:T(1024)S(1)} %fusion.4), kind=kCustom, calls=%fused_computation.1 | custom fusion | bytes 8396800 | tf_op jit(solution)/shard_map/jit(_take)/gather | solution.py:54
  107.1 112.8 %all-reduce.3.cloned.1.call-done = f32[2048,512]{1,0:T(8,128)} async-done(((f32[2048,512]{1,0:T(8,128)}), f32[2048,512]{1,0:T(8,128)}) %all-reduce.3.cloned.1.call-update) | async-done | bytes 4194320 | tf_op jit(solution)/shard_map/psum | solution.py:53
  219.9 4.7 %multiply_convert_fusion = bf16[2048,512]{1,0:T(8,128)(2,1)} fusion(f32[2048,512]{1,0:T(8,128)} %all-reduce.3.cloned.1.call-done, f32[2048,512]{1,0:T(8,128)} %gather_fusion.1, pred[2048]{0:T(1024)(128)(4,1)S(1)} %compare_and_fusion), kind=kLoop, calls=%fused_computation.10 | loop fusion | flops 3145728 | bytes 10487808 | tf_op jit(solution)/shard_map/convert_element_type | solution.py:54
  224.6 4.7 %all-to-all-start.1 = ((f32[8,2048,64]{1,2,0:T(8,128)}), f32[8,2048,64]{1,2,0:T(8,128)}, u32[]{:S(2)}, u32[]{:S(2)}) async-start(f32[8,2048,64]{1,2,0:T(8,128)} %get-tuple-element.41), calls=%async_computation.1 | async-start | bytes 8388608 | tf_op jit(solution)/shard_map/all_to_all | solution.py:34
  229.4 22.9 %while.10 = (s32[]{:T(128)}, f32[4,512]{1,0:T(4,128)S(1)}, bf16[4,512,512]{2,1,0:T(8,128)(2,1)}, bf16[4096,512]{1,0:T(8,128)(2,1)}, f32[4,512]{1,0:T(4,128)S(1)}, /*index=5*/s32[]{:T(128)}, s32[]{:T(128)}) while((s32[]{:T(128)}, f32[4,512]{1,0:T(4,128)S(1)}, bf16[4,512,512]{2,1,0:T(8,128)(2,1)}, bf16[4096,512]{1,0:T(8,128)(2,1)}, ...), condition=%wide.region_3.4_spmd, body=%wide.region_1.3_spmd.sunk | while | flops 2160066560 | bytes 4735073 | solution.py:67
  229.4 5.6 %fusion.17 = f32[512]{0:T(512)S(1)} fusion(bf16[4096,512]{1,0:T(8,128)(2,1)} %get-tuple-element.156, f32[512]{0:T(512)S(1)} %bitcast.91, bf16[4,512,512]{2,1,0:T(8,128)(2,1)} %get-tuple-element.155, s32[]{:T(128)S(6)} %copy.20), kind=kOutput, calls=%fused_computation.3.clone.1 | convolution fusion | flops 2160066048 | bytes 4722692 | tf_op jit(solution)/shard_map/while/body/eval_jaxpr/dot_general | solution.py:63
  235.1 5.6 %fusion.17 = f32[512]{0:T(512)S(1)} fusion(bf16[4096,512]{1,0:T(8,128)(2,1)} %get-tuple-element.156, f32[512]{0:T(512)S(1)} %bitcast.91, bf16[4,512,512]{2,1,0:T(8,128)(2,1)} %get-tuple-element.155, s32[]{:T(128)S(6)} %copy.20), kind=kOutput, calls=%fused_computation.3.clone.1 | convolution fusion | flops 2160066048 | bytes 4722692 | tf_op jit(solution)/shard_map/while/body/eval_jaxpr/dot_general | solution.py:63
  240.9 5.6 %fusion.17 = f32[512]{0:T(512)S(1)} fusion(bf16[4096,512]{1,0:T(8,128)(2,1)} %get-tuple-element.156, f32[512]{0:T(512)S(1)} %bitcast.91, bf16[4,512,512]{2,1,0:T(8,128)(2,1)} %get-tuple-element.155, s32[]{:T(128)S(6)} %copy.20), kind=kOutput, calls=%fused_computation.3.clone.1 | convolution fusion | flops 2160066048 | bytes 4722692 | tf_op jit(solution)/shard_map/while/body/eval_jaxpr/dot_general | solution.py:63
  246.6 5.6 %fusion.17 = f32[512]{0:T(512)S(1)} fusion(bf16[4096,512]{1,0:T(8,128)(2,1)} %get-tuple-element.156, f32[512]{0:T(512)S(1)} %bitcast.91, bf16[4,512,512]{2,1,0:T(8,128)(2,1)} %get-tuple-element.155, s32[]{:T(128)S(6)} %copy.20), kind=kOutput, calls=%fused_computation.3.clone.1 | convolution fusion | flops 2160066048 | bytes 4722692 | tf_op jit(solution)/shard_map/while/body/eval_jaxpr/dot_general | solution.py:63
  252.4 81.6 %all-reduce = f32[2048]{0:T(1024)S(1)} all-reduce(f32[2048]{0:T(1024)S(1)} %bitcast.92), channel_id=2, replica_groups=mesh['rows'=16,'dim'=8] {'rows','dim'}, use_global_device_ids=true, to_apply=%region_4.5.clone | all-reduce | flops 2048 | bytes 16384
  334.0 0.6 dynamic-slice
  334.6 4.0 %maximum_bitcast_fusion = f32[8,8,8,4096]{3,2,1,0:T(8,128)S(1)} fusion(f32[8,2048,64]{1,2,0:T(8,128)} %all-to-all-done.1, f32[8,2048,64]{1,2,0:T(8,128)} %all-to-all-done), kind=kLoop, calls=%fused_computation.9 | loop fusion | flops 2097152 | bytes 16777216
  338.6 3.9 %copy.14 = f32[8,8,8,4096]{3,2,0,1:T(8,128)} copy(f32[8,8,8,4096]{3,2,1,0:T(8,128)S(1)} %maximum_bitcast_fusion) | data formatting | bytes 16777216 | tf_op jit(solution)/shard_map/reshape | solution.py:25
  (35 shorter events, 0.4 us)
Async XLA Ops:
  7.2 91.0 %copy-start = (f32[822,512]{1,0:T(8,128)S(1)}, f32[822,512]{1,0:T(8,128)}, u32[]{:S(2)}) copy-start(f32[822,512]{1,0:T(8,128)} %param.9) | copy-start | bytes 5050372
  24.1 8.7 %copy-start.4 = (s32[2048]{0:T(1024)S(1)}, s32[2048]{0:T(1024)}, u32[]{:S(2)}) copy-start(s32[2048]{0:T(1024)} %param.11) | copy-start | bytes 24580
  24.1 200.6 %all-to-all-start = ((f32[8,2048,64]{1,2,0:T(8,128)}), f32[8,2048,64]{1,2,0:T(8,128)}, u32[]{:S(2)}, u32[]{:S(2)}) async-start(f32[8,2048,64]{1,2,0:T(8,128)} %get-tuple-element.40), calls=%async_computation | async-start | bytes 8388608 | tf_op jit(solution)/shard_map/all_to_all | solution.py:34
  32.7 187.2 %all-reduce.3.cloned.1.call-start = ((), (), s32[]{:S(2)}) async-start(), calls=%async_computation.2 | async-start | bytes 8388608 | tf_op jit(solution)/shard_map/psum | solution.py:53
  49.7 5.9 %copy-start.2 = (f32[64]{0:T(128)S(1)}, f32[64]{0:T(128)}, u32[]{:S(2)}) copy-start(f32[64]{0:T(128)} %param.10) | copy-start | bytes 772
  49.7 8.7 %copy-start.5 = (s32[2048]{0:T(1024)S(1)}, s32[2048]{0:T(1024)}, u32[]{:S(2)}) copy-start(s32[2048]{0:T(1024)} %param.13) | copy-start | bytes 24580
  49.7 48.5 %copy-start.3 = (s32[2048]{0:T(1024)S(1)}, s32[2048]{0:T(1024)}, u32[]{:S(2)}) copy-start(s32[2048]{0:T(1024)} %param.12) | copy-start | bytes 24580
  224.6 109.9 %all-to-all-start.1 = ((f32[8,2048,64]{1,2,0:T(8,128)}), f32[8,2048,64]{1,2,0:T(8,128)}, u32[]{:S(2)}, u32[]{:S(2)}) async-start(f32[8,2048,64]{1,2,0:T(8,128)} %get-tuple-element.41), calls=%async_computation.1 | async-start | bytes 8388608 | tf_op jit(solution)/shard_map/all_to_all | solution.py:34
  338.6 4.0 %copy-start.1 = (f32[822,512]{1,0:T(8,128)S(1)}, f32[822,512]{1,0:T(8,128)}, u32[]{:S(2)}) copy-start(f32[822,512]{1,0:T(8,128)} %param.9) | copy-start | bytes 5050372
Sparse Core Ops, SparseCore 0:
  49.8 170.1 all-reduce.2
where the time goes:
time: 351 us; the launch traced here: 349 us
  waiting for transfers between devices  113 us (32%)
  blocking collectives  81.6 us (23%)
  other arithmetic  58.3 us (17%)
  local copies, waits for them, and re-layouts  46.3 us (13%)
  matrix products  22.6 us (6%)
  between operations  14.2 us (4%)
  starting transfers between devices  13.4 us (4%)
    psum x1, waiting for transfers between devices, shards(): head_vecs = lax.psum(partial_value, ('rows', 'dim'))  113 us
    unnamed x1, blocking collectives  81.6 us
    select_n x1, other arithmetic, shards(): level = jnp.take(thresholds, thr_idx)  39.7 us
    dot_general x4, matrix products, score_block(): score = jnp.dot(rows_q, ent_low.T, preferred_element_type=jnp.float32)  22.6 us
    all_to_all x2, starting transfers between devices, several_exchanges(): lax.all_to_all(slab, axis, split_axis=0, concat_axis=0, tiled=True)  13.4 us
    gather x1, local copies, waits for them, and re-layouts, pick_rows(): picked = jnp.take(table, jnp.clip(local, 0, count - 1), axis=0)  12.9 us
    unnamed x15, local copies, waits for them, and re-layouts  9.66 us
    gather x1, local copies, waits for them, and re-layouts, shards(): jnp.take(relations, rel_ids, axis=0)  8.9 us
  transfers between devices with their start and end apart: 3, of which 1 were waited for; matrix products, arithmetic and copies ran while one was open for 29% of the time, Pallas kernels for 0%

commit v1 on v0

v1 whole, which is shorter than its diff:
```python
import functools

import jax
import jax.numpy as jnp
from jax import lax
from jax.experimental import pallas as pl
from jax.experimental.pallas import tpu as pltpu
from jax.sharding import Mesh
from jax.sharding import PartitionSpec as P


sharpness = 2.0
ALL = ("x", "yl", "c", "yh", "z")
DIM = ("yh", "z")
YZ = ("yl", "yh", "z")
PARTS = ((0, 2048), (2048, 2048))
BLK = 512


def exchange(value, axis):
    return lax.all_to_all(value, axis, split_axis=0, concat_axis=0, tiled=True)


def spread(value, axis):
    count = lax.axis_size(axis)
    copies = jnp.broadcast_to(value[None], (count,) + value.shape)
    return exchange(copies, axis)


HOPS = tuple((dy, dz) for dz in (0, 1, 3, 2) for dy in (0, 1))


def flip_kernel(to_ref, x_ref, *refs):
    outs, turned = refs[:-1], refs[-1]
    turned[...] = x_ref[...].T
    cols = outs[0].shape[0]
    for k, o_ref in enumerate(outs):
        first = pl.multiple_of(to_ref[k] * cols, cols)
        o_ref[...] = turned[pl.ds(first, cols), :]


def flipped(table, to, start, length):
    width = table.shape[1]
    cols = width // len(HOPS)
    first = start // BLK
    spec = pl.BlockSpec((cols, BLK), lambda i, to: (0, i))
    return pl.pallas_call(
        flip_kernel,
        grid_spec=pltpu.PrefetchScalarGridSpec(
            num_scalar_prefetch=1,
            grid=(length // BLK,),
            in_specs=[pl.BlockSpec((BLK, width), lambda i, to: (first + i, 0))],
            out_specs=[spec] * len(HOPS),
            scratch_shapes=[pltpu.VMEM((width, BLK), table.dtype)],
        ),
        out_shape=[jax.ShapeDtypeStruct((cols, length), table.dtype)] * len(HOPS),
        cost_estimate=pl.CostEstimate(flops=0, transcendentals=0, bytes_accessed=8 * width * length),
        name="flip",
    )(to, table)


def place_kernel(start, rows, from_ref, *refs):
    count = len(HOPS)
    parts, out, sems = refs[:count], refs[-2], refs[-1]
    copies = []
    for k, part in enumerate(parts):
        at = pl.multiple_of(from_ref[k] * rows + start, 128)
        copies.append(
            pltpu.make_async_copy(part, out.at[:, pl.ds(at, part.shape[1])], sems.at[k])
        )
    for copy in copies:
        copy.start()
    for copy in copies:
        copy.wait()


def placed(parts, origin, start, rows, held):
    count = len(parts)
    cols = parts[0].shape[0]
    args = list(parts)
    if held is not None:
        args.append(held)
    return pl.pallas_call(
        functools.partial(place_kernel, start, rows),
        in_specs=[pl.BlockSpec(memory_space=pltpu.SMEM)] + [pl.BlockSpec(memory_space=pl.ANY)] * len(args),
        out_specs=pl.BlockSpec(memory_space=pl.ANY),
        out_shape=jax.ShapeDtypeStruct((cols, count * rows), parts[0].dtype),
        scratch_shapes=[pltpu.SemaphoreType.DMA((count,))],
        input_output_aliases={} if held is None else {count + 1: 0},
        name="place",
    )(origin, *args)


def sent(parts):
    got = [parts[0]]
    for (dy, dz), part in list(zip(HOPS, parts))[1:]:
        way = [(y * 4 + z, (y ^ dy) * 4 + (z + dz) % 4) for y in range(2) for z in range(4)]
        got.append(lax.ppermute(part, DIM, way))
    return got


def score_kernel(q_ref, lvl_ref, e_ref, o_ref, ql_ref):
    queries = q_ref.shape[0]

    @pl.when(pl.program_id(0) == 0)
    def _():
        ql_ref[...] = q_ref[...].astype(jnp.bfloat16)
        o_ref[...] = jnp.zeros_like(o_ref)

    ent = e_ref[...].astype(jnp.bfloat16)
    score = lax.dot_general(
        ent, ql_ref[...], (((1,), (1,)), ((), ())), preferred_element_type=jnp.float32
    )
    soft = 1.0 / (1.0 + jnp.exp(-sharpness * (score - lvl_ref[...])))
    o_ref[...] += jnp.sum(soft.reshape(-1, 8, queries), axis=0)


def soft_counts(query, level, table):
    queries, width = query.shape
    rows = table.shape[0]
    eb = 512
    out = pl.pallas_call(
        score_kernel,
        grid=(rows // eb,),
        in_specs=[
            pl.BlockSpec((queries, width), lambda i: (0, 0)),
            pl.BlockSpec((1, queries), lambda i: (0, 0)),
            pl.BlockSpec((eb, width), lambda i: (i, 0)),
        ],
        out_specs=pl.BlockSpec((8, queries), lambda i: (0, 0)),
        out_shape=jax.ShapeDtypeStruct((8, queries), jnp.float32),
        scratch_shapes=[pltpu.VMEM((queries, width), jnp.bfloat16)],
        cost_estimate=pl.CostEstimate(
            flops=2 * queries * rows * width,
            transcendentals=2 * queries * rows,
            bytes_accessed=4 * width * (rows + queries),
        ),
        name="soft_counts",
    )(query, level.reshape(1, queries), table)
    return jnp.sum(out, axis=0)


def pick_rows(table, ids, start):
    count = table.shape[0]
    local = ids - start
    owned = (local >= 0) & (local < count)
    picked = jnp.take(table, jnp.clip(local, 0, count - 1), axis=0, mode="clip")
    return jnp.where(owned[:, None], picked, 0.0)


def shards(entity_table, relations, thresholds, head_ids, rel_ids, thr_idx):
    rows, width = entity_table.shape
    devices = lax.axis_size(ALL)
    queries = head_ids.shape[0]
    ents = rows * devices
    me = lax.axis_index(ALL)
    core = lax.axis_index("c")
    swap = [(0, 1), (1, 0)]
    start = me * rows
    home = queries // devices

    sizes = [lax.axis_size(a) for a in ALL]
    order = lambda v: v.reshape(*sizes, home).transpose(2, 0, 1, 3, 4, 5).reshape(2, queries // 2)

    high, z = lax.axis_index("yh"), lax.axis_index("z")
    hop_y = jnp.asarray([h[0] for h in HOPS], jnp.int32)
    hop_z = jnp.asarray([h[1] for h in HOPS], jnp.int32)
    to = (high ^ hop_y) * 4 + (z + hop_z) % 4
    origin = (high ^ hop_y) * 4 + (z - hop_z) % 4

    flat1 = flipped(entity_table, to, *PARTS[0])
    got1 = sent(flat1)

    ids = order(head_ids)
    ids, flat1 = lax.optimization_barrier((ids, flat1))
    theirs = pick_rows(entity_table, jnp.take(ids, 1 - core, axis=0), start)
    passed = lax.ppermute(theirs, "c", swap)
    mine = pick_rows(entity_table, jnp.take(ids, core, axis=0), start) + passed
    part = exchange(mine, "x")
    part = jnp.sum(part.reshape(4, -1, width), axis=0)
    part = exchange(part, YZ)
    head_vecs = jnp.sum(part.reshape(16, home, width), axis=0)

    my_rel = lax.dynamic_slice(rel_ids, (me * home,), (home,))
    query = head_vecs * jnp.take(relations, my_rel, axis=0, mode="clip")

    flat2 = flipped(entity_table, to, *PARTS[1])
    query = spread(query, YZ).reshape(-1, width)
    flat2, got1, query = lax.optimization_barrier((flat2, got1, query))
    got2 = sent(flat2)
    query = spread(query, "x").reshape(-1, width)
    other = lax.ppermute(query, "c", swap)

    hot = thr_idx[:, None] == jnp.arange(thresholds.shape[0])[None, :]
    level = order(jnp.sum(jnp.where(hot, thresholds[None, :], 0.0), axis=1))
    sum_own = soft_counts(query, jnp.take(level, core, axis=0), entity_table)
    sum_other = soft_counts(other, jnp.take(level, 1 - core, axis=0), entity_table)
    pair = jnp.stack([sum_own, sum_other])
    pair = jnp.where(core == 0, pair, pair[::-1])
    share = pair.reshape(2, 4, 2, 2, 4, home).transpose(1, 2, 0, 3, 4, 5).reshape(devices, home)
    got = exchange(share, ALL)
    fraction = jnp.sum(got, axis=0) * (1.0 / ents)

    table = placed(got1, origin, PARTS[0][0], rows, None)
    table = placed(got2, origin, PARTS[1][0], rows, table)
    return (table.T, fraction)


def solution(mesh):
    fine = Mesh(mesh.devices.reshape(4, 2, 2, 2, 4), ALL)
    whole = P(ALL, None)

    return jax.shard_map(
        shards,
        mesh=fine,
        in_specs=(whole, P(), P(), P(), P(), P()),
        out_specs=(P(("x", "yl", "c"), DIM), P(ALL)),
        check_vma=False,
    )
```

time: 351 us -> 478 us (1.36)
  Pallas kernels: 0 us -> 293 us
  waiting for transfers between devices: 113 us -> 56.7 us
  blocking collectives: 81.6 us -> 28.1 us
  starting transfers between devices: 13.4 us -> 61.9 us
  other arithmetic: 58.3 us -> 14 us
  local copies, waits for them, and re-layouts: 46.3 us -> 22.7 us
  matrix products: 22.6 us -> 0 us
  between operations: 14.2 us -> 0.98 us
    pallas_call x0 -> x6, Pallas kernels: none -> 293 us  [the longest x2 258 us: placed(): pl.pallas_call(functools.partial(place_kernel, start, rows), in_specs=[pl...]
    psum x1 -> x0, waiting for transfers between devices: 113 us -> none  [shards(): head_vecs = lax.psum(partial_value, ('rows', 'dim'))]
    unnamed x1 -> x0, blocking collectives: 81.6 us -> none
    select_n x2 -> x4, other arithmetic: 43.7 us -> 3.77 us  [the longest x1 3.13 us: pick_rows(): return jnp.where(owned[:, None], picked, 0.0)]
    all_to_all x2 -> x4, waiting for transfers between devices: 0.01 us -> 35.3 us  [exchange(): return lax.all_to_all(value, axis, split_axis=0, concat_axis=0, tiled=True)]
    ppermute x0 -> x16, starting transfers between devices: none -> 33.5 us  [the longest x14 29.5 us: sent(): got.append(lax.ppermute(part, DIM, way))]
    all_to_all x0 -> x1, blocking collectives: none -> 28.1 us  [exchange(): return lax.all_to_all(value, axis, split_axis=0, concat_axis=0, tiled=True)]
    dot_general x4 -> x0, matrix products: 22.6 us -> none  [score_block(): score = jnp.dot(rows_q, ent_low.T, preferred_element_type=jnp.float32)]
  transfers between devices with their start and end apart: 3 -> 20, of which waited for: 1 -> 5; matrix products, arithmetic and copies ran while one was open for 29% -> 4% of each run, Pallas kernels for 0% -> 60%
where the time goes in v1:
time: 478 us; the launch traced here: 477 us
  Pallas kernels  293 us (61%)
  starting transfers between devices  61.9 us (13%)
  waiting for transfers between devices  56.7 us (12%)
  blocking collectives  28.1 us (6%)
  local copies, waits for them, and re-layouts  22.7 us (5%)
  other arithmetic  14 us (3%)
    pallas_call x2, Pallas kernels, placed(): pl.pallas_call(functools.partial(place_kernel, start, rows), in_specs=[pl...  258 us
    all_to_all x4, waiting for transfers between devices, exchange(): return lax.all_to_all(value, axis, split_axis=0, concat_axis=0, tiled=True)  35.3 us
    ppermute x14, starting transfers between devices, sent(): got.append(lax.ppermute(part, DIM, way))  29.5 us
    all_to_all x4, starting transfers between devices, exchange(): return lax.all_to_all(value, axis, split_axis=0, concat_axis=0, tiled=True)  28.4 us
    all_to_all x1, blocking collectives, exchange(): return lax.all_to_all(value, axis, split_axis=0, concat_axis=0, tiled=True)  28.1 us
    pallas_call x2, Pallas kernels, soft_counts(): pl.pallas_call(score_kernel, grid=(rows // eb,), in_specs=[pl.BlockSpec((...  22.9 us
    ppermute x14, waiting for transfers between devices, sent(): got.append(lax.ppermute(part, DIM, way))  21.4 us
    gather x2, local copies, waits for them, and re-layouts, pick_rows(): picked = jnp.take(table, jnp.clip(local, 0, count - 1), axis=0, mode='clip')  17.3 us
  transfers between devices with their start and end apart: 20, of which 5 were waited for; matrix products, arithmetic and copies ran while one was open for 4% of the time, Pallas kernels for 60%

profile of v1, /device:TPU:1, one launch (start us, length us, event | category | flops | bytes accessed | tf_op | source)
XLA Modules:
  0.0 477.1 jit_solution(16913849141715168739)
XLA Ops:
  3.0 6.0 %flip.3 = (f32[64,2048]{1,0:T(8,128)}, f32[64,2048]{1,0:T(8,128)}, f32[64,2048]{1,0:T(8,128)}, f32[64,2048]{1,0:T(8,128)}, f32[64,2048]{1,0:T(8,128)}, /*index=5...) custom-call(s32[8]{0:T(128)} %get-tuple-element.98.to_ref, f32[4096,512]{1,0:T(8,128)} %e_ref.3), custom_call_target="tpu_custom_call" | custom-call | bytes 8388608 | tf_op jit(solution)/shard_map/flip/pallas_call | solution.py:47
  9.1 8.7 %gather_fusion.1 = f32[1024,512]{1,0:T(8,128)} fusion(f32[4096,512]{1,0:T(8,128)} %e_ref.3, s32[1024]{0:T(1024)S(1)} %clamp_clamp_fusion), kind=kCustom, calls=%fused_computation.1 | custom fusion | bytes 4198400 | tf_op jit(solution)/shard_map/jit(_take)/gather | solution.py:147
  17.7 3.1 broadcast_select_fusion
  22.3 8.7 %gather_fusion = f32[1024,512]{1,0:T(8,128)} fusion(f32[4096,512]{1,0:T(8,128)} %e_ref.3, s32[1024]{0:T(1024)S(1)} %clamp_clamp_fusion.1), kind=kCustom, calls=%fused_computation | custom fusion | bytes 4198400 | tf_op jit(solution)/shard_map/jit(_take)/gather | solution.py:147
  30.9 3.8 select_add_fusion
  34.7 4.5 all-to-all-start
  39.2 3.1 collective-permute-start
  43.9 21.7 %all-to-all-done = f32[4,256,512]{2,1,0:T(8,128)} async-done(((f32[4,256,512]{2,1,0:T(8,128)}), f32[4,256,512]{2,1,0:T(8,128)}, u32[]{:S(2)}, u32[]{:S(2)}) %all-to-all-start) | async-done | bytes 2097184 | tf_op jit(solution)/shard_map/all_to_all | solution.py:21
  65.7 2.7 reduce_sum.54
  68.3 7.9 %all-to-all-start.1 = ((f32[16,16,512]{2,1,0:T(8,128)}), f32[16,16,512]{2,1,0:T(8,128)S(1)}, u32[]{:S(2)}, u32[]{:S(2)}) async-start(f32[16,16,512]{2,1,0:T(8,128)} %bitcast.4), calls=%async_computation.1 | async-start | bytes 1048576 | tf_op jit(solution)/shard_map/all_to_all | solution.py:21
  76.2 3.8 collective-permute-start.2
  84.0 4.8 %collective-permute-start.6 = (f32[64,2048]{1,0:T(8,128)}, f32[64,2048]{1,0:T(8,128)}, u32[]{:S(2)}, u32[]{:S(2)}) collective-permute-start(f32[64,2048]{1,0:T(8,128)} %get-tuple-element.53), channel_id=1, source_target_pairs={{0,6},{1,7},{2,4},{3,5},{4,2},{5,3},{6,0},{7,1},{8,14},{9,15},{10,... | collective-permute-start | bytes 1572872 | tf_op jit(solution)/shard_map/ppermute | solution.py:98
  90.4 3.6 all-to-all-start.2
  93.9 6.0 %flip.2 = (f32[64,2048]{1,0:T(8,128)}, f32[64,2048]{1,0:T(8,128)}, f32[64,2048]{1,0:T(8,128)}, f32[64,2048]{1,0:T(8,128)}, f32[64,2048]{1,0:T(8,128)}, /*index=5...) custom-call(s32[8]{0:T(128)} %get-tuple-element.98.to_ref, f32[4096,512]{1,0:T(8,128)} %e_ref.3), custom_call_target="tpu_custom_call" | custom-call | bytes 8388608 | tf_op jit(solution)/shard_map/flip/pallas_call | solution.py:47
  100.0 8.4 %collective-permute-done.4.refs_5_ = f32[64,2048]{1,0:T(8,128)} collective-permute-done((f32[64,2048]{1,0:T(8,128)}, f32[64,2048]{1,0:T(8,128)}, u32[]{:S(2)}, u32[]{:S(2)}) %collective-permute-start.4) | collective-permute-done | bytes 524320 | tf_op jit(solution)/shard_map/ppermute | solution.py:98
  110.7 10.6 %collective-permute-done.6.refs_7_ = f32[64,2048]{1,0:T(8,128)} collective-permute-done((f32[64,2048]{1,0:T(8,128)}, f32[64,2048]{1,0:T(8,128)}, u32[]{:S(2)}, u32[]{:S(2)}) %collective-permute-start.6) | collective-permute-done | bytes 524320 | tf_op jit(solution)/shard_map/ppermute | solution.py:98
  121.3 13.6 %all-to-all-done.2 = f32[16,16,512]{2,1,0:T(8,128)S(1)} async-done(((f32[16,16,512]{2,1,0:T(8,128)}), f32[16,16,512]{2,1,0:T(8,128)S(1)}, u32[]{:S(2)}, u32[]{:S(2)}) %all-to-all-start.2) | async-done | bytes 524320 | tf_op jit(solution)/shard_map/all_to_all | solution.py:21
  135.2 28.1 %all_to_all.37 = f32[4,256,512]{2,1,0:T(8,128)} all-to-all(f32[4,256,512]{2,1,0:T(8,128)S(1)} %broadcast_in_dim.83), channel_id=1, replica_groups=mesh['x'=4,'yl'=2,'c'=2,'yh'=2,'z'=4] {'x'}, dimensions={0} | all-to-all | bytes 4194304 | tf_op jit(solution)/shard_map/all_to_all | solution.py:21
  174.4 11.4 %soft_counts.2 = f32[8,1024]{1,0:T(8,128)} custom-call(f32[1024,512]{1,0:T(8,128)} %bitcast.7.q_ref, f32[1,1024]{1,0:T(1,128)} %get-tuple-element.94.lvl_ref, f32[4096,512]{1,0:T(8,128)} %e_ref.3), custom_call_target="tpu_custom_call" | custom-call | flops 4294967296 | bytes 10485760 | tf_op jit(solution)/shard_map/soft_counts/pallas_call | solution.py:122
  189.2 2.9 collective-permute-start.14
  192.1 11.5 %soft_counts.3 = f32[8,1024]{1,0:T(8,128)} custom-call(f32[1024,512]{1,0:T(8,128)} %collective-permute-done.15.q_ref, f32[1,1024]{1,0:T(1,128)} %get-tuple-element.95.lvl_ref, f32[4096,512]{1,0:T(8,128)} %e_ref.3), custom_call_target="tpu_custom_call" | custom-call | flops 4294967296 | bytes 10485760 | tf_op jit(solution)/shard_map/soft_counts/pallas_call | solution.py:122
  205.3 12.5 %all-to-all-start.4 = ((f32[128,1,16]{2,1,0:T(1,128)}), f32[128,1,16]{2,1,0:T(1,128)S(1)}, u32[]{:S(2)}, u32[]{:S(2)}) async-start(f32[128,1,16]{2,1,0:T(1,128)} %bitcast.15), calls=%async_computation.4 | async-start | bytes 131072 | tf_op jit(solution)/shard_map/all_to_all | solution.py:21
  217.8 128.9 %place.2.refs_8_ = f32[64,32768]{1,0:T(8,128)} custom-call(s32[8]{0:T(128)} %get-tuple-element.99.from_ref, f32[64,2048]{1,0:T(8,128)} %get-tuple-element.63.refs_0_, f32[64,2048]{1,0:T(8,128)} %copy-done.1, f32[64,2048]{1,0:T(8,128)} %copy-done.2, f32[64,2048]{1,0:T(8,128)} %collective-permute-done.2.refs_3_, f32[64,2048]{1,0:T(8,128)} %collective-permute-done.3.refs_4_, ...), custom_call_target="tpu_custom_call" | custom-call | tf_op jit(solution)/shard_map/place/pallas_call | solution.py:83
  347.5 128.9 %place.3 = f32[64,32768]{1,0:T(8,128)} custom-call(s32[8]{0:T(128)} %get-tuple-element.99.from_ref, f32[64,2048]{1,0:T(8,128)} %get-tuple-element.55.refs_0_, f32[64,2048]{1,0:T(8,128)} %copy-done.3, f32[64,2048]{1,0:T(8,128)} %copy-done.4, f32[64,2048]{1,0:T(8,128)} %copy-done.5, ...), custom_call_target="tpu_custom_call", output_to_operand_aliasing={{}: (9, {})} | custom-call | tf_op jit(solution)/shard_map/place/pallas_call | solution.py:83
  (74 shorter events, 31.1 us)
Async XLA Ops:
  0.6 88.2 %copy-start = (f32[822,512]{1,0:T(8,128)S(1)}, f32[822,512]{1,0:T(8,128)}, u32[]{:S(2)}) copy-start(f32[822,512]{1,0:T(8,128)} %param.13) | copy-start | bytes 5050372
  20.9 10.1 %collective-permute-start.7 = (f32[1024,512]{1,0:T(8,128)}, f32[1024,512]{1,0:T(8,128)}, u32[]{:S(2)}, u32[]{:S(2)}) collective-permute-start(f32[1024,512]{1,0:T(8,128)} %broadcast_select_fusion), channel_id=1, source_target_pairs={{0,8},{8,0},{1,9},{9,1},{2,10},{10,2},{3,11},{11,3},{4,12},{12,4},... | collective-permute-start | bytes 6291464 | tf_op jit(solution)/shard_map/ppermute | solution.py:177
  34.7 30.9 %all-to-all-start = ((f32[4,256,512]{2,1,0:T(8,128)}), f32[4,256,512]{2,1,0:T(8,128)}, u32[]{:S(2)}, u32[]{:S(2)}) async-start(f32[4,256,512]{2,1,0:T(8,128)} %bitcast.18), calls=%async_computation | async-start | bytes 4194304 | tf_op jit(solution)/shard_map/all_to_all | solution.py:21
  39.2 44.2 %collective-permute-start = (f32[64,2048]{1,0:T(8,128)}, f32[64,2048]{1,0:T(8,128)S(1)}, u32[]{:S(2)}, u32[]{:S(2)}) collective-permute-start(f32[64,2048]{1,0:T(8,128)} %get-tuple-element.47), channel_id=1, source_target_pairs={{0,4},{1,5},{2,6},{3,7},{4,0},{5,1},{6,2},{7,3},{8,12},{9,13},{10,... | collective-permute-start | bytes 1572872 | tf_op jit(solution)/shard_map/ppermute | solution.py:98
  42.3 41.7 %collective-permute-start.1 = (f32[64,2048]{1,0:T(8,128)}, f32[64,2048]{1,0:T(8,128)S(1)}, u32[]{:S(2)}, u32[]{:S(2)}) collective-permute-start(f32[64,2048]{1,0:T(8,128)} %get-tuple-element.48), channel_id=1, source_target_pairs={{0,1},{1,2},{2,3},{3,0},{4,5},{5,6},{6,7},{7,4},{8,9},{9,10},{10,1... | collective-permute-start | bytes 1572872 | tf_op jit(solution)/shard_map/ppermute | solution.py:98
  68.3 21.1 %all-to-all-start.1 = ((f32[16,16,512]{2,1,0:T(8,128)}), f32[16,16,512]{2,1,0:T(8,128)S(1)}, u32[]{:S(2)}, u32[]{:S(2)}) async-start(f32[16,16,512]{2,1,0:T(8,128)} %bitcast.4), calls=%async_computation.1 | async-start | bytes 1048576 | tf_op jit(solution)/shard_map/all_to_all | solution.py:21
  76.2 23.7 %collective-permute-start.2 = (f32[64,2048]{1,0:T(8,128)}, f32[64,2048]{1,0:T(8,128)}, u32[]{:S(2)}, u32[]{:S(2)}) collective-permute-start(f32[64,2048]{1,0:T(8,128)} %get-tuple-element.49), channel_id=1, source_target_pairs={{0,5},{1,6},{2,7},{3,4},{4,1},{5,2},{6,3},{7,0},{8,13},{9,14},{10,... | collective-permute-start | bytes 1572872 | tf_op jit(solution)/shard_map/ppermute | solution.py:98
  80.0 20.0 %collective-permute-start.3 = (f32[64,2048]{1,0:T(8,128)}, f32[64,2048]{1,0:T(8,128)}, u32[]{:S(2)}, u32[]{:S(2)}) collective-permute-start(f32[64,2048]{1,0:T(8,128)} %get-tuple-element.50), channel_id=1, source_target_pairs={{0,3},{1,0},{2,1},{3,2},{4,7},{5,4},{6,5},{7,6},{8,11},{9,8},{10,9... | collective-permute-start | bytes 1572872 | tf_op jit(solution)/shard_map/ppermute | solution.py:98
  81.5 26.9 %collective-permute-start.4 = (f32[64,2048]{1,0:T(8,128)}, f32[64,2048]{1,0:T(8,128)}, u32[]{:S(2)}, u32[]{:S(2)}) collective-permute-start(f32[64,2048]{1,0:T(8,128)} %get-tuple-element.51), channel_id=1, source_target_pairs={{0,7},{1,4},{2,5},{3,6},{4,3},{5,0},{6,1},{7,2},{8,15},{9,12},{10,... | collective-permute-start | bytes 1572872 | tf_op jit(solution)/shard_map/ppermute | solution.py:98
  83.4 27.3 %collective-permute-start.5 = (f32[64,2048]{1,0:T(8,128)}, f32[64,2048]{1,0:T(8,128)}, u32[]{:S(2)}, u32[]{:S(2)}) collective-permute-start(f32[64,2048]{1,0:T(8,128)} %get-tuple-element.52), channel_id=1, source_target_pairs={{0,2},{1,3},{2,0},{3,1},{4,6},{5,7},{6,4},{7,5},{8,10},{9,11},{10,... | collective-permute-start | bytes 1572872 | tf_op jit(solution)/shard_map/ppermute | solution.py:98
  84.0 37.3 %collective-permute-start.6 = (f32[64,2048]{1,0:T(8,128)}, f32[64,2048]{1,0:T(8,128)}, u32[]{:S(2)}, u32[]{:S(2)}) collective-permute-start(f32[64,2048]{1,0:T(8,128)} %get-tuple-element.53), channel_id=1, source_target_pairs={{0,6},{1,7},{2,4},{3,5},{4,2},{5,3},{6,0},{7,1},{8,14},{9,15},{10,... | collective-permute-start | bytes 1572872 | tf_op jit(solution)/shard_map/ppermute | solution.py:98
  90.4 44.6 %all-to-all-start.2 = ((f32[16,16,512]{2,1,0:T(8,128)}), f32[16,16,512]{2,1,0:T(8,128)S(1)}, u32[]{:S(2)}, u32[]{:S(2)}) async-start(f32[16,16,512]{2,1,0:T(8,128)} %broadcast_in_dim.82), calls=%async_computation.2 | async-start | bytes 1048576 | tf_op jit(solution)/shard_map/all_to_all | solution.py:21
  135.2 34.2 %copy-start.6 = (s32[2048]{0:T(1024)S(1)}, s32[2048]{0:T(1024)}, u32[]{:S(2)}) copy-start(s32[2048]{0:T(1024)} %param.17) | copy-start | bytes 24580
  135.2 34.2 %copy-start.7 = (f32[64]{0:T(128)S(1)}, f32[64]{0:T(128)}, u32[]{:S(2)}) copy-start(f32[64]{0:T(128)} %param.14) | copy-start | bytes 772
  163.3 25.9 %collective-permute-start.15 = (f32[1024,512]{1,0:T(8,128)}, f32[1024,512]{1,0:T(8,128)}, u32[]{:S(2)}, u32[]{:S(2)}) collective-permute-start(f32[1024,512]{1,0:T(8,128)} %bitcast.7.q_ref), channel_id=1, source_target_pairs={{0,8},{8,0},{1,9},{9,1},{2,10},{10,2},{3,11},{11,3},{4,12},{12,4},... | collective-permute-start | bytes 6291464 | tf_op jit(solution)/shard_map/ppermute | solution.py:192
  165.9 20.7 %collective-permute-start.8 = (f32[64,2048]{1,0:T(8,128)}, f32[64,2048]{1,0:T(8,128)S(1)}, u32[]{:S(2)}, u32[]{:S(2)}) collective-permute-start(f32[64,2048]{1,0:T(8,128)} %get-tuple-element.56), channel_id=1, source_target_pairs={{0,4},{1,5},{2,6},{3,7},{4,0},{5,1},{6,2},{7,3},{8,12},{9,13},{10,... | collective-permute-start | bytes 1572872 | tf_op jit(solution)/shard_map/ppermute | solution.py:98
  167.5 20.5 %collective-permute-start.9 = (f32[64,2048]{1,0:T(8,128)}, f32[64,2048]{1,0:T(8,128)S(1)}, u32[]{:S(2)}, u32[]{:S(2)}) collective-permute-start(f32[64,2048]{1,0:T(8,128)} %get-tuple-element.57), channel_id=1, source_target_pairs={{0,1},{1,2},{2,3},{3,0},{4,5},{5,6},{6,7},{7,4},{8,9},{9,10},{10,1... | collective-permute-start | bytes 1572872 | tf_op jit(solution)/shard_map/ppermute | solution.py:98
  170.4 176.4 %collective-permute-start.10 = (f32[64,2048]{1,0:T(8,128)}, f32[64,2048]{1,0:T(8,128)S(1)}, u32[]{:S(2)}, u32[]{:S(2)}) collective-permute-start(f32[64,2048]{1,0:T(8,128)} %get-tuple-element.58), channel_id=1, source_target_pairs={{0,5},{1,6},{2,7},{3,4},{4,1},{5,2},{6,3},{7,0},{8,13},{9,14},{10,... | collective-permute-start | bytes 1572872 | tf_op jit(solution)/shard_map/ppermute | solution.py:98
  172.3 174.5 %collective-permute-start.11 = (f32[64,2048]{1,0:T(8,128)}, f32[64,2048]{1,0:T(8,128)}, u32[]{:S(2)}, u32[]{:S(2)}) collective-permute-start(f32[64,2048]{1,0:T(8,128)} %get-tuple-element.59), channel_id=1, source_target_pairs={{0,3},{1,0},{2,1},{3,2},{4,7},{5,4},{6,5},{7,6},{8,11},{9,8},{10,9... | collective-permute-start | bytes 1572872 | tf_op jit(solution)/shard_map/ppermute | solution.py:98
  186.6 16.9 %copy-start.3 = (f32[64,2048]{1,0:T(8,128)}, f32[64,2048]{1,0:T(8,128)S(1)}, u32[]{:S(2)}) copy-start(f32[64,2048]{1,0:T(8,128)S(1)} %collective-permute-done.8.refs_1_) | copy-start | bytes 1572868
  186.6 160.2 %collective-permute-start.12 = (f32[64,2048]{1,0:T(8,128)}, f32[64,2048]{1,0:T(8,128)}, u32[]{:S(2)}, u32[]{:S(2)}) collective-permute-start(f32[64,2048]{1,0:T(8,128)} %get-tuple-element.60), channel_id=1, source_target_pairs={{0,7},{1,4},{2,5},{3,6},{4,3},{5,0},{6,1},{7,2},{8,15},{9,12},{10,... | collective-permute-start | bytes 1572872 | tf_op jit(solution)/shard_map/ppermute | solution.py:98
  188.0 158.8 %collective-permute-start.13 = (f32[64,2048]{1,0:T(8,128)}, f32[64,2048]{1,0:T(8,128)}, u32[]{:S(2)}, u32[]{:S(2)}) collective-permute-start(f32[64,2048]{1,0:T(8,128)} %get-tuple-element.61), channel_id=1, source_target_pairs={{0,2},{1,3},{2,0},{3,1},{4,6},{5,7},{6,4},{7,5},{8,10},{9,11},{10,... | collective-permute-start | bytes 1572872 | tf_op jit(solution)/shard_map/ppermute | solution.py:98
  189.2 157.6 %collective-permute-start.14 = (f32[64,2048]{1,0:T(8,128)}, f32[64,2048]{1,0:T(8,128)}, u32[]{:S(2)}, u32[]{:S(2)}) collective-permute-start(f32[64,2048]{1,0:T(8,128)} %get-tuple-element.62), channel_id=1, source_target_pairs={{0,6},{1,7},{2,4},{3,5},{4,2},{5,3},{6,0},{7,1},{8,14},{9,15},{10,... | collective-permute-start | bytes 1572872 | tf_op jit(solution)/shard_map/ppermute | solution.py:98
  205.3 271.1 %all-to-all-start.4 = ((f32[128,1,16]{2,1,0:T(1,128)}), f32[128,1,16]{2,1,0:T(1,128)S(1)}, u32[]{:S(2)}, u32[]{:S(2)}) async-start(f32[128,1,16]{2,1,0:T(1,128)} %bitcast.15), calls=%async_computation.4 | async-start | bytes 131072 | tf_op jit(solution)/shard_map/all_to_all | solution.py:21
  (4 other events, 48.7 us)

commit v2 on v1

--- a/solution.py
+++ b/solution.py
@@ -13,7 +13,8 @@
 ALL = ("x", "yl", "c", "yh", "z")
 DIM = ("yh", "z")
 YZ = ("yl", "yh", "z")
-PARTS = ((0, 2048), (2048, 2048))
+PARTS = ((0, 1024), (1024, 3072))
+CAP = 16
 BLK = 512
 
 
@@ -61,22 +62,26 @@
 
 def place_kernel(start, rows, from_ref, *refs):
     count = len(HOPS)
-    parts, out, sems = refs[:count], refs[-2], refs[-1]
-    copies = []
+    parts, (out, held, sems_in, sems_out) = refs[:count], refs[-4:]
+    loads, stores = [], []
     for k, part in enumerate(parts):
         at = pl.multiple_of(from_ref[k] * rows + start, 128)
-        copies.append(
-            pltpu.make_async_copy(part, out.at[:, pl.ds(at, part.shape[1])], sems.at[k])
+        loads.append(pltpu.make_async_copy(part, held.at[k], sems_in.at[k]))
+        stores.append(
+            pltpu.make_async_copy(held.at[k], out.at[:, pl.ds(at, part.shape[1])], sems_out.at[k])
         )
-    for copy in copies:
-        copy.start()
-    for copy in copies:
-        copy.wait()
+    for load in loads:
+        load.start()
+    for load, store in zip(loads, stores):
+        load.wait()
+        store.start()
+    for store in stores:
+        store.wait()
 
 
 def placed(parts, origin, start, rows, held):
     count = len(parts)
-    cols = parts[0].shape[0]
+    cols, length = parts[0].shape
     args = list(parts)
     if held is not None:
         args.append(held)
@@ -85,7 +90,11 @@
         in_specs=[pl.BlockSpec(memory_space=pltpu.SMEM)] + [pl.BlockSpec(memory_space=pl.ANY)] * len(args),
         out_specs=pl.BlockSpec(memory_space=pl.ANY),
         out_shape=jax.ShapeDtypeStruct((cols, count * rows), parts[0].dtype),
-        scratch_shapes=[pltpu.SemaphoreType.DMA((count,))],
+        scratch_shapes=[
+            pltpu.VMEM((count, cols, length), parts[0].dtype),
+            pltpu.SemaphoreType.DMA((count,)),
+            pltpu.SemaphoreType.DMA((count,)),
+        ],
         input_output_aliases={} if held is None else {count + 1: 0},
         name="place",
     )(origin, *args)
@@ -168,25 +177,42 @@
     to = (high ^ hop_y) * 4 + (z + hop_z) % 4
     origin = (high ^ hop_y) * 4 + (z - hop_z) % 4
 
+    classes = lambda v: v.reshape(*sizes, home).transpose(1, 3, 4, 0, 2, 5).reshape(16, queries // 16)
+    ids = classes(head_ids)
+    owner = ids // rows
+    local = ids - owner * rows
+    spot = jnp.arange(queries // 16)
+    same = owner[:, :, None] == owner[:, None, :]
+    rank = jnp.sum((same & (spot[None, None, :] < spot[None, :, None])).astype(jnp.int32), axis=2)
+    fits = jnp.max(rank) < CAP
+    slot = jnp.arange(CAP)
+    hit = (owner == me)[:, None, :] & (rank[:, None, :] == slot[None, :, None])
+    wanted = jnp.sum(jnp.where(hit, local[:, None, :], 0), axis=2).reshape(-1)
+    out_rows = jnp.take(entity_table, wanted, axis=0, mode="clip").reshape(16, CAP, width)
+    found = exchange(out_rows, YZ).reshape(-1, width)
     flat1 = flipped(entity_table, to, *PARTS[0])
     got1 = sent(flat1)
-
-    ids = order(head_ids)
-    ids, flat1 = lax.optimization_barrier((ids, flat1))
-    theirs = pick_rows(entity_table, jnp.take(ids, 1 - core, axis=0), start)
-    passed = lax.ppermute(theirs, "c", swap)
-    mine = pick_rows(entity_table, jnp.take(ids, core, axis=0), start) + passed
-    part = exchange(mine, "x")
-    part = jnp.sum(part.reshape(4, -1, width), axis=0)
-    part = exchange(part, YZ)
-    head_vecs = jnp.sum(part.reshape(16, home, width), axis=0)
-
+    my_class = lax.axis_index(YZ)
+    my_owner = jnp.take(owner, my_class, axis=0)
+    my_rank = jnp.take(rank, my_class, axis=0)
+    mine = (my_owner // 32 == lax.axis_index("x")) & ((my_owner // 8) % 2 == core)
+    source = (my_owner // 16) % 2 * 8 + my_owner % 8
+    at = jnp.where(mine, source * CAP + my_rank, 0)
+    part = jnp.where(mine[:, None], jnp.take(found, at, axis=0, mode="clip"), 0.0)
+    part = exchange(part.reshape(8, home, width), ("x", "c"))
+    head_vecs = jnp.sum(part, axis=0)
+
+    def every_row(unused):
+        full = pick_rows(entity_table, head_ids, start)
+        full = exchange(full.reshape(devices, home, width), ALL)
+        return jnp.sum(full, axis=0)
+
+    head_vecs = lax.cond(fits, lambda h: h, every_row, head_vecs)
     my_rel = lax.dynamic_slice(rel_ids, (me * home,), (home,))
     query = head_vecs * jnp.take(relations, my_rel, axis=0, mode="clip")
 
     flat2 = flipped(entity_table, to, *PARTS[1])
     query = spread(query, YZ).reshape(-1, width)
-    flat2, got1, query = lax.optimization_barrier((flat2, got1, query))
     got2 = sent(flat2)
     query = spread(query, "x").reshape(-1, width)
     other = lax.ppermute(query, "c", swap)

time: 478 us -> 216 us (0.45)
  the two profiles are of different devices: /device:TPU:1 before, /device:TPU:32 now
where the time goes in v2:
time: 216 us; the launch traced here: 215 us
  waiting for transfers between devices  64 us (30%)
  starting transfers between devices  46.6 us (22%)
  Pallas kernels  44.2 us (20%)
  blocking collectives  41.6 us (19%)
  local copies, waits for them, and re-layouts  11 us (5%)
  other arithmetic  6.04 us (3%)
    ppermute x14, waiting for transfers between devices, sent(): got.append(lax.ppermute(part, DIM, way))  49.5 us
    all_to_all x2, blocking collectives, exchange(): return lax.all_to_all(value, axis, split_axis=0, concat_axis=0, tiled=True)  41.6 us
    ppermute x14, starting transfers between devices, sent(): got.append(lax.ppermute(part, DIM, way))  28.4 us
    pallas_call x2, Pallas kernels, soft_counts(): pl.pallas_call(score_kernel, grid=(rows // eb,), in_specs=[pl.BlockSpec((...  22.9 us
    all_to_all x3, starting transfers between devices, exchange(): return lax.all_to_all(value, axis, split_axis=0, concat_axis=0, tiled=True)  18.2 us
    all_to_all x3, waiting for transfers between devices, exchange(): return lax.all_to_all(value, axis, split_axis=0, concat_axis=0, tiled=True)  14.5 us
    pallas_call x2, Pallas kernels, flipped(): pl.pallas_call(flip_kernel, grid_spec=pltpu.PrefetchScalarGridSpec(num_sc...  12 us
    pallas_call x2, Pallas kernels, placed(): pl.pallas_call(functools.partial(place_kernel, start, rows), in_specs=[pl...  9.24 us
  transfers between devices with their start and end apart: 18, of which 7 were waited for; matrix products, arithmetic and copies ran while one was open for 3% of the time, Pallas kernels for 21%

profile of v2, /device:TPU:32, one launch (start us, length us, event | category | flops | bytes accessed | tf_op | source)
XLA Modules:
  0.0 215.0 jit_solution(14474257214352464468)
XLA Ops:
  2.9 5.4 %gather_fusion.1 = f32[256,512]{1,0:T(8,128)} fusion(f32[4096,512]{1,0:T(8,128)} %e_ref.3, s32[1024]{0:T(1024)S(1)} %pad_clamp_fusion.2), kind=kCustom, calls=%fused_computation.1 | custom fusion | bytes 1049600 | tf_op jit(solution)/shard_map/jit(_take)/gather | solution.py:191
  8.3 8.1 %all-to-all-start.1 = ((f32[16,16,512]{2,1,0:T(8,128)}), f32[16,16,512]{2,1,0:T(8,128)S(1)}, u32[]{:S(2)}, u32[]{:S(2)}) async-start(f32[16,16,512]{2,1,0:T(8,128)} %bitcast.4), calls=%async_computation.1 | async-start | bytes 1048576 | tf_op jit(solution)/shard_map/all_to_all | solution.py:22
  16.5 9.7 %all-to-all-done.1 = f32[16,16,512]{2,1,0:T(8,128)S(1)} async-done(((f32[16,16,512]{2,1,0:T(8,128)}), f32[16,16,512]{2,1,0:T(8,128)S(1)}, u32[]{:S(2)}, u32[]{:S(2)}) %all-to-all-start.1) | async-done | bytes 524320 | tf_op jit(solution)/shard_map/all_to_all | solution.py:22
  27.7 4.3 %all-to-all-start.2 = ((f32[8,16,512]{2,1,0:T(8,128)}), f32[8,16,512]{2,1,0:T(8,128)S(1)}, u32[]{:S(2)}, u32[]{:S(2)}) async-start(f32[8,16,512]{2,1,0:T(8,128)} %broadcast_select_fusion.1), calls=%async_computation.2 | async-start | bytes 524288 | tf_op jit(solution)/shard_map/all_to_all | solution.py:22
  34.6 4.9 %all-to-all-done.2 = f32[8,16,512]{2,1,0:T(8,128)S(1)} async-done(((f32[8,16,512]{2,1,0:T(8,128)}), f32[8,16,512]{2,1,0:T(8,128)S(1)}, u32[]{:S(2)}, u32[]{:S(2)}) %all-to-all-start.2) | async-done | bytes 262176 | tf_op jit(solution)/shard_map/all_to_all | solution.py:22
  39.6 14.0 %all_to_all.35 = f32[16,16,512]{2,1,0:T(8,128)S(1)} all-to-all(f32[16,16,512]{2,1,0:T(8,128)S(1)} %broadcast_in_dim.122), channel_id=1, replica_groups=mesh['x'=4,'yl'=2,'c'=2,'yh'=2,'z'=4] {'yl','yh','z'}, dimensions={0} | all-to-all | bytes 1048576 | tf_op jit(solution)/shard_map/all_to_all | solution.py:22
  53.9 27.7 %all_to_all.36 = f32[4,256,512]{2,1,0:T(8,128)} all-to-all(f32[4,256,512]{2,1,0:T(8,128)S(1)} %broadcast_in_dim.124), channel_id=1, replica_groups=mesh['x'=4,'yl'=2,'c'=2,'yh'=2,'z'=4] {'x'}, dimensions={0} | all-to-all | bytes 4194304 | tf_op jit(solution)/shard_map/all_to_all | solution.py:22
  82.1 3.7 %flip.3 = (f32[64,1024]{1,0:T(8,128)}, f32[64,1024]{1,0:T(8,128)}, f32[64,1024]{1,0:T(8,128)}, f32[64,1024]{1,0:T(8,128)}, f32[64,1024]{1,0:T(8,128)}, /*index=5...) custom-call(s32[8]{0:T(128)} %get-tuple-element.82.to_ref, f32[4096,512]{1,0:T(8,128)} %e_ref.3), custom_call_target="tpu_custom_call" | custom-call | bytes 4194304 | tf_op jit(solution)/shard_map/flip/pallas_call | solution.py:48
  88.4 3.1 %collective-permute-start.9 = (f32[64,1024]{1,0:T(8,128)}, f32[64,1024]{1,0:T(8,128)}, u32[]{:S(2)}, u32[]{:S(2)}) collective-permute-start(f32[64,1024]{1,0:T(8,128)} %get-tuple-element.49), channel_id=1, source_target_pairs={{0,5},{1,6},{2,7},{3,4},{4,1},{5,2},{6,3},{7,0},{8,13},{9,14},{10,... | collective-permute-start | bytes 786440 | tf_op jit(solution)/shard_map/ppermute | solution.py:107
  91.5 8.3 %flip.2 = (f32[64,3072]{1,0:T(8,128)}, f32[64,3072]{1,0:T(8,128)}, f32[64,3072]{1,0:T(8,128)}, f32[64,3072]{1,0:T(8,128)}, f32[64,3072]{1,0:T(8,128)}, /*index=5...) custom-call(s32[8]{0:T(128)} %get-tuple-element.82.to_ref, f32[4096,512]{1,0:T(8,128)} %e_ref.3), custom_call_target="tpu_custom_call" | custom-call | bytes 12582912 | tf_op jit(solution)/shard_map/flip/pallas_call | solution.py:48
  100.9 3.0 %collective-permute-start.1 = (f32[64,3072]{1,0:T(8,128)}, f32[64,3072]{1,0:T(8,128)S(1)}, u32[]{:S(2)}, u32[]{:S(2)}) collective-permute-start(f32[64,3072]{1,0:T(8,128)} %get-tuple-element.40), channel_id=1, source_target_pairs={{0,1},{1,2},{2,3},{3,0},{4,5},{5,6},{6,7},{7,4},{8,9},{9,10},{10,1... | collective-permute-start | bytes 2359304 | tf_op jit(solution)/shard_map/ppermute | solution.py:107
  104.0 4.0 %collective-permute-start.11 = (f32[64,1024]{1,0:T(8,128)}, f32[64,1024]{1,0:T(8,128)}, u32[]{:S(2)}, u32[]{:S(2)}) collective-permute-start(f32[64,1024]{1,0:T(8,128)} %get-tuple-element.51), channel_id=1, source_target_pairs={{0,7},{1,4},{2,5},{3,6},{4,3},{5,0},{6,1},{7,2},{8,15},{9,12},{10,... | collective-permute-start | bytes 786440 | tf_op jit(solution)/shard_map/ppermute | solution.py:107
  108.0 3.6 %collective-permute-done.10.refs_4_ = f32[64,1024]{1,0:T(8,128)} collective-permute-done((f32[64,1024]{1,0:T(8,128)}, f32[64,1024]{1,0:T(8,128)}, u32[]{:S(2)}, u32[]{:S(2)}) %collective-permute-start.10) | collective-permute-done | bytes 262176 | tf_op jit(solution)/shard_map/ppermute | solution.py:107
  113.4 13.9 %collective-permute-done.11.refs_5_ = f32[64,1024]{1,0:T(8,128)} collective-permute-done((f32[64,1024]{1,0:T(8,128)}, f32[64,1024]{1,0:T(8,128)}, u32[]{:S(2)}, u32[]{:S(2)}) %collective-permute-start.11) | collective-permute-done | bytes 262176 | tf_op jit(solution)/shard_map/ppermute | solution.py:107
  132.8 7.9 %collective-permute-done.13.refs_7_ = f32[64,1024]{1,0:T(8,128)} collective-permute-done((f32[64,1024]{1,0:T(8,128)}, f32[64,1024]{1,0:T(8,128)}, u32[]{:S(2)}, u32[]{:S(2)}) %collective-permute-start.13) | collective-permute-done | bytes 262176 | tf_op jit(solution)/shard_map/ppermute | solution.py:107
  140.7 3.2 %collective-permute-start.4 = (f32[64,3072]{1,0:T(8,128)}, f32[64,3072]{1,0:T(8,128)}, u32[]{:S(2)}, u32[]{:S(2)}) collective-permute-start(f32[64,3072]{1,0:T(8,128)} %get-tuple-element.43), channel_id=1, source_target_pairs={{0,7},{1,4},{2,5},{3,6},{4,3},{5,0},{6,1},{7,2},{8,15},{9,12},{10,... | collective-permute-start | bytes 2359304 | tf_op jit(solution)/shard_map/ppermute | solution.py:107
  145.5 4.1 %collective-permute-start.6 = (f32[64,3072]{1,0:T(8,128)}, f32[64,3072]{1,0:T(8,128)}, u32[]{:S(2)}, u32[]{:S(2)}) collective-permute-start(f32[64,3072]{1,0:T(8,128)} %get-tuple-element.45), channel_id=1, source_target_pairs={{0,6},{1,7},{2,4},{3,5},{4,2},{5,3},{6,0},{7,1},{8,14},{9,15},{10,... | collective-permute-start | bytes 2359304 | tf_op jit(solution)/shard_map/ppermute | solution.py:107
  149.6 11.5 %soft_counts.2 = f32[8,1024]{1,0:T(8,128)} custom-call(f32[1024,512]{1,0:T(8,128)} %bitcast.9.q_ref, f32[1,1024]{1,0:T(1,128)} %get-tuple-element.78.lvl_ref, f32[4096,512]{1,0:T(8,128)} %e_ref.3), custom_call_target="tpu_custom_call" | custom-call | flops 4294967296 | bytes 10485760 | tf_op jit(solution)/shard_map/soft_counts/pallas_call | solution.py:131
  161.8 11.5 %soft_counts.3 = f32[8,1024]{1,0:T(8,128)} custom-call(f32[1024,512]{1,0:T(8,128)} %collective-permute-done.14.q_ref, f32[1,1024]{1,0:T(1,128)} %get-tuple-element.79.lvl_ref, f32[4096,512]{1,0:T(8,128)} %e_ref.3), custom_call_target="tpu_custom_call" | custom-call | flops 4294967296 | bytes 10485760 | tf_op jit(solution)/shard_map/soft_counts/pallas_call | solution.py:131
  175.1 5.9 %all-to-all-start.5 = ((f32[128,1,16]{2,1,0:T(1,128)}), f32[128,1,16]{2,1,0:T(1,128)S(1)}, u32[]{:S(2)}, u32[]{:S(2)}) async-start(f32[128,1,16]{2,1,0:T(1,128)} %bitcast.17), calls=%async_computation.5 | async-start | bytes 131072 | tf_op jit(solution)/shard_map/all_to_all | solution.py:22
  181.0 3.1 %place.2.refs_8_ = f32[64,32768]{1,0:T(8,128)} custom-call(s32[8]{0:T(128)} %get-tuple-element.83.from_ref, f32[64,1024]{1,0:T(8,128)} %get-tuple-element.46.refs_0_, f32[64,1024]{1,0:T(8,128)} %copy-done.3, f32[64,1024]{1,0:T(8,128)} %copy-done.4, f32[64,1024]{1,0:T(8,128)} %collective-permute-done.9.refs_3_, f32[64,1024]{1,0:T(8,128)} %collective-permute-done.10.refs_4_, ...), custom_call_target="tpu_custom_call" | custom-call | tf_op jit(solution)/shard_map/place/pallas_call | solution.py:88
  184.1 11.6 %collective-permute-done.3.refs_4_ = f32[64,3072]{1,0:T(8,128)} collective-permute-done((f32[64,3072]{1,0:T(8,128)}, f32[64,3072]{1,0:T(8,128)}, u32[]{:S(2)}, u32[]{:S(2)}) %collective-permute-start.3) | collective-permute-done | bytes 786464 | tf_op jit(solution)/shard_map/ppermute | solution.py:107
  195.7 12.4 %collective-permute-done.5.refs_6_ = f32[64,3072]{1,0:T(8,128)} collective-permute-done((f32[64,3072]{1,0:T(8,128)}, f32[64,3072]{1,0:T(8,128)}, u32[]{:S(2)}, u32[]{:S(2)}) %collective-permute-start.5) | collective-permute-done | bytes 786464 | tf_op jit(solution)/shard_map/ppermute | solution.py:107
  208.1 6.2 %place.3 = f32[64,32768]{1,0:T(8,128)} custom-call(s32[8]{0:T(128)} %get-tuple-element.83.from_ref, f32[64,3072]{1,0:T(8,128)} %get-tuple-element.38.refs_0_, f32[64,3072]{1,0:T(8,128)} %copy-done.1, f32[64,3072]{1,0:T(8,128)} %copy-done.2, f32[64,3072]{1,0:T(8,128)} %collective-permute-done.2.refs_3_, ...), custom_call_target="tpu_custom_call", output_to_operand_aliasing={{}: (9, {})} | custom-call | tf_op jit(solution)/shard_map/place/pallas_call | solution.py:88
  (82 shorter events, 22.6 us)
Async XLA Ops:
  0.6 33.4 %copy-start = (f32[822,512]{1,0:T(8,128)S(1)}, f32[822,512]{1,0:T(8,128)}, u32[]{:S(2)}) copy-start(f32[822,512]{1,0:T(8,128)} %param.15) | copy-start | bytes 5050372
  8.3 17.8 %all-to-all-start.1 = ((f32[16,16,512]{2,1,0:T(8,128)}), f32[16,16,512]{2,1,0:T(8,128)S(1)}, u32[]{:S(2)}, u32[]{:S(2)}) async-start(f32[16,16,512]{2,1,0:T(8,128)} %bitcast.4), calls=%async_computation.1 | async-start | bytes 1048576 | tf_op jit(solution)/shard_map/all_to_all | solution.py:22
  27.7 11.8 %all-to-all-start.2 = ((f32[8,16,512]{2,1,0:T(8,128)}), f32[8,16,512]{2,1,0:T(8,128)S(1)}, u32[]{:S(2)}, u32[]{:S(2)}) async-start(f32[8,16,512]{2,1,0:T(8,128)} %broadcast_select_fusion.1), calls=%async_computation.2 | async-start | bytes 524288 | tf_op jit(solution)/shard_map/all_to_all | solution.py:22
  39.5 42.0 %copy-start.8 = (s32[8]{0:T(128)S(1)}, s32[8]{0:T(128)}, u32[]{:S(2)}) copy-start(s32[8]{0:T(128)} %constant.209) | copy-start | bytes 100
  39.6 42.0 %copy-start.9 = (s32[8]{0:T(128)S(1)}, s32[8]{0:T(128)}, u32[]{:S(2)}) copy-start(s32[8]{0:T(128)} %constant.170.clone) | copy-start | bytes 100
  39.6 42.0 %copy-start.10 = (s32[8]{0:T(128)S(1)}, s32[8]{0:T(128)}, u32[]{:S(2)}) copy-start(s32[8]{0:T(128)} %constant.169.clone) | copy-start | bytes 100
  81.5 64.0 %collective-permute-start.14 = (f32[1024,512]{1,0:T(8,128)}, f32[1024,512]{1,0:T(8,128)}, u32[]{:S(2)}, u32[]{:S(2)}) collective-permute-start(f32[1024,512]{1,0:T(8,128)} %bitcast.9.q_ref), channel_id=1, source_target_pairs={{0,8},{8,0},{1,9},{9,1},{2,10},{10,2},{3,11},{11,3},{4,12},{12,4},... | collective-permute-start | bytes 6291464 | tf_op jit(solution)/shard_map/ppermute | solution.py:218
  85.7 14.5 %collective-permute-start.7 = (f32[64,1024]{1,0:T(8,128)}, f32[64,1024]{1,0:T(8,128)S(1)}, u32[]{:S(2)}, u32[]{:S(2)}) collective-permute-start(f32[64,1024]{1,0:T(8,128)} %get-tuple-element.47), channel_id=1, source_target_pairs={{0,4},{1,5},{2,6},{3,7},{4,0},{5,1},{6,2},{7,3},{8,12},{9,13},{10,... | collective-permute-start | bytes 786440 | tf_op jit(solution)/shard_map/ppermute | solution.py:107
  87.7 16.3 %collective-permute-start.8 = (f32[64,1024]{1,0:T(8,128)}, f32[64,1024]{1,0:T(8,128)S(1)}, u32[]{:S(2)}, u32[]{:S(2)}) collective-permute-start(f32[64,1024]{1,0:T(8,128)} %get-tuple-element.48), channel_id=1, source_target_pairs={{0,1},{1,2},{2,3},{3,0},{4,5},{5,6},{6,7},{7,4},{8,9},{9,10},{10,1... | collective-permute-start | bytes 786440 | tf_op jit(solution)/shard_map/ppermute | solution.py:107
  88.4 40.9 %copy-start.6 = (s32[2048]{0:T(1024)S(1)}, s32[2048]{0:T(1024)}, u32[]{:S(2)}) copy-start(s32[2048]{0:T(1024)} %param.19) | copy-start | bytes 24580
  88.4 40.9 %copy-start.7 = (f32[64]{0:T(128)S(1)}, f32[64]{0:T(128)}, u32[]{:S(2)}) copy-start(f32[64]{0:T(128)} %param.16) | copy-start | bytes 772
  88.4 15.5 %collective-permute-start.9 = (f32[64,1024]{1,0:T(8,128)}, f32[64,1024]{1,0:T(8,128)}, u32[]{:S(2)}, u32[]{:S(2)}) collective-permute-start(f32[64,1024]{1,0:T(8,128)} %get-tuple-element.49), channel_id=1, source_target_pairs={{0,5},{1,6},{2,7},{3,4},{4,1},{5,2},{6,3},{7,0},{8,13},{9,14},{10,... | collective-permute-start | bytes 786440 | tf_op jit(solution)/shard_map/ppermute | solution.py:107
  99.9 40.8 %collective-permute-start = (f32[64,3072]{1,0:T(8,128)}, f32[64,3072]{1,0:T(8,128)S(1)}, u32[]{:S(2)}, u32[]{:S(2)}) collective-permute-start(f32[64,3072]{1,0:T(8,128)} %get-tuple-element.39), channel_id=1, source_target_pairs={{0,4},{1,5},{2,6},{3,7},{4,0},{5,1},{6,2},{7,3},{8,12},{9,13},{10,... | collective-permute-start | bytes 2359304 | tf_op jit(solution)/shard_map/ppermute | solution.py:107
  100.9 42.9 %collective-permute-start.1 = (f32[64,3072]{1,0:T(8,128)}, f32[64,3072]{1,0:T(8,128)S(1)}, u32[]{:S(2)}, u32[]{:S(2)}) collective-permute-start(f32[64,3072]{1,0:T(8,128)} %get-tuple-element.40), channel_id=1, source_target_pairs={{0,1},{1,2},{2,3},{3,0},{4,5},{5,6},{6,7},{7,4},{8,9},{9,10},{10,1... | collective-permute-start | bytes 2359304 | tf_op jit(solution)/shard_map/ppermute | solution.py:107
  103.9 7.6 %collective-permute-start.10 = (f32[64,1024]{1,0:T(8,128)}, f32[64,1024]{1,0:T(8,128)}, u32[]{:S(2)}, u32[]{:S(2)}) collective-permute-start(f32[64,1024]{1,0:T(8,128)} %get-tuple-element.50), channel_id=1, source_target_pairs={{0,3},{1,0},{2,1},{3,2},{4,7},{5,4},{6,5},{7,6},{8,11},{9,8},{10,9... | collective-permute-start | bytes 786440 | tf_op jit(solution)/shard_map/ppermute | solution.py:107
  104.0 23.3 %collective-permute-start.11 = (f32[64,1024]{1,0:T(8,128)}, f32[64,1024]{1,0:T(8,128)}, u32[]{:S(2)}, u32[]{:S(2)}) collective-permute-start(f32[64,1024]{1,0:T(8,128)} %get-tuple-element.51), channel_id=1, source_target_pairs={{0,7},{1,4},{2,5},{3,6},{4,3},{5,0},{6,1},{7,2},{8,15},{9,12},{10,... | collective-permute-start | bytes 786440 | tf_op jit(solution)/shard_map/ppermute | solution.py:107
  111.6 18.8 %collective-permute-start.12 = (f32[64,1024]{1,0:T(8,128)}, f32[64,1024]{1,0:T(8,128)}, u32[]{:S(2)}, u32[]{:S(2)}) collective-permute-start(f32[64,1024]{1,0:T(8,128)} %get-tuple-element.52), channel_id=1, source_target_pairs={{0,2},{1,3},{2,0},{3,1},{4,6},{5,7},{6,4},{7,5},{8,10},{9,11},{10,... | collective-permute-start | bytes 786440 | tf_op jit(solution)/shard_map/ppermute | solution.py:107
  127.3 13.4 %collective-permute-start.13 = (f32[64,1024]{1,0:T(8,128)}, f32[64,1024]{1,0:T(8,128)}, u32[]{:S(2)}, u32[]{:S(2)}) collective-permute-start(f32[64,1024]{1,0:T(8,128)} %get-tuple-element.53), channel_id=1, source_target_pairs={{0,6},{1,7},{2,4},{3,5},{4,2},{5,3},{6,0},{7,1},{8,14},{9,15},{10,... | collective-permute-start | bytes 786440 | tf_op jit(solution)/shard_map/ppermute | solution.py:107
  130.3 53.7 %collective-permute-start.2 = (f32[64,3072]{1,0:T(8,128)}, f32[64,3072]{1,0:T(8,128)}, u32[]{:S(2)}, u32[]{:S(2)}) collective-permute-start(f32[64,3072]{1,0:T(8,128)} %get-tuple-element.41), channel_id=1, source_target_pairs={{0,5},{1,6},{2,7},{3,4},{4,1},{5,2},{6,3},{7,0},{8,13},{9,14},{10,... | collective-permute-start | bytes 2359304 | tf_op jit(solution)/shard_map/ppermute | solution.py:107
  140.7 55.0 %collective-permute-start.3 = (f32[64,3072]{1,0:T(8,128)}, f32[64,3072]{1,0:T(8,128)}, u32[]{:S(2)}, u32[]{:S(2)}) collective-permute-start(f32[64,3072]{1,0:T(8,128)} %get-tuple-element.42), channel_id=1, source_target_pairs={{0,3},{1,0},{2,1},{3,2},{4,7},{5,4},{6,5},{7,6},{8,11},{9,8},{10,9... | collective-permute-start | bytes 2359304 | tf_op jit(solution)/shard_map/ppermute | solution.py:107
  140.7 55.0 %collective-permute-start.4 = (f32[64,3072]{1,0:T(8,128)}, f32[64,3072]{1,0:T(8,128)}, u32[]{:S(2)}, u32[]{:S(2)}) collective-permute-start(f32[64,3072]{1,0:T(8,128)} %get-tuple-element.43), channel_id=1, source_target_pairs={{0,7},{1,4},{2,5},{3,6},{4,3},{5,0},{6,1},{7,2},{8,15},{9,12},{10,... | collective-permute-start | bytes 2359304 | tf_op jit(solution)/shard_map/ppermute | solution.py:107
  143.9 64.3 %collective-permute-start.5 = (f32[64,3072]{1,0:T(8,128)}, f32[64,3072]{1,0:T(8,128)}, u32[]{:S(2)}, u32[]{:S(2)}) collective-permute-start(f32[64,3072]{1,0:T(8,128)} %get-tuple-element.44), channel_id=1, source_target_pairs={{0,2},{1,3},{2,0},{3,1},{4,6},{5,7},{6,4},{7,5},{8,10},{9,11},{10,... | collective-permute-start | bytes 2359304 | tf_op jit(solution)/shard_map/ppermute | solution.py:107
  145.5 62.6 %collective-permute-start.6 = (f32[64,3072]{1,0:T(8,128)}, f32[64,3072]{1,0:T(8,128)}, u32[]{:S(2)}, u32[]{:S(2)}) collective-permute-start(f32[64,3072]{1,0:T(8,128)} %get-tuple-element.45), channel_id=1, source_target_pairs={{0,6},{1,7},{2,4},{3,5},{4,2},{5,3},{6,0},{7,1},{8,14},{9,15},{10,... | collective-permute-start | bytes 2359304 | tf_op jit(solution)/shard_map/ppermute | solution.py:107
  175.1 39.2 %all-to-all-start.5 = ((f32[128,1,16]{2,1,0:T(1,128)}), f32[128,1,16]{2,1,0:T(1,128)S(1)}, u32[]{:S(2)}, u32[]{:S(2)}) async-start(f32[128,1,16]{2,1,0:T(1,128)} %bitcast.17), calls=%async_computation.5 | async-start | bytes 131072 | tf_op jit(solution)/shard_map/all_to_all | solution.py:22
  (5 other events, 95.4 us)

commit v3 on v2

v3 whole, which is shorter than its diff:
```python
import functools

import jax
import jax.numpy as jnp
from jax import lax
from jax.experimental import pallas as pl
from jax.experimental.pallas import tpu as pltpu
from jax.sharding import Mesh
from jax.sharding import PartitionSpec as P


sharpness = 2.0
ALL = ("x", "yl", "c", "yh", "z")
DIM = ("yh", "z")
YZ = ("yl", "yh", "z")
PARTS = ((0, 1536), (1536, 2560))
CAP = 16
BLK = 512


def exchange(value, axis):
    return lax.all_to_all(value, axis, split_axis=0, concat_axis=0, tiled=True)


def spread(value, axis):
    count = lax.axis_size(axis)
    copies = jnp.broadcast_to(value[None], (count,) + value.shape)
    return exchange(copies, axis)


HOPS = ((0, 0), (1, 0), (0, 1), (0, 3), (1, 2), (1, 1), (1, 3), (0, 2))
GROUPS = ((0, 1, 2, 3), (4, 5), (6, 7))


def flip_kernel(to_ref, x_ref, *refs):
    outs, turned = refs[:-1], refs[-1]
    turned[...] = x_ref[...].T
    cols = outs[0].shape[0]
    for k, o_ref in enumerate(outs):
        first = pl.multiple_of(to_ref[k] * cols, cols)
        o_ref[...] = turned[pl.ds(first, cols), :]


def flipped(table, to, start, length):
    width = table.shape[1]
    cols = width // len(HOPS)
    first = start // BLK
    spec = pl.BlockSpec((cols, BLK), lambda i, to: (0, i))
    return pl.pallas_call(
        flip_kernel,
        grid_spec=pltpu.PrefetchScalarGridSpec(
            num_scalar_prefetch=1,
            grid=(length // BLK,),
            in_specs=[pl.BlockSpec((BLK, width), lambda i, to: (first + i, 0))],
            out_specs=[spec] * len(HOPS),
            scratch_shapes=[pltpu.VMEM((width, BLK), table.dtype)],
        ),
        out_shape=[jax.ShapeDtypeStruct((cols, length), table.dtype)] * len(HOPS),
        cost_estimate=pl.CostEstimate(flops=0, transcendentals=0, bytes_accessed=8 * width * length),
        name="flip",
    )(to, table)


def place_kernel(start, rows, hops, from_ref, *refs):
    count = len(hops)
    parts, (out, held, sems_in, sems_out) = refs[:count], refs[-4:]
    loads, stores = [], []
    for k, part in enumerate(parts):
        at = pl.multiple_of(from_ref[hops[k]] * rows + start, 128)
        loads.append(pltpu.make_async_copy(part, held.at[k], sems_in.at[k]))
        stores.append(
            pltpu.make_async_copy(held.at[k], out.at[:, pl.ds(at, part.shape[1])], sems_out.at[k])
        )
    for load in loads:
        load.start()
    for load, store in zip(loads, stores):
        load.wait()
        store.start()
    for store in stores:
        store.wait()


def placed(parts, origin, hops, start, rows, held):
    count = len(hops)
    cols, length = parts[0].shape
    args = [parts[k] for k in hops]
    if held is not None:
        args.append(held)
    return pl.pallas_call(
        functools.partial(place_kernel, start, rows, hops),
        in_specs=[pl.BlockSpec(memory_space=pltpu.SMEM)] + [pl.BlockSpec(memory_space=pl.ANY)] * len(args),
        out_specs=pl.BlockSpec(memory_space=pl.ANY),
        out_shape=jax.ShapeDtypeStruct((cols, len(HOPS) * rows), parts[0].dtype),
        scratch_shapes=[
            pltpu.VMEM((count, cols, length), parts[0].dtype),
            pltpu.SemaphoreType.DMA((count,)),
            pltpu.SemaphoreType.DMA((count,)),
        ],
        input_output_aliases={} if held is None else {count + 1: 0},
        name="place",
    )(origin, *args)


def hopped(part, hop):
    dy, dz = hop
    way = [(y * 4 + z, (y ^ dy) * 4 + (z + dz) % 4) for y in range(2) for z in range(4)]
    return lax.ppermute(part, DIM, way)


def score_kernel(*refs):
    q_refs, (lvl_ref, e_ref, o_ref, ql_ref, acc_ref) = refs[:-5], refs[-5:]
    queries = ql_ref.shape[0]
    piece = queries // len(q_refs)
    step = pl.program_id(0)

    @pl.when(step == 0)
    def _():
        for k, q_ref in enumerate(q_refs):
            ql_ref[k * piece : (k + 1) * piece, :] = q_ref[...].astype(jnp.bfloat16)
        acc_ref[...] = jnp.zeros_like(acc_ref)

    ent = e_ref[...].astype(jnp.bfloat16)
    score = lax.dot_general(
        ent, ql_ref[...], (((1,), (1,)), ((), ())), preferred_element_type=jnp.float32
    )
    soft = 1.0 / (1.0 + jnp.exp(-sharpness * (score - lvl_ref[...])))
    acc_ref[...] += jnp.sum(soft.reshape(-1, 8, queries), axis=0)

    @pl.when(step == pl.num_programs(0) - 1)
    def _():
        o_ref[...] = jnp.sum(acc_ref[...], axis=0, keepdims=True)


def soft_counts(pieces, level, table):
    piece, width = pieces[0].shape
    queries = piece * len(pieces)
    rows = table.shape[0]
    eb = 512
    return pl.pallas_call(
        score_kernel,
        grid=(rows // eb,),
        in_specs=[pl.BlockSpec((piece, width), lambda i: (0, 0))] * len(pieces)
        + [
            pl.BlockSpec((1, queries), lambda i: (0, 0)),
            pl.BlockSpec((eb, width), lambda i: (i, 0)),
        ],
        out_specs=pl.BlockSpec((1, queries), lambda i: (0, 0)),
        out_shape=jax.ShapeDtypeStruct((1, queries), jnp.float32),
        scratch_shapes=[
            pltpu.VMEM((queries, width), jnp.bfloat16),
            pltpu.VMEM((8, queries), jnp.float32),
        ],
        cost_estimate=pl.CostEstimate(
            flops=2 * queries * rows * width,
            transcendentals=2 * queries * rows,
            bytes_accessed=4 * width * (rows + queries),
        ),
        name="soft_counts",
    )(*pieces, level.reshape(1, queries), table)


def pick_rows(table, ids, start):
    count = table.shape[0]
    local = ids - start
    owned = (local >= 0) & (local < count)
    picked = jnp.take(table, jnp.clip(local, 0, count - 1), axis=0, mode="clip")
    return jnp.where(owned[:, None], picked, 0.0)


def shards(entity_table, relations, thresholds, head_ids, rel_ids, thr_idx):
    rows, width = entity_table.shape
    devices = lax.axis_size(ALL)
    queries = head_ids.shape[0]
    ents = rows * devices
    me = lax.axis_index(ALL)
    core = lax.axis_index("c")
    swap = [(0, 1), (1, 0)]
    start = me * rows
    home = queries // devices

    sizes = [lax.axis_size(a) for a in ALL]
    x = lax.axis_index("x")
    classes = lambda v: v.reshape(*sizes, home).transpose(0, 2, 1, 3, 4, 5).reshape(8, queries // 8)
    high, z = lax.axis_index("yh"), lax.axis_index("z")
    hop_y = jnp.asarray([h[0] for h in HOPS], jnp.int32)
    hop_z = jnp.asarray([h[1] for h in HOPS], jnp.int32)
    to = (high ^ hop_y) * 4 + (z + hop_z) % 4
    origin = (high ^ hop_y) * 4 + (z - hop_z) % 4

    flat1 = flipped(entity_table, to, *PARTS[0])
    got1 = [flat1[0]] + [hopped(p, h) for p, h in zip(flat1[1:], HOPS[1:])]

    ids = classes(head_ids)
    owner = ids // rows
    local = ids - owner * rows
    spot = jnp.arange(queries // 8)
    same = owner[:, :, None] == owner[:, None, :]
    rank = jnp.sum((same & (spot[None, None, :] < spot[None, :, None])).astype(jnp.int32), axis=2)
    fits = jnp.max(rank) < CAP
    slot = jnp.arange(CAP)
    hit = (owner == me)[:, None, :] & (rank[:, None, :] == slot[None, :, None])
    wanted = jnp.sum(jnp.where(hit, local[:, None, :], 0), axis=2).reshape(-1)
    out_rows = jnp.take(entity_table, wanted, axis=0, mode="clip").reshape(8, CAP, width)
    found = exchange(out_rows, ("x", "c")).reshape(-1, width)
    my_class = x * 2 + core
    my_owner = jnp.take(owner, my_class, axis=0)
    my_rank = jnp.take(rank, my_class, axis=0)
    mine = ((my_owner // 16) % 2 == lax.axis_index("yl")) & (my_owner % 8 == lax.axis_index(DIM))
    source = my_owner // 32 * 2 + (my_owner // 8) % 2
    at = jnp.where(mine, source * CAP + my_rank, 0)
    part = jnp.where(mine[:, None], jnp.take(found, at, axis=0, mode="clip"), 0.0)
    part = exchange(part.reshape(16, home, width), YZ)
    head_vecs = jnp.sum(part, axis=0)

    def every_row(unused):
        full = pick_rows(entity_table, head_ids, start)
        full = exchange(full.reshape(devices, home, width), ALL)
        return jnp.sum(full, axis=0)

    head_vecs = lax.cond(fits, lambda h: h, every_row, head_vecs)
    my_rel = lax.dynamic_slice(rel_ids, (me * home,), (home,))
    query = head_vecs * jnp.take(relations, my_rel, axis=0, mode="clip")

    flat2 = flipped(entity_table, to, *PARTS[1])
    query = spread(query, YZ).reshape(-1, width)
    got2 = [flat2[0]] + [hopped(p, h) for p, h in zip(flat2[1:5], HOPS[1:5])]
    blocks = [query]
    for shift in (1, 3, 2):
        blocks.append(lax.ppermute(query, "x", [(i, (i + shift) % 4) for i in range(4)]))
    got2 += [hopped(p, h) for p, h in zip(flat2[5:], HOPS[5:])]
    others = [lax.ppermute(b, "c", swap) for b in blocks]

    hot = thr_idx[:, None] == jnp.arange(thresholds.shape[0])[None, :]
    level = classes(jnp.sum(jnp.where(hot, thresholds[None, :], 0.0), axis=1))
    turn = jnp.asarray([0, 0, 1, 3, 1, 3, 2, 2], jnp.int32)
    side = jnp.asarray([0, 1, 0, 0, 1, 1, 0, 1], jnp.int32)
    level = jnp.take(level, (x - turn) % 4 * 2 + (core ^ side), axis=0)
    calls = (
        ([blocks[0]], level[0]),
        ([others[0]], level[1]),
        (blocks[1:3], level[2:4]),
        (others[1:3], level[4:6]),
        ([blocks[3], others[3]], level[6:8]),
    )
    sums = [soft_counts(q, lv, entity_table) for q, lv in calls]
    sums = jnp.concatenate(sums, axis=1).reshape(8, queries // 8)
    place = jnp.asarray([0, 1, 2, 4, 6, 7, 3, 5], jnp.int32)
    spin = (x - jnp.arange(4)[:, None]) % 4 * 2 + (core ^ jnp.arange(2)[None, :])
    sums = jnp.take(sums, jnp.take(place, spin.reshape(8)), axis=0)
    got = exchange(sums.reshape(devices, home), ("x", "c", "yl", "yh", "z"))
    fraction = jnp.sum(got, axis=0) * (1.0 / ents)

    table = placed(got1, origin, tuple(range(8)), PARTS[0][0], rows, None)
    for group in GROUPS:
        table = placed(got2, origin, group, PARTS[1][0], rows, table)
    return (table.T, fraction)


def solution(mesh):
    fine = Mesh(mesh.devices.reshape(4, 2, 2, 2, 4), ALL)
    whole = P(ALL, None)

    return jax.shard_map(
        shards,
        mesh=fine,
        in_specs=(whole, P(), P(), P(), P(), P()),
        out_specs=(P(("x", "yl", "c"), DIM), P(ALL)),
        check_vma=False,
    )
```

time: 216 us -> 220 us (1.019)
  the two profiles are of different devices: /device:TPU:32 before, /device:TPU:1 now
where the time goes in v3:
time: 220 us; the launch traced here: 218 us
  starting transfers between devices  89.6 us (41%)
  Pallas kernels  69.1 us (31%)
  waiting for transfers between devices  33.6 us (15%)
  local copies, waits for them, and re-layouts  18.6 us (8%)
  other arithmetic  5.73 us (3%)
    ppermute x14, starting transfers between devices, hopped(): return lax.ppermute(part, DIM, way)  48.7 us
    pallas_call x5, Pallas kernels, soft_counts(): pl.pallas_call(score_kernel, grid=(rows // eb,), in_specs=[pl.BlockSpec((...  43.2 us
    all_to_all x4, starting transfers between devices, exchange(): return lax.all_to_all(value, axis, split_axis=0, concat_axis=0, tiled=True)  20.4 us
    ppermute x14, waiting for transfers between devices, hopped(): return lax.ppermute(part, DIM, way)  19.4 us
    ppermute x4, starting transfers between devices, shards(): others = [lax.ppermute(b, 'c', swap) for b in blocks]  16.2 us
    all_to_all x4, waiting for transfers between devices, exchange(): return lax.all_to_all(value, axis, split_axis=0, concat_axis=0, tiled=True)  14.2 us
    pallas_call x2, Pallas kernels, flipped(): pl.pallas_call(flip_kernel, grid_spec=pltpu.PrefetchScalarGridSpec(num_sc...  13.6 us
    pallas_call x4, Pallas kernels, placed(): pl.pallas_call(functools.partial(place_kernel, start, rows, hops), in_spe...  12.4 us
  transfers between devices with their start and end apart: 25, of which 4 were waited for; matrix products, arithmetic and copies ran while one was open for 7% of the time, Pallas kernels for 32%

profile of v3, /device:TPU:1, one launch (start us, length us, event | category | flops | bytes accessed | tf_op | source)
XLA Modules:
  0.0 218.5 jit_solution(2514942891905596240)
XLA Ops:
  2.9 5.0 %gather_fusion.1 = f32[128,512]{1,0:T(8,128)} fusion(f32[4096,512]{1,0:T(8,128)} %refs_3_.5, s32[1024]{0:T(1024)S(1)} %pad_clamp_fusion.4), kind=kCustom, calls=%fused_computation.3 | custom fusion | bytes 524800 | tf_op jit(solution)/shard_map/jit(_take)/gather | solution.py:203
  7.8 5.8 %all-to-all-start.1 = ((f32[8,16,512]{2,1,0:T(8,128)}), f32[8,16,512]{2,1,0:T(8,128)S(1)}, u32[]{:S(2)}, u32[]{:S(2)}) async-start(f32[8,16,512]{2,1,0:T(8,128)} %bitcast.5), calls=%async_computation.1 | async-start | bytes 524288 | tf_op jit(solution)/shard_map/all_to_all | solution.py:22
  14.8 5.7 %flip.3 = (f32[64,1536]{1,0:T(8,128)}, f32[64,1536]{1,0:T(8,128)}, f32[64,1536]{1,0:T(8,128)}, f32[64,1536]{1,0:T(8,128)}, f32[64,1536]{1,0:T(8,128)}, /*index=5...) custom-call(s32[8]{0:T(128)} %get-tuple-element.78.to_ref, f32[4096,512]{1,0:T(8,128)} %refs_3_.5), custom_call_target="tpu_custom_call" | custom-call | bytes 6291456 | tf_op jit(solution)/shard_map/flip/pallas_call | solution.py:49
  29.3 3.6 %all-to-all-start.2 = ((f32[16,16,512]{2,1,0:T(8,128)}), f32[16,16,512]{2,1,0:T(8,128)S(1)}, u32[]{:S(2)}, u32[]{:S(2)}) async-start(f32[16,16,512]{2,1,0:T(8,128)} %broadcast_select_fusion.1), calls=%async_computation.2 | async-start | bytes 1048576 | tf_op jit(solution)/shard_map/all_to_all | solution.py:22
  35.9 6.9 %all-to-all-done.2 = f32[16,16,512]{2,1,0:T(8,128)S(1)} async-done(((f32[16,16,512]{2,1,0:T(8,128)}), f32[16,16,512]{2,1,0:T(8,128)S(1)}, u32[]{:S(2)}, u32[]{:S(2)}) %all-to-all-start.2) | async-done | bytes 524320 | tf_op jit(solution)/shard_map/all_to_all | solution.py:22
  43.7 3.6 %all-to-all-start.3 = ((f32[16,16,512]{2,1,0:T(8,128)}), f32[16,16,512]{2,1,0:T(8,128)S(1)}, u32[]{:S(2)}, u32[]{:S(2)}) async-start(f32[16,16,512]{2,1,0:T(8,128)} %broadcast_in_dim.119), calls=%async_computation.3 | async-start | bytes 1048576 | tf_op jit(solution)/shard_map/all_to_all | solution.py:22
  49.1 7.3 %all-to-all-done.3 = f32[16,16,512]{2,1,0:T(8,128)S(1)} async-done(((f32[16,16,512]{2,1,0:T(8,128)}), f32[16,16,512]{2,1,0:T(8,128)S(1)}, u32[]{:S(2)}, u32[]{:S(2)}) %all-to-all-start.3) | async-done | bytes 524320 | tf_op jit(solution)/shard_map/all_to_all | solution.py:22
  65.7 4.6 %collective-permute-done.10.refs_4_ = f32[64,1536]{1,0:T(8,128)S(1)} collective-permute-done((f32[64,1536]{1,0:T(8,128)}, f32[64,1536]{1,0:T(8,128)S(1)}, u32[]{:S(2)}, u32[]{:S(2)}) %collective-permute-start.10) | collective-permute-done | bytes 393248 | tf_op jit(solution)/shard_map/ppermute | solution.py:107
  70.3 9.0 %collective-permute-start.14 = (f32[256,512]{1,0:T(8,128)S(1)}, f32[256,512]{1,0:T(8,128)}, u32[]{:S(2)}, u32[]{:S(2)}) collective-permute-start(f32[256,512]{1,0:T(8,128)S(1)} %bitcast.31), channel_id=1, source_target_pairs={{0,8},{8,0},{1,9},{9,1},{2,10},{10,2},{3,11},{11,3},{4,12},{12,4},... | collective-permute-start | bytes 1572872 | tf_op jit(solution)/shard_map/ppermute | solution.py:231
  82.4 3.5 %collective-permute-start.17 = (f32[256,512]{1,0:T(8,128)}, f32[256,512]{1,0:T(8,128)}, u32[]{:S(2)}, u32[]{:S(2)}) collective-permute-start(f32[256,512]{1,0:T(8,128)} %collective-permute-done.15.refs_0_), channel_id=1, source_target_pairs={{0,8},{8,0},{1,9},{9,1},{2,10},{10,2},{3,11},{11,3},{4,12},{12,4},... | collective-permute-start | bytes 1572872 | tf_op jit(solution)/shard_map/ppermute | solution.py:231
  85.9 7.9 %flip.2 = (f32[64,2560]{1,0:T(8,128)}, f32[64,2560]{1,0:T(8,128)}, f32[64,2560]{1,0:T(8,128)}, f32[64,2560]{1,0:T(8,128)}, f32[64,2560]{1,0:T(8,128)}, /*index=5...) custom-call(s32[8]{0:T(128)} %get-tuple-element.78.to_ref, f32[4096,512]{1,0:T(8,128)} %refs_3_.5), custom_call_target="tpu_custom_call" | custom-call | bytes 10485760 | tf_op jit(solution)/shard_map/flip/pallas_call | solution.py:49
  95.6 7.7 %soft_counts.5 = f32[1,256]{1,0:T(1,128)} custom-call(f32[256,512]{1,0:T(8,128)} %bitcast.32, f32[1,256]{1,0:T(1,128)} %get-tuple-element.75.refs_1_, f32[4096,512]{1,0:T(8,128)} %refs_3_.5), custom_call_target="tpu_custom_call" | custom-call | flops 1073741824 | bytes 8912896 | tf_op jit(solution)/shard_map/soft_counts/pallas_call | solution.py:139
  106.2 9.3 %soft_counts.7 = f32[1,512]{1,0:T(1,128)} custom-call(f32[256,512]{1,0:T(8,128)} %collective-permute-done.15.refs_0_, f32[256,512]{1,0:T(8,128)} %collective-permute-done.16.refs_1_, f32[1,512]{1,0:T(1,128)} %bitcast.38, f32[4096,512]{1,0:T(8,128)} %refs_3_.5), custom_call_target="tpu_custom_call" | custom-call | flops 2147483648 | bytes 9437184 | tf_op jit(solution)/shard_map/soft_counts/pallas_call | solution.py:139
  116.0 7.7 %soft_counts.6 = f32[1,256]{1,0:T(1,128)} custom-call(f32[256,512]{1,0:T(8,128)} %collective-permute-done.14.refs_0_, f32[1,256]{1,0:T(1,128)} %get-tuple-element.74.refs_1_, f32[4096,512]{1,0:T(8,128)} %refs_3_.5), custom_call_target="tpu_custom_call" | custom-call | flops 1073741824 | bytes 8912896 | tf_op jit(solution)/shard_map/soft_counts/pallas_call | solution.py:139
  123.7 4.1 %collective-permute-start.12 = (f32[64,1536]{1,0:T(8,128)}, f32[64,1536]{1,0:T(8,128)}, u32[]{:S(2)}, u32[]{:S(2)}) collective-permute-start(f32[64,1536]{1,0:T(8,128)} %get-tuple-element.52), channel_id=1, source_target_pairs={{0,7},{1,4},{2,5},{3,6},{4,3},{5,0},{6,1},{7,2},{8,15},{9,12},{10,... | collective-permute-start | bytes 1179656 | tf_op jit(solution)/shard_map/ppermute | solution.py:107
  129.0 9.2 %soft_counts.8 = f32[1,512]{1,0:T(1,128)} custom-call(f32[256,512]{1,0:T(8,128)} %collective-permute-done.17.refs_0_, f32[256,512]{1,0:T(8,128)} %collective-permute-done.18.refs_1_, f32[1,512]{1,0:T(1,128)} %bitcast.37, f32[4096,512]{1,0:T(8,128)} %refs_3_.5), custom_call_target="tpu_custom_call" | custom-call | flops 2147483648 | bytes 9437184 | tf_op jit(solution)/shard_map/soft_counts/pallas_call | solution.py:139
  138.2 4.7 %collective-permute-start = (f32[64,2560]{1,0:T(8,128)}, f32[64,2560]{1,0:T(8,128)}, u32[]{:S(2)}, u32[]{:S(2)}) collective-permute-start(f32[64,2560]{1,0:T(8,128)} %get-tuple-element.38), channel_id=1, source_target_pairs={{0,7},{1,4},{2,5},{3,6},{4,3},{5,0},{6,1},{7,2},{8,15},{9,12},{10,... | collective-permute-start | bytes 1966088 | tf_op jit(solution)/shard_map/ppermute | solution.py:107
  142.9 3.5 %collective-permute-start.2 = (f32[64,2560]{1,0:T(8,128)}, f32[64,2560]{1,0:T(8,128)}, u32[]{:S(2)}, u32[]{:S(2)}) collective-permute-start(f32[64,2560]{1,0:T(8,128)} %get-tuple-element.40), channel_id=1, source_target_pairs={{0,6},{1,7},{2,4},{3,5},{4,2},{5,3},{6,0},{7,1},{8,14},{9,15},{10,... | collective-permute-start | bytes 1966088 | tf_op jit(solution)/shard_map/ppermute | solution.py:107
  146.4 21.6 %collective-permute-start.3 = (f32[64,2560]{1,0:T(8,128)}, f32[64,2560]{1,0:T(8,128)}, u32[]{:S(2)}, u32[]{:S(2)}) collective-permute-start(f32[64,2560]{1,0:T(8,128)} %get-tuple-element.41), channel_id=1, source_target_pairs={{0,5},{1,6},{2,7},{3,4},{4,1},{5,2},{6,3},{7,0},{8,13},{9,14},{10,... | collective-permute-start | bytes 1966088 | tf_op jit(solution)/shard_map/ppermute | solution.py:107
  170.6 9.2 %soft_counts.9 = f32[1,512]{1,0:T(1,128)} custom-call(f32[256,512]{1,0:T(8,128)} %copy-done.5, f32[256,512]{1,0:T(8,128)} %copy-done.6, f32[1,512]{1,0:T(1,128)} %bitcast.36, f32[4096,512]{1,0:T(8,128)} %refs_3_.5), custom_call_target="tpu_custom_call" | custom-call | flops 2147483648 | bytes 9437184 | tf_op jit(solution)/shard_map/soft_counts/pallas_call | solution.py:139
  183.1 7.4 %all-to-all-start.4 = ((f32[128,1,16]{2,1,0:T(1,128)}), f32[128,1,16]{2,1,0:T(1,128)S(1)}, u32[]{:S(2)}, u32[]{:S(2)}) async-start(f32[128,1,16]{2,1,0:T(1,128)} %bitcast.11), calls=%async_computation.4 | async-start | bytes 131072 | tf_op jit(solution)/shard_map/all_to_all | solution.py:22
  190.5 3.5 %place.4.refs_4_ = f32[64,32768]{1,0:T(8,128)} custom-call(s32[8]{0:T(128)} %get-tuple-element.79.from_ref, f32[64,1536]{1,0:T(8,128)} %get-tuple-element.46.refs_0_, f32[64,1536]{1,0:T(8,128)} %copy-done.7, f32[64,1536]{1,0:T(8,128)} %copy-done.8, f32[64,1536]{1,0:T(8,128)} %collective-permute-done.9.refs_3_, f32[64,1536]{1,0:T(8,128)} %copy-done.9, ...), custom_call_target="tpu_custom_call" | custom-call | tf_op jit(solution)/shard_map/place/pallas_call | solution.py:89
  194.0 14.7 %collective-permute-done.6.refs_3_ = f32[64,2560]{1,0:T(8,128)} collective-permute-done((f32[64,2560]{1,0:T(8,128)}, f32[64,2560]{1,0:T(8,128)}, u32[]{:S(2)}, u32[]{:S(2)}) %collective-permute-start.6) | collective-permute-done | bytes 655392 | tf_op jit(solution)/shard_map/ppermute | solution.py:107
  208.7 3.3 %place.5.refs_2_ = f32[64,32768]{1,0:T(8,128)} custom-call(s32[8]{0:T(128)} %get-tuple-element.79.from_ref, f32[64,2560]{1,0:T(8,128)} %get-tuple-element.42.refs_0_, f32[64,2560]{1,0:T(8,128)} %copy-done.3, f32[64,2560]{1,0:T(8,128)} %copy-done.4, f32[64,2560]{1,0:T(8,128)} %collective-permute-done.6.refs_3_, ...), custom_call_target="tpu_custom_call", output_to_operand_aliasing={{}: (5, {})} | custom-call | tf_op jit(solution)/shard_map/place/pallas_call | solution.py:89
  (130 shorter events, 47.9 us)
Async XLA Ops:
  7.8 19.6 %all-to-all-start.1 = ((f32[8,16,512]{2,1,0:T(8,128)}), f32[8,16,512]{2,1,0:T(8,128)S(1)}, u32[]{:S(2)}, u32[]{:S(2)}) async-start(f32[8,16,512]{2,1,0:T(8,128)} %bitcast.5), calls=%async_computation.1 | async-start | bytes 524288 | tf_op jit(solution)/shard_map/all_to_all | solution.py:22
  20.5 38.6 %collective-permute-start.7 = (f32[64,1536]{1,0:T(8,128)}, f32[64,1536]{1,0:T(8,128)S(1)}, u32[]{:S(2)}, u32[]{:S(2)}) collective-permute-start(f32[64,1536]{1,0:T(8,128)} %get-tuple-element.47), channel_id=1, source_target_pairs={{0,4},{1,5},{2,6},{3,7},{4,0},{5,1},{6,2},{7,3},{8,12},{9,13},{10,... | collective-permute-start | bytes 1179656 | tf_op jit(solution)/shard_map/ppermute | solution.py:107
  23.5 37.5 %collective-permute-start.8 = (f32[64,1536]{1,0:T(8,128)}, f32[64,1536]{1,0:T(8,128)S(1)}, u32[]{:S(2)}, u32[]{:S(2)}) collective-permute-start(f32[64,1536]{1,0:T(8,128)} %get-tuple-element.48), channel_id=1, source_target_pairs={{0,1},{1,2},{2,3},{3,0},{4,5},{5,6},{6,7},{7,4},{8,9},{9,10},{10,1... | collective-permute-start | bytes 1179656 | tf_op jit(solution)/shard_map/ppermute | solution.py:107
  25.1 38.2 %collective-permute-start.9 = (f32[64,1536]{1,0:T(8,128)}, f32[64,1536]{1,0:T(8,128)}, u32[]{:S(2)}, u32[]{:S(2)}) collective-permute-start(f32[64,1536]{1,0:T(8,128)} %get-tuple-element.49), channel_id=1, source_target_pairs={{0,3},{1,0},{2,1},{3,2},{4,7},{5,4},{6,5},{7,6},{8,11},{9,8},{10,9... | collective-permute-start | bytes 1179656 | tf_op jit(solution)/shard_map/ppermute | solution.py:107
  29.3 13.5 %all-to-all-start.2 = ((f32[16,16,512]{2,1,0:T(8,128)}), f32[16,16,512]{2,1,0:T(8,128)S(1)}, u32[]{:S(2)}, u32[]{:S(2)}) async-start(f32[16,16,512]{2,1,0:T(8,128)} %broadcast_select_fusion.1), calls=%async_computation.2 | async-start | bytes 1048576 | tf_op jit(solution)/shard_map/all_to_all | solution.py:22
  43.7 12.7 %all-to-all-start.3 = ((f32[16,16,512]{2,1,0:T(8,128)}), f32[16,16,512]{2,1,0:T(8,128)S(1)}, u32[]{:S(2)}, u32[]{:S(2)}) async-start(f32[16,16,512]{2,1,0:T(8,128)} %broadcast_in_dim.119), calls=%async_computation.3 | async-start | bytes 1048576 | tf_op jit(solution)/shard_map/all_to_all | solution.py:22
  56.4 22.9 %collective-permute-start.16 = (f32[256,512]{1,0:T(8,128)S(1)}, f32[256,512]{1,0:T(8,128)}, u32[]{:S(2)}, u32[]{:S(2)}) collective-permute-start(f32[256,512]{1,0:T(8,128)S(1)} %bitcast.28), channel_id=1, source_target_pairs={{0,96},{32,0},{64,32},{96,64},{1,97},{33,1},{65,33},{97,65},{2,98}... | collective-permute-start | bytes 1572872 | tf_op jit(solution)/shard_map/ppermute | solution.py:229
  59.0 23.4 %collective-permute-start.15 = (f32[256,512]{1,0:T(8,128)S(1)}, f32[256,512]{1,0:T(8,128)}, u32[]{:S(2)}, u32[]{:S(2)}) collective-permute-start(f32[256,512]{1,0:T(8,128)S(1)} %bitcast.29), channel_id=1, source_target_pairs={{0,32},{32,64},{64,96},{96,0},{1,33},{33,65},{65,97},{97,1},{2,34}... | collective-permute-start | bytes 1572872 | tf_op jit(solution)/shard_map/ppermute | solution.py:229
  61.0 43.0 %collective-permute-start.11 = (f32[64,1536]{1,0:T(8,128)}, f32[64,1536]{1,0:T(8,128)}, u32[]{:S(2)}, u32[]{:S(2)}) collective-permute-start(f32[64,1536]{1,0:T(8,128)} %get-tuple-element.51), channel_id=1, source_target_pairs={{0,5},{1,6},{2,7},{3,4},{4,1},{5,2},{6,3},{7,0},{8,13},{9,14},{10,... | collective-permute-start | bytes 1179656 | tf_op jit(solution)/shard_map/ppermute | solution.py:107
  63.4 41.7 %collective-permute-start.19 = (f32[256,512]{1,0:T(8,128)S(1)}, f32[256,512]{1,0:T(8,128)S(1)}, u32[]{:S(2)}, u32[]{:S(2)}) collective-permute-start(f32[256,512]{1,0:T(8,128)S(1)} %bitcast.30), channel_id=1, source_target_pairs={{0,64},{32,96},{64,0},{96,32},{1,65},{33,97},{65,1},{97,33},{2,66}... | collective-permute-start | bytes 1572872 | tf_op jit(solution)/shard_map/ppermute | solution.py:229
  70.3 45.1 %collective-permute-start.14 = (f32[256,512]{1,0:T(8,128)S(1)}, f32[256,512]{1,0:T(8,128)}, u32[]{:S(2)}, u32[]{:S(2)}) collective-permute-start(f32[256,512]{1,0:T(8,128)S(1)} %bitcast.31), channel_id=1, source_target_pairs={{0,8},{8,0},{1,9},{9,1},{2,10},{10,2},{3,11},{11,3},{4,12},{12,4},... | collective-permute-start | bytes 1572872 | tf_op jit(solution)/shard_map/ppermute | solution.py:231
  79.3 44.4 %collective-permute-start.18 = (f32[256,512]{1,0:T(8,128)}, f32[256,512]{1,0:T(8,128)}, u32[]{:S(2)}, u32[]{:S(2)}) collective-permute-start(f32[256,512]{1,0:T(8,128)} %collective-permute-done.16.refs_1_), channel_id=1, source_target_pairs={{0,8},{8,0},{1,9},{9,1},{2,10},{10,2},{3,11},{11,3},{4,12},{12,4},... | collective-permute-start | bytes 1572872 | tf_op jit(solution)/shard_map/ppermute | solution.py:231
  82.4 45.4 %collective-permute-start.17 = (f32[256,512]{1,0:T(8,128)}, f32[256,512]{1,0:T(8,128)}, u32[]{:S(2)}, u32[]{:S(2)}) collective-permute-start(f32[256,512]{1,0:T(8,128)} %collective-permute-done.15.refs_0_), channel_id=1, source_target_pairs={{0,8},{8,0},{1,9},{9,1},{2,10},{10,2},{3,11},{11,3},{4,12},{12,4},... | collective-permute-start | bytes 1572872 | tf_op jit(solution)/shard_map/ppermute | solution.py:231
  104.0 38.9 %collective-permute-start.4 = (f32[64,2560]{1,0:T(8,128)}, f32[64,2560]{1,0:T(8,128)S(1)}, u32[]{:S(2)}, u32[]{:S(2)}) collective-permute-start(f32[64,2560]{1,0:T(8,128)} %get-tuple-element.43), channel_id=1, source_target_pairs={{0,4},{1,5},{2,6},{3,7},{4,0},{5,1},{6,2},{7,3},{8,12},{9,13},{10,... | collective-permute-start | bytes 1966088 | tf_op jit(solution)/shard_map/ppermute | solution.py:107
  105.9 40.6 %collective-permute-start.5 = (f32[64,2560]{1,0:T(8,128)}, f32[64,2560]{1,0:T(8,128)S(1)}, u32[]{:S(2)}, u32[]{:S(2)}) collective-permute-start(f32[64,2560]{1,0:T(8,128)} %get-tuple-element.44), channel_id=1, source_target_pairs={{0,1},{1,2},{2,3},{3,0},{4,5},{5,6},{6,7},{7,4},{8,9},{9,10},{10,1... | collective-permute-start | bytes 1966088 | tf_op jit(solution)/shard_map/ppermute | solution.py:107
  115.4 52.6 %collective-permute-start.20 = (f32[256,512]{1,0:T(8,128)}, f32[256,512]{1,0:T(8,128)S(1)}, u32[]{:S(2)}, u32[]{:S(2)}) collective-permute-start(f32[256,512]{1,0:T(8,128)} %copy-done.5), channel_id=1, source_target_pairs={{0,8},{8,0},{1,9},{9,1},{2,10},{10,2},{3,11},{11,3},{4,12},{12,4},... | collective-permute-start | bytes 1572872 | tf_op jit(solution)/shard_map/ppermute | solution.py:231
  123.7 14.5 %collective-permute-start.12 = (f32[64,1536]{1,0:T(8,128)}, f32[64,1536]{1,0:T(8,128)}, u32[]{:S(2)}, u32[]{:S(2)}) collective-permute-start(f32[64,1536]{1,0:T(8,128)} %get-tuple-element.52), channel_id=1, source_target_pairs={{0,7},{1,4},{2,5},{3,6},{4,3},{5,0},{6,1},{7,2},{8,15},{9,12},{10,... | collective-permute-start | bytes 1179656 | tf_op jit(solution)/shard_map/ppermute | solution.py:107
  127.8 15.1 %collective-permute-start.13 = (f32[64,1536]{1,0:T(8,128)}, f32[64,1536]{1,0:T(8,128)}, u32[]{:S(2)}, u32[]{:S(2)}) collective-permute-start(f32[64,1536]{1,0:T(8,128)} %get-tuple-element.53), channel_id=1, source_target_pairs={{0,2},{1,3},{2,0},{3,1},{4,6},{5,7},{6,4},{7,5},{8,10},{9,11},{10,... | collective-permute-start | bytes 1179656 | tf_op jit(solution)/shard_map/ppermute | solution.py:107
  138.2 76.7 %collective-permute-start = (f32[64,2560]{1,0:T(8,128)}, f32[64,2560]{1,0:T(8,128)}, u32[]{:S(2)}, u32[]{:S(2)}) collective-permute-start(f32[64,2560]{1,0:T(8,128)} %get-tuple-element.38), channel_id=1, source_target_pairs={{0,7},{1,4},{2,5},{3,6},{4,3},{5,0},{6,1},{7,2},{8,15},{9,12},{10,... | collective-permute-start | bytes 1966088 | tf_op jit(solution)/shard_map/ppermute | solution.py:107
  142.9 72.1 %collective-permute-start.1 = (f32[64,2560]{1,0:T(8,128)}, f32[64,2560]{1,0:T(8,128)}, u32[]{:S(2)}, u32[]{:S(2)}) collective-permute-start(f32[64,2560]{1,0:T(8,128)} %get-tuple-element.39), channel_id=1, source_target_pairs={{0,2},{1,3},{2,0},{3,1},{4,6},{5,7},{6,4},{7,5},{8,10},{9,11},{10,... | collective-permute-start | bytes 1966088 | tf_op jit(solution)/shard_map/ppermute | solution.py:107
  142.9 69.2 %collective-permute-start.2 = (f32[64,2560]{1,0:T(8,128)}, f32[64,2560]{1,0:T(8,128)}, u32[]{:S(2)}, u32[]{:S(2)}) collective-permute-start(f32[64,2560]{1,0:T(8,128)} %get-tuple-element.40), channel_id=1, source_target_pairs={{0,6},{1,7},{2,4},{3,5},{4,2},{5,3},{6,0},{7,1},{8,14},{9,15},{10,... | collective-permute-start | bytes 1966088 | tf_op jit(solution)/shard_map/ppermute | solution.py:107
  146.4 65.6 %collective-permute-start.3 = (f32[64,2560]{1,0:T(8,128)}, f32[64,2560]{1,0:T(8,128)}, u32[]{:S(2)}, u32[]{:S(2)}) collective-permute-start(f32[64,2560]{1,0:T(8,128)} %get-tuple-element.41), channel_id=1, source_target_pairs={{0,5},{1,6},{2,7},{3,4},{4,1},{5,2},{6,3},{7,0},{8,13},{9,14},{10,... | collective-permute-start | bytes 1966088 | tf_op jit(solution)/shard_map/ppermute | solution.py:107
  168.0 40.7 %collective-permute-start.6 = (f32[64,2560]{1,0:T(8,128)}, f32[64,2560]{1,0:T(8,128)}, u32[]{:S(2)}, u32[]{:S(2)}) collective-permute-start(f32[64,2560]{1,0:T(8,128)} %get-tuple-element.45), channel_id=1, source_target_pairs={{0,3},{1,0},{2,1},{3,2},{4,7},{5,4},{6,5},{7,6},{8,11},{9,8},{10,9... | collective-permute-start | bytes 1966088 | tf_op jit(solution)/shard_map/ppermute | solution.py:107
  183.1 34.7 %all-to-all-start.4 = ((f32[128,1,16]{2,1,0:T(1,128)}), f32[128,1,16]{2,1,0:T(1,128)S(1)}, u32[]{:S(2)}, u32[]{:S(2)}) async-start(f32[128,1,16]{2,1,0:T(1,128)} %bitcast.11), calls=%async_computation.4 | async-start | bytes 131072 | tf_op jit(solution)/shard_map/all_to_all | solution.py:22
  (17 other events, 295.2 us)

commit v4 on v3

v4 whole, which is shorter than its diff:
```python
import functools

import jax
import jax.numpy as jnp
from jax import lax
from jax.experimental import pallas as pl
from jax.experimental.pallas import tpu as pltpu
from jax.sharding import Mesh
from jax.sharding import PartitionSpec as P


sharpness = 2.0
ALL = ("x", "yl", "c", "yh", "z")
DIM = ("yh", "z")
YZ = ("yl", "yh", "z")
PARTS = ((0, 1536), (1536, 2560))
CAP = 16
CAP_YZ = 40
BLK = 256
SPLIT = 4
STEP = 1024
SUB = 512
SHIFTS = (0, 1, 3, 2)


def exchange(value, axis):
    return lax.all_to_all(value, axis, split_axis=0, concat_axis=0, tiled=True)


def spread(value, axis):
    count = lax.axis_size(axis)
    copies = jnp.broadcast_to(value[None], (count,) + value.shape)
    return exchange(copies, axis)


HOPS = ((0, 0), (1, 0), (0, 1), (0, 3), (1, 2), (1, 1), (1, 3), (0, 2))


def slab_to(hop):
    return (lax.axis_index("yh") ^ hop[0]) * 4 + lax.rem(lax.axis_index("z") + hop[1], 4)


def slab_from(hop):
    return (lax.axis_index("yh") ^ hop[0]) * 4 + lax.rem(lax.axis_index("z") + 4 - hop[1], 4)


def flip_kernel(x_ref, *refs):
    outs, turned = refs[:-1], refs[-1]
    turned[...] = x_ref[...].T
    cols = outs[0].shape[0]
    for hop, o_ref in zip(HOPS, outs):
        first = pl.multiple_of(slab_to(hop) * cols, cols)
        o_ref[...] = turned[pl.ds(first, cols), :]


def flipped(table, start, length):
    width = table.shape[1]
    cols = width // len(HOPS)
    first = start // BLK
    return pl.pallas_call(
        flip_kernel,
        grid=(length // BLK,),
        in_specs=[pl.BlockSpec((BLK, width), lambda i: (first + i, 0))],
        out_specs=[pl.BlockSpec((cols, BLK), lambda i: (0, i))] * len(HOPS),
        scratch_shapes=[pltpu.VMEM((width, BLK), table.dtype)],
        out_shape=[jax.ShapeDtypeStruct((cols, length), table.dtype)] * len(HOPS),
        cost_estimate=pl.CostEstimate(flops=0, transcendentals=0, bytes_accessed=8 * width * length),
        name="flip",
    )(table)


def place_kernel(start, rows, hops, *refs):
    count = len(hops)
    parts, (out, held, sems_in, sems_out) = refs[:count], refs[-4:]
    loads, stores = [], []
    for k, part in enumerate(parts):
        at = pl.multiple_of(slab_from(HOPS[hops[k]]) * rows + start, 128)
        loads.append(pltpu.make_async_copy(part, held.at[k], sems_in.at[k]))
        stores.append(
            pltpu.make_async_copy(held.at[k], out.at[:, pl.ds(at, part.shape[1])], sems_out.at[k])
        )
    for load in loads:
        load.start()
    for load, store in zip(loads, stores):
        load.wait()
        store.start()
    for store in stores:
        store.wait()


def placed(parts, hops, start, rows, held):
    count = len(hops)
    cols, length = parts[0].shape
    args = [parts[k] for k in hops]
    if held is not None:
        args.append(held)
    return pl.pallas_call(
        functools.partial(place_kernel, start, rows, hops),
        in_specs=[pl.BlockSpec(memory_space=pl.ANY)] * len(args),
        out_specs=pl.BlockSpec(memory_space=pl.ANY),
        out_shape=jax.ShapeDtypeStruct((cols, len(HOPS) * rows), parts[0].dtype),
        scratch_shapes=[
            pltpu.VMEM((count, cols, length), parts[0].dtype),
            pltpu.SemaphoreType.DMA((count,)),
            pltpu.SemaphoreType.DMA((count,)),
        ],
        input_output_aliases={} if held is None else {count: 0},
        name="place",
    )(*args)


def hopped(part, hop):
    dy, dz = hop
    way = [(y * 4 + z, (y ^ dy) * 4 + (z + dz) % 4) for y in range(2) for z in range(4)]
    return lax.ppermute(part, DIM, way)


def block_class(block):
    shift, side = block
    return lax.rem(lax.axis_index("x") + 4 - shift, 4) * 2 + (lax.axis_index("c") ^ side)


def score_kernel(blocks, *refs):
    count = len(blocks)
    q_refs, e_refs, (lvl_ref, old_ref, o_ref, ql_ref, row_ref, acc_ref, ent_ref) = (
        refs[:count],
        refs[count : count + SPLIT],
        refs[count + SPLIT :],
    )
    queries = ql_ref.shape[0]
    piece = queries // count
    step = pl.program_id(0)

    @pl.when(step == 0)
    def _():
        for k, block in enumerate(blocks):
            ql_ref[k * piece : (k + 1) * piece, :] = q_refs[k][...].astype(jnp.bfloat16)
            row_ref[:, k * piece : (k + 1) * piece] = lvl_ref[pl.ds(block_class(block), 1), :]
        acc_ref[...] = jnp.zeros_like(acc_ref)

    for k, e_ref in enumerate(e_refs):
        span = e_ref.shape[0]
        ent_ref[k * span : (k + 1) * span, :] = e_ref[...].astype(jnp.bfloat16)
    for first in range(0, STEP, SUB):
        score = lax.dot_general(
            ent_ref[first : first + SUB, :],
            ql_ref[...],
            (((1,), (1,)), ((), ())),
            preferred_element_type=jnp.float32,
        )
        soft = 1.0 / (1.0 + jnp.exp(-sharpness * (score - row_ref[...])))
        acc_ref[...] += jnp.sum(soft.reshape(-1, 8, queries), axis=0)

    @pl.when(step == pl.num_programs(0) - 1)
    def _():
        o_ref[...] = old_ref[...]
        for k, block in enumerate(blocks):
            total = jnp.sum(acc_ref[:, k * piece : (k + 1) * piece], axis=0, keepdims=True)
            o_ref[pl.ds(block_class(block), 1), :] = total


def soft_counts(blocks, pieces, table, level, old):
    piece, width = pieces[0].shape
    queries = piece * len(pieces)
    rows = table.shape[0]
    eb = STEP // SPLIT
    whole = pl.BlockSpec(level.shape, lambda i: (0, 0))
    return pl.pallas_call(
        functools.partial(score_kernel, blocks),
        grid=(rows // STEP,),
        in_specs=[pl.BlockSpec((piece, width), lambda i: (0, 0))] * len(pieces)
        + [pl.BlockSpec((eb, width), lambda i, j=j: (i * SPLIT + j, 0)) for j in range(SPLIT)]
        + [whole, whole],
        out_specs=whole,
        out_shape=jax.ShapeDtypeStruct(old.shape, jnp.float32),
        scratch_shapes=[
            pltpu.VMEM((queries, width), jnp.bfloat16),
            pltpu.VMEM((1, queries), jnp.float32),
            pltpu.VMEM((8, queries), jnp.float32),
            pltpu.VMEM((STEP, width), jnp.bfloat16),
        ],
        cost_estimate=pl.CostEstimate(
            flops=2 * queries * rows * width,
            transcendentals=2 * queries * rows,
            bytes_accessed=4 * width * (rows + queries),
        ),
        name="soft_counts",
    )(*pieces, *([table] * SPLIT), level, old)


def pick_rows(table, ids, start):
    count = table.shape[0]
    local = ids - start
    owned = (local >= 0) & (local < count)
    picked = jnp.take(table, jnp.clip(local, 0, count - 1), axis=0, mode="clip")
    return jnp.where(owned[:, None], picked, 0.0)


def shards(entity_table, relations, thresholds, head_ids, rel_ids, thr_idx):
    rows, width = entity_table.shape
    devices = lax.axis_size(ALL)
    queries = head_ids.shape[0]
    ents = rows * devices
    me = lax.axis_index(ALL)
    core = lax.axis_index("c")
    swap = [(0, 1), (1, 0)]
    start = me * rows
    home = queries // devices

    sizes = [lax.axis_size(a) for a in ALL]
    x = lax.axis_index("x")
    classes = lambda v: v.reshape(*sizes, home).transpose(0, 2, 1, 3, 4, 5).reshape(8, queries // 8)
    flat1 = flipped(entity_table, *PARTS[0])
    got1 = [flat1[0]] + [hopped(p, h) for p, h in zip(flat1[1:5], HOPS[1:5])]

    ids = classes(head_ids)
    owner = ids // rows
    local = ids - owner * rows
    members = queries // 8
    spot = jnp.arange(members)
    earlier = spot[None, None, :] < spot[None, :, None]

    def rank_of(key):
        same = key[:, :, None] == key[:, None, :]
        return jnp.sum((same & earlier).astype(jnp.int32), axis=2)

    rank = rank_of(owner)
    slot = jnp.arange(CAP)
    hit = (owner == me)[:, None, :] & (rank[:, None, :] == slot[None, :, None])
    wanted = jnp.sum(jnp.where(hit, local[:, None, :], 0), axis=2).reshape(-1)
    out_rows = jnp.take(entity_table, wanted, axis=0, mode="clip").reshape(8, CAP, width)
    found = exchange(out_rows, ("x", "c")).reshape(-1, width)
    got1 += [hopped(p, h) for p, h in zip(flat1[5:], HOPS[5:])]

    plane = (owner // 16) % 2 * 8 + owner % 8
    plane_rank = rank_of(plane)
    fits = (jnp.max(rank) < CAP) & (jnp.max(plane_rank) < CAP_YZ)
    source = owner // 32 * 2 + (owner // 8) % 2
    stack = jnp.stack([plane, plane_rank, source * CAP + rank, classes(rel_ids)])
    my_plane, my_rank, my_spot, my_rel = jnp.take(stack, x * 2 + core, axis=1)
    place = jnp.arange(CAP_YZ)[:, None]
    chosen = (my_plane == lax.axis_index(YZ))[None, :] & (my_rank[None, :] == place)
    from_spot = jnp.sum(jnp.where(chosen, my_spot[None, :], 0), axis=1)
    from_rel = jnp.sum(jnp.where(chosen, my_rel[None, :], 0), axis=1)
    back = my_plane * CAP_YZ + my_rank
    factor = jnp.take(relations, from_rel, axis=0, mode="clip")
    sent_rows = jnp.take(found, from_spot, axis=0, mode="clip") * factor

    def every_row(unused):
        full = pick_rows(entity_table, head_ids, start)
        full = exchange(full.reshape(devices, home, width), ALL)
        one_rel = lax.dynamic_slice(rel_ids, (me * home,), (home,))
        one = jnp.sum(full, axis=0) * jnp.take(relations, one_rel, axis=0, mode="clip")
        return spread(one, YZ).reshape(-1, width)

    flat2 = flipped(entity_table, *PARTS[1])
    query = spread(sent_rows, YZ).reshape(-1, width)
    query = jnp.take(query, back, axis=0, mode="clip")
    query = lax.cond(fits, lambda q: q, every_row, query)
    got2 = [flat2[0]] + [hopped(p, h) for p, h in zip(flat2[1:5], HOPS[1:5])]
    held = {(0, 0): query}
    for shift in SHIFTS[1:]:
        held[shift, 0] = lax.ppermute(query, "x", [(i, (i + shift) % 4) for i in range(4)])
    got2 += [hopped(p, h) for p, h in zip(flat2[5:], HOPS[5:])]
    for shift in SHIFTS:
        held[shift, 1] = lax.ppermute(held[shift, 0], "c", swap)

    hot = classes(thr_idx)[:, :, None] == jnp.arange(thresholds.shape[0])[None, None, :]
    level = jnp.sum(jnp.where(hot, thresholds[None, None, :], 0.0), axis=2)
    sums = jnp.zeros_like(level)
    for shifts in (SHIFTS[:1], SHIFTS[1:]):
        blocks = tuple((shift, side) for side in (0, 1) for shift in shifts)
        sums = soft_counts(blocks, [held[b] for b in blocks], entity_table, level, sums)
    got = exchange(sums.reshape(devices, home), ("x", "c", "yl", "yh", "z"))
    fraction = jnp.sum(got, axis=0) * (1.0 / ents)

    table = placed(got1, tuple(range(8)), PARTS[0][0], rows, None)
    table = placed(got2, tuple(range(8)), PARTS[1][0], rows, table)
    return (table.T, fraction)


def solution(mesh):
    fine = Mesh(mesh.devices.reshape(4, 2, 2, 2, 4), ALL)
    whole = P(ALL, None)

    return jax.shard_map(
        shards,
        mesh=fine,
        in_specs=(whole, P(), P(), P(), P(), P()),
        out_specs=(P(("x", "yl", "c"), DIM), P(ALL)),
        check_vma=False,
    )
```

time: 220 us -> 174 us (0.79)
  the two profiles are of different devices: /device:TPU:1 before, /device:TPU:32 now
where the time goes in v4:
time: 174 us; the launch traced here: 173 us
  waiting for transfers between devices  54.6 us (31%)
  starting transfers between devices  52.7 us (30%)
  Pallas kernels  43 us (25%)
  local copies, waits for them, and re-layouts  15.7 us (9%)
  other arithmetic  4.52 us (3%)
  between operations  2.24 us (1%)
    ppermute x14, waiting for transfers between devices, hopped(): return lax.ppermute(part, DIM, way)  43.2 us
    ppermute x14, starting transfers between devices, hopped(): return lax.ppermute(part, DIM, way)  27 us
    all_to_all x3, starting transfers between devices, exchange(): return lax.all_to_all(value, axis, split_axis=0, concat_axis=0, tiled=True)  21 us
    pallas_call x2, Pallas kernels, soft_counts(): pl.pallas_call(functools.partial(score_kernel, blocks), grid=(rows // STE...  20.7 us
    pallas_call x2, Pallas kernels, flipped(): pl.pallas_call(flip_kernel, grid=(length // BLK,), in_specs=[pl.BlockSpec...  14.9 us
    pallas_call x2, Pallas kernels, placed(): pl.pallas_call(functools.partial(place_kernel, start, rows, hops), in_spe...  7.42 us
    ppermute x3, waiting for transfers between devices, shards(): lax.ppermute(query, 'x', [(i, (i + shift) % 4) for i in range(4)])  7.28 us
    gather x1, local copies, waits for them, and re-layouts, shards(): jnp.take(entity_table, wanted, axis=0, mode='clip').reshape(8, CAP, width)  4.96 us
  transfers between devices with their start and end apart: 24, of which 9 were waited for; matrix products, arithmetic and copies ran while one was open for 4% of the time, Pallas kernels for 25%

profile of v4, /device:TPU:32, one launch (start us, length us, event | category | flops | bytes accessed | tf_op | source)
XLA Modules:
  0.0 172.8 jit_solution(12678674100882689979)
XLA Ops:
  3.3 5.0 %gather_fusion.3 = f32[128,512]{1,0:T(8,128)} fusion(f32[4096,512]{1,0:T(8,128)} %refs_9_.1, s32[1024]{0:T(1024)S(1)} %pad_clamp_fusion.4), kind=kCustom, calls=%fused_computation.3 | custom fusion | bytes 524800 | tf_op jit(solution)/shard_map/jit(_take)/gather | solution.py:231
  8.2 4.3 %all-to-all-start.2 = ((f32[8,16,512]{2,1,0:T(8,128)}), f32[8,16,512]{2,1,0:T(8,128)S(1)}, u32[]{:S(2)}, u32[]{:S(2)}) async-start(f32[8,16,512]{2,1,0:T(8,128)} %bitcast.7), calls=%async_computation.2 | async-start | bytes 524288 | tf_op jit(solution)/shard_map/all_to_all | solution.py:27
  15.9 4.1 %all-to-all-done.2 = f32[8,16,512]{2,1,0:T(8,128)S(1)} async-done(((f32[8,16,512]{2,1,0:T(8,128)}), f32[8,16,512]{2,1,0:T(8,128)S(1)}, u32[]{:S(2)}, u32[]{:S(2)}) %all-to-all-start.2) | async-done | bytes 262176 | tf_op jit(solution)/shard_map/all_to_all | solution.py:27
  21.9 8.1 %all-to-all-start.3 = ((f32[16,40,512]{2,1,0:T(8,128)}), f32[16,40,512]{2,1,0:T(8,128)S(1)}, u32[]{:S(2)}, u32[]{:S(2)}) async-start(f32[16,40,512]{2,1,0:T(8,128)} %broadcast_in_dim.137), calls=%async_computation.3 | async-start | bytes 2621440 | tf_op jit(solution)/shard_map/all_to_all | solution.py:27
  30.0 5.9 %flip.3 = (f32[64,1536]{1,0:T(8,128)}, f32[64,1536]{1,0:T(8,128)}, f32[64,1536]{1,0:T(8,128)}, f32[64,1536]{1,0:T(8,128)}, f32[64,1536]{1,0:T(8,128)}, /*index=5...) custom-call(f32[4096,512]{1,0:T(8,128)} %refs_9_.1), custom_call_target="tpu_custom_call" | custom-call | bytes 6291456 | tf_op jit(solution)/shard_map/flip/pallas_call | solution.py:60
  35.9 3.0 %collective-permute-start.7 = (f32[64,1536]{1,0:T(8,128)}, f32[64,1536]{1,0:T(8,128)S(1)}, u32[]{:S(2)}, u32[]{:S(2)}) collective-permute-start(f32[64,1536]{1,0:T(8,128)} %get-tuple-element.66), channel_id=1, source_target_pairs={{0,4},{1,5},{2,6},{3,7},{4,0},{5,1},{6,2},{7,3},{8,12},{9,13},{10,... | collective-permute-start | bytes 1179656 | tf_op jit(solution)/shard_map/ppermute | solution.py:115
  43.0 3.6 %collective-permute-start.11 = (f32[64,1536]{1,0:T(8,128)}, f32[64,1536]{1,0:T(8,128)}, u32[]{:S(2)}, u32[]{:S(2)}) collective-permute-start(f32[64,1536]{1,0:T(8,128)} %get-tuple-element.70), channel_id=1, source_target_pairs={{0,5},{1,6},{2,7},{3,4},{4,1},{5,2},{6,3},{7,0},{8,13},{9,14},{10,... | collective-permute-start | bytes 1179656 | tf_op jit(solution)/shard_map/ppermute | solution.py:115
  46.6 10.6 %collective-permute-done.7.refs_1_ = f32[64,1536]{1,0:T(8,128)S(1)} collective-permute-done((f32[64,1536]{1,0:T(8,128)}, f32[64,1536]{1,0:T(8,128)S(1)}, u32[]{:S(2)}, u32[]{:S(2)}) %collective-permute-start.7) | collective-permute-done | bytes 393248 | tf_op jit(solution)/shard_map/ppermute | solution.py:115
  57.2 9.0 %flip.2 = (f32[64,2560]{1,0:T(8,128)}, f32[64,2560]{1,0:T(8,128)}, f32[64,2560]{1,0:T(8,128)}, f32[64,2560]{1,0:T(8,128)}, f32[64,2560]{1,0:T(8,128)}, /*index=5...) custom-call(f32[4096,512]{1,0:T(8,128)} %refs_9_.1), custom_call_target="tpu_custom_call" | custom-call | bytes 10485760 | tf_op jit(solution)/shard_map/flip/pallas_call | solution.py:60
  67.0 5.3 %collective-permute-start = (f32[64,2560]{1,0:T(8,128)}, f32[64,2560]{1,0:T(8,128)S(1)}, u32[]{:S(2)}, u32[]{:S(2)}) collective-permute-start(f32[64,2560]{1,0:T(8,128)} %get-tuple-element.58), channel_id=1, source_target_pairs={{0,4},{1,5},{2,6},{3,7},{4,0},{5,1},{6,2},{7,3},{8,12},{9,13},{10,... | collective-permute-start | bytes 1966088 | tf_op jit(solution)/shard_map/ppermute | solution.py:115
  74.8 2.3 %collective-permute-start.13 = (f32[64,1536]{1,0:T(8,128)}, f32[64,1536]{1,0:T(8,128)S(1)}, u32[]{:S(2)}, u32[]{:S(2)}) collective-permute-start(f32[64,1536]{1,0:T(8,128)} %get-tuple-element.72), channel_id=1, source_target_pairs={{0,2},{1,3},{2,0},{3,1},{4,6},{5,7},{6,4},{7,5},{8,10},{9,11},{10,... | collective-permute-start | bytes 1179656 | tf_op jit(solution)/shard_map/ppermute | solution.py:115
  78.9 2.7 %collective-permute-start.15 = (f32[256,512]{1,0:T(8,128)S(1)}, f32[256,512]{1,0:T(8,128)}, u32[]{:S(2)}, u32[]{:S(2)}) collective-permute-start(f32[256,512]{1,0:T(8,128)S(1)} %get-tuple-element.100.refs_0_), channel_id=1, source_target_pairs={{0,96},{32,0},{64,32},{96,64},{1,97},{33,1},{65,33},{97,65},{2,98}... | collective-permute-start | bytes 1572872 | tf_op jit(solution)/shard_map/ppermute | solution.py:263
  84.3 6.5 %collective-permute-done.13.refs_7_ = f32[64,1536]{1,0:T(8,128)S(1)} collective-permute-done((f32[64,1536]{1,0:T(8,128)}, f32[64,1536]{1,0:T(8,128)S(1)}, u32[]{:S(2)}, u32[]{:S(2)}) %collective-permute-start.13) | collective-permute-done | bytes 393248 | tf_op jit(solution)/shard_map/ppermute | solution.py:115
  90.8 3.9 %collective-permute-done.refs_1_ = f32[64,2560]{1,0:T(8,128)S(1)} collective-permute-done((f32[64,2560]{1,0:T(8,128)}, f32[64,2560]{1,0:T(8,128)S(1)}, u32[]{:S(2)}, u32[]{:S(2)}) %collective-permute-start) | collective-permute-done | bytes 655392 | tf_op jit(solution)/shard_map/ppermute | solution.py:115
  94.7 7.3 %collective-permute-done.14.refs_0_ = f32[256,512]{1,0:T(8,128)} collective-permute-done((f32[256,512]{1,0:T(8,128)S(1)}, f32[256,512]{1,0:T(8,128)}, u32[]{:S(2)}, u32[]{:S(2)}) %collective-permute-start.14) | collective-permute-done | bytes 524320 | tf_op jit(solution)/shard_map/ppermute | solution.py:263
  103.6 4.2 %collective-permute-done.1.refs_2_ = f32[64,2560]{1,0:T(8,128)S(1)} collective-permute-done((f32[64,2560]{1,0:T(8,128)}, f32[64,2560]{1,0:T(8,128)S(1)}, u32[]{:S(2)}, u32[]{:S(2)}) %collective-permute-start.1) | collective-permute-done | bytes 655392 | tf_op jit(solution)/shard_map/ppermute | solution.py:115
  110.4 4.1 %collective-permute-start.4 = (f32[64,2560]{1,0:T(8,128)}, f32[64,2560]{1,0:T(8,128)}, u32[]{:S(2)}, u32[]{:S(2)}) collective-permute-start(f32[64,2560]{1,0:T(8,128)} %get-tuple-element.62), channel_id=1, source_target_pairs={{0,5},{1,6},{2,7},{3,4},{4,1},{5,2},{6,3},{7,0},{8,13},{9,14},{10,... | collective-permute-start | bytes 1966088 | tf_op jit(solution)/shard_map/ppermute | solution.py:115
  117.8 7.2 %soft_counts.2.refs_11_ = f32[8,256]{1,0:T(8,128)} custom-call(f32[256,512]{1,0:T(8,128)S(1)} %get-tuple-element.100.refs_0_, f32[256,512]{1,0:T(8,128)} %copy-done.4, f32[4096,512]{1,0:T(8,128)} %refs_9_.1, f32[4096,512]{1,0:T(8,128)} %refs_9_.1, f32[4096,512]{1,0:T(8,128)} %refs_9_.1, f32[4096,512]{1,0:T(8,128)} %refs_9_.1, ...), custom_call_target="tpu_custom_call" | custom-call | flops 2147483648 | bytes 9437184 | tf_op jit(solution)/shard_map/soft_counts/pallas_call | solution.py:168
  125.1 13.5 %soft_counts.3 = f32[8,256]{1,0:T(8,128)} custom-call(f32[256,512]{1,0:T(8,128)} %collective-permute-done.14.refs_0_, f32[256,512]{1,0:T(8,128)} %collective-permute-done.15.refs_1_, f32[256,512]{1,0:T(8,128)} %collective-permute-done.16.refs_2_, f32[256,512]{1,0:T(8,128)} %collective-permute-done.17.refs_3_, f32[256,512]{1,0:T(8,128)} %collective-permute-done.18.refs_4_, ...), custom_call_target="tpu_custom_call" | custom-call | flops 6442450944 | bytes 11534336 | tf_op jit(solution)/shard_map/soft_counts/pallas_call | solution.py:168
  139.9 8.6 %all-to-all-start.4 = ((f32[128,1,16]{2,1,0:T(1,128)}), f32[128,1,16]{2,1,0:T(1,128)S(1)}, u32[]{:S(2)}, u32[]{:S(2)}) async-start(f32[128,1,16]{2,1,0:T(1,128)} %bitcast.18), calls=%async_computation.4 | async-start | bytes 131072 | tf_op jit(solution)/shard_map/all_to_all | solution.py:27
  148.5 2.8 %place.2.refs_8_ = f32[64,32768]{1,0:T(8,128)} custom-call(f32[64,1536]{1,0:T(8,128)} %get-tuple-element.65.refs_0_, f32[64,1536]{1,0:T(8,128)} %copy-done.5, f32[64,1536]{1,0:T(8,128)} %copy-done.6, f32[64,1536]{1,0:T(8,128)} %copy-done.7, f32[64,1536]{1,0:T(8,128)} %copy-done.8, f32[64,1536]{1,0:T(8,128)} %collective-permute-done.11.refs_5_, ...), custom_call_target="tpu_custom_call" | custom-call | tf_op jit(solution)/shard_map/place/pallas_call | solution.py:97
  151.4 6.7 %collective-permute-done.5.refs_6_ = f32[64,2560]{1,0:T(8,128)} collective-permute-done((f32[64,2560]{1,0:T(8,128)}, f32[64,2560]{1,0:T(8,128)}, u32[]{:S(2)}, u32[]{:S(2)}) %collective-permute-start.5) | collective-permute-done | bytes 655392 | tf_op jit(solution)/shard_map/ppermute | solution.py:115
  158.1 9.4 %collective-permute-done.6.refs_7_ = f32[64,2560]{1,0:T(8,128)} collective-permute-done((f32[64,2560]{1,0:T(8,128)}, f32[64,2560]{1,0:T(8,128)}, u32[]{:S(2)}, u32[]{:S(2)}) %collective-permute-start.6) | collective-permute-done | bytes 655392 | tf_op jit(solution)/shard_map/ppermute | solution.py:115
  167.5 4.6 %place.3 = f32[64,32768]{1,0:T(8,128)} custom-call(f32[64,2560]{1,0:T(8,128)} %get-tuple-element.57.refs_0_, f32[64,2560]{1,0:T(8,128)} %copy-done, f32[64,2560]{1,0:T(8,128)} %copy-done.1, f32[64,2560]{1,0:T(8,128)} %copy-done.2, f32[64,2560]{1,0:T(8,128)} %copy-done.3, f32[64,2560]{1,0:T(8,128)} %collective-permute-done.4.refs_5_, ...), custom_call_target="tpu_custom_call", output_to_operand_aliasing={{}: (8, {})} | custom-call | tf_op jit(solution)/shard_map/place/pallas_call | solution.py:97
  (95 shorter events, 29.0 us)
Async XLA Ops:
  8.2 11.8 %all-to-all-start.2 = ((f32[8,16,512]{2,1,0:T(8,128)}), f32[8,16,512]{2,1,0:T(8,128)S(1)}, u32[]{:S(2)}, u32[]{:S(2)}) async-start(f32[8,16,512]{2,1,0:T(8,128)} %bitcast.7), calls=%async_computation.2 | async-start | bytes 524288 | tf_op jit(solution)/shard_map/all_to_all | solution.py:27
  21.9 55.3 %all-to-all-start.3 = ((f32[16,40,512]{2,1,0:T(8,128)}), f32[16,40,512]{2,1,0:T(8,128)S(1)}, u32[]{:S(2)}, u32[]{:S(2)}) async-start(f32[16,40,512]{2,1,0:T(8,128)} %broadcast_in_dim.137), calls=%async_computation.3 | async-start | bytes 2621440 | tf_op jit(solution)/shard_map/all_to_all | solution.py:27
  35.9 21.3 %collective-permute-start.7 = (f32[64,1536]{1,0:T(8,128)}, f32[64,1536]{1,0:T(8,128)S(1)}, u32[]{:S(2)}, u32[]{:S(2)}) collective-permute-start(f32[64,1536]{1,0:T(8,128)} %get-tuple-element.66), channel_id=1, source_target_pairs={{0,4},{1,5},{2,6},{3,7},{4,0},{5,1},{6,2},{7,3},{8,12},{9,13},{10,... | collective-permute-start | bytes 1179656 | tf_op jit(solution)/shard_map/ppermute | solution.py:115
  38.9 27.3 %collective-permute-start.8 = (f32[64,1536]{1,0:T(8,128)}, f32[64,1536]{1,0:T(8,128)S(1)}, u32[]{:S(2)}, u32[]{:S(2)}) collective-permute-start(f32[64,1536]{1,0:T(8,128)} %get-tuple-element.67), channel_id=1, source_target_pairs={{0,1},{1,2},{2,3},{3,0},{4,5},{5,6},{6,7},{7,4},{8,9},{9,10},{10,1... | collective-permute-start | bytes 1179656 | tf_op jit(solution)/shard_map/ppermute | solution.py:115
  40.4 34.4 %collective-permute-start.9 = (f32[64,1536]{1,0:T(8,128)}, f32[64,1536]{1,0:T(8,128)S(1)}, u32[]{:S(2)}, u32[]{:S(2)}) collective-permute-start(f32[64,1536]{1,0:T(8,128)} %get-tuple-element.68), channel_id=1, source_target_pairs={{0,3},{1,0},{2,1},{3,2},{4,7},{5,4},{6,5},{7,6},{8,11},{9,8},{10,9... | collective-permute-start | bytes 1179656 | tf_op jit(solution)/shard_map/ppermute | solution.py:115
  40.9 37.3 %collective-permute-start.10 = (f32[64,1536]{1,0:T(8,128)}, f32[64,1536]{1,0:T(8,128)S(1)}, u32[]{:S(2)}, u32[]{:S(2)}) collective-permute-start(f32[64,1536]{1,0:T(8,128)} %get-tuple-element.69), channel_id=1, source_target_pairs={{0,6},{1,7},{2,4},{3,5},{4,2},{5,3},{6,0},{7,1},{8,14},{9,15},{10,... | collective-permute-start | bytes 1179656 | tf_op jit(solution)/shard_map/ppermute | solution.py:115
  43.0 35.9 %collective-permute-start.11 = (f32[64,1536]{1,0:T(8,128)}, f32[64,1536]{1,0:T(8,128)}, u32[]{:S(2)}, u32[]{:S(2)}) collective-permute-start(f32[64,1536]{1,0:T(8,128)} %get-tuple-element.70), channel_id=1, source_target_pairs={{0,5},{1,6},{2,7},{3,4},{4,1},{5,2},{6,3},{7,0},{8,13},{9,14},{10,... | collective-permute-start | bytes 1179656 | tf_op jit(solution)/shard_map/ppermute | solution.py:115
  57.1 26.3 %collective-permute-start.12 = (f32[64,1536]{1,0:T(8,128)}, f32[64,1536]{1,0:T(8,128)}, u32[]{:S(2)}, u32[]{:S(2)}) collective-permute-start(f32[64,1536]{1,0:T(8,128)} %get-tuple-element.71), channel_id=1, source_target_pairs={{0,7},{1,4},{2,5},{3,6},{4,3},{5,0},{6,1},{7,2},{8,15},{9,12},{10,... | collective-permute-start | bytes 1179656 | tf_op jit(solution)/shard_map/ppermute | solution.py:115
  67.0 27.8 %collective-permute-start = (f32[64,2560]{1,0:T(8,128)}, f32[64,2560]{1,0:T(8,128)S(1)}, u32[]{:S(2)}, u32[]{:S(2)}) collective-permute-start(f32[64,2560]{1,0:T(8,128)} %get-tuple-element.58), channel_id=1, source_target_pairs={{0,4},{1,5},{2,6},{3,7},{4,0},{5,1},{6,2},{7,3},{8,12},{9,13},{10,... | collective-permute-start | bytes 1966088 | tf_op jit(solution)/shard_map/ppermute | solution.py:115
  74.8 16.0 %collective-permute-start.13 = (f32[64,1536]{1,0:T(8,128)}, f32[64,1536]{1,0:T(8,128)S(1)}, u32[]{:S(2)}, u32[]{:S(2)}) collective-permute-start(f32[64,1536]{1,0:T(8,128)} %get-tuple-element.72), channel_id=1, source_target_pairs={{0,2},{1,3},{2,0},{3,1},{4,6},{5,7},{6,4},{7,5},{8,10},{9,11},{10,... | collective-permute-start | bytes 1179656 | tf_op jit(solution)/shard_map/ppermute | solution.py:115
  78.2 23.8 %collective-permute-start.14 = (f32[256,512]{1,0:T(8,128)S(1)}, f32[256,512]{1,0:T(8,128)}, u32[]{:S(2)}, u32[]{:S(2)}) collective-permute-start(f32[256,512]{1,0:T(8,128)S(1)} %get-tuple-element.100.refs_0_), channel_id=1, source_target_pairs={{0,32},{32,64},{64,96},{96,0},{1,33},{33,65},{65,97},{97,1},{2,34}... | collective-permute-start | bytes 1572872 | tf_op jit(solution)/shard_map/ppermute | solution.py:263
  78.9 23.1 %collective-permute-start.15 = (f32[256,512]{1,0:T(8,128)S(1)}, f32[256,512]{1,0:T(8,128)}, u32[]{:S(2)}, u32[]{:S(2)}) collective-permute-start(f32[256,512]{1,0:T(8,128)S(1)} %get-tuple-element.100.refs_0_), channel_id=1, source_target_pairs={{0,96},{32,0},{64,32},{96,64},{1,97},{33,1},{65,33},{97,65},{2,98}... | collective-permute-start | bytes 1572872 | tf_op jit(solution)/shard_map/ppermute | solution.py:263
  83.4 19.1 %collective-permute-start.16 = (f32[256,512]{1,0:T(8,128)S(1)}, f32[256,512]{1,0:T(8,128)}, u32[]{:S(2)}, u32[]{:S(2)}) collective-permute-start(f32[256,512]{1,0:T(8,128)S(1)} %get-tuple-element.100.refs_0_), channel_id=1, source_target_pairs={{0,64},{32,96},{64,0},{96,32},{1,65},{33,97},{65,1},{97,33},{2,66}... | collective-permute-start | bytes 1572872 | tf_op jit(solution)/shard_map/ppermute | solution.py:263
  90.8 17.0 %collective-permute-start.1 = (f32[64,2560]{1,0:T(8,128)}, f32[64,2560]{1,0:T(8,128)S(1)}, u32[]{:S(2)}, u32[]{:S(2)}) collective-permute-start(f32[64,2560]{1,0:T(8,128)} %get-tuple-element.59), channel_id=1, source_target_pairs={{0,1},{1,2},{2,3},{3,0},{4,5},{5,6},{6,7},{7,4},{8,9},{9,10},{10,1... | collective-permute-start | bytes 1966088 | tf_op jit(solution)/shard_map/ppermute | solution.py:115
  94.7 13.4 %collective-permute-start.20 = (f32[256,512]{1,0:T(8,128)S(1)}, f32[256,512]{1,0:T(8,128)S(1)}, u32[]{:S(2)}, u32[]{:S(2)}) collective-permute-start(f32[256,512]{1,0:T(8,128)S(1)} %get-tuple-element.100.refs_0_), channel_id=1, source_target_pairs={{0,8},{8,0},{1,9},{9,1},{2,10},{10,2},{3,11},{11,3},{4,12},{12,4},... | collective-permute-start | bytes 1572872 | tf_op jit(solution)/shard_map/ppermute | solution.py:266
  102.0 8.4 %collective-permute-start.17 = (f32[256,512]{1,0:T(8,128)}, f32[256,512]{1,0:T(8,128)}, u32[]{:S(2)}, u32[]{:S(2)}) collective-permute-start(f32[256,512]{1,0:T(8,128)} %collective-permute-done.14.refs_0_), channel_id=1, source_target_pairs={{0,8},{8,0},{1,9},{9,1},{2,10},{10,2},{3,11},{11,3},{4,12},{12,4},... | collective-permute-start | bytes 1572872 | tf_op jit(solution)/shard_map/ppermute | solution.py:266
  102.0 12.5 %collective-permute-start.18 = (f32[256,512]{1,0:T(8,128)}, f32[256,512]{1,0:T(8,128)}, u32[]{:S(2)}, u32[]{:S(2)}) collective-permute-start(f32[256,512]{1,0:T(8,128)} %collective-permute-done.15.refs_1_), channel_id=1, source_target_pairs={{0,8},{8,0},{1,9},{9,1},{2,10},{10,2},{3,11},{11,3},{4,12},{12,4},... | collective-permute-start | bytes 1572872 | tf_op jit(solution)/shard_map/ppermute | solution.py:266
  102.5 12.8 %collective-permute-start.19 = (f32[256,512]{1,0:T(8,128)}, f32[256,512]{1,0:T(8,128)}, u32[]{:S(2)}, u32[]{:S(2)}) collective-permute-start(f32[256,512]{1,0:T(8,128)} %collective-permute-done.16.refs_2_), channel_id=1, source_target_pairs={{0,8},{8,0},{1,9},{9,1},{2,10},{10,2},{3,11},{11,3},{4,12},{12,4},... | collective-permute-start | bytes 1572872 | tf_op jit(solution)/shard_map/ppermute | solution.py:266
  107.8 43.5 %collective-permute-start.2 = (f32[64,2560]{1,0:T(8,128)}, f32[64,2560]{1,0:T(8,128)S(1)}, u32[]{:S(2)}, u32[]{:S(2)}) collective-permute-start(f32[64,2560]{1,0:T(8,128)} %get-tuple-element.60), channel_id=1, source_target_pairs={{0,3},{1,0},{2,1},{3,2},{4,7},{5,4},{6,5},{7,6},{8,11},{9,8},{10,9... | collective-permute-start | bytes 1966088 | tf_op jit(solution)/shard_map/ppermute | solution.py:115
  108.9 42.5 %collective-permute-start.3 = (f32[64,2560]{1,0:T(8,128)}, f32[64,2560]{1,0:T(8,128)S(1)}, u32[]{:S(2)}, u32[]{:S(2)}) collective-permute-start(f32[64,2560]{1,0:T(8,128)} %get-tuple-element.61), channel_id=1, source_target_pairs={{0,6},{1,7},{2,4},{3,5},{4,2},{5,3},{6,0},{7,1},{8,14},{9,15},{10,... | collective-permute-start | bytes 1966088 | tf_op jit(solution)/shard_map/ppermute | solution.py:115
  110.4 40.9 %collective-permute-start.4 = (f32[64,2560]{1,0:T(8,128)}, f32[64,2560]{1,0:T(8,128)}, u32[]{:S(2)}, u32[]{:S(2)}) collective-permute-start(f32[64,2560]{1,0:T(8,128)} %get-tuple-element.62), channel_id=1, source_target_pairs={{0,5},{1,6},{2,7},{3,4},{4,1},{5,2},{6,3},{7,0},{8,13},{9,14},{10,... | collective-permute-start | bytes 1966088 | tf_op jit(solution)/shard_map/ppermute | solution.py:115
  114.5 43.6 %collective-permute-start.5 = (f32[64,2560]{1,0:T(8,128)}, f32[64,2560]{1,0:T(8,128)}, u32[]{:S(2)}, u32[]{:S(2)}) collective-permute-start(f32[64,2560]{1,0:T(8,128)} %get-tuple-element.63), channel_id=1, source_target_pairs={{0,7},{1,4},{2,5},{3,6},{4,3},{5,0},{6,1},{7,2},{8,15},{9,12},{10,... | collective-permute-start | bytes 1966088 | tf_op jit(solution)/shard_map/ppermute | solution.py:115
  115.3 52.1 %collective-permute-start.6 = (f32[64,2560]{1,0:T(8,128)}, f32[64,2560]{1,0:T(8,128)}, u32[]{:S(2)}, u32[]{:S(2)}) collective-permute-start(f32[64,2560]{1,0:T(8,128)} %get-tuple-element.64), channel_id=1, source_target_pairs={{0,2},{1,3},{2,0},{3,1},{4,6},{5,7},{6,4},{7,5},{8,10},{9,11},{10,... | collective-permute-start | bytes 1966088 | tf_op jit(solution)/shard_map/ppermute | solution.py:115
  139.9 32.2 %all-to-all-start.4 = ((f32[128,1,16]{2,1,0:T(1,128)}), f32[128,1,16]{2,1,0:T(1,128)S(1)}, u32[]{:S(2)}, u32[]{:S(2)}) async-start(f32[128,1,16]{2,1,0:T(1,128)} %bitcast.18), calls=%async_computation.4 | async-start | bytes 131072 | tf_op jit(solution)/shard_map/all_to_all | solution.py:27
  (13 other events, 210.8 us)

commit v5 on v4

--- a/solution.py
+++ b/solution.py
@@ -16,10 +16,10 @@
 PARTS = ((0, 1536), (1536, 2560))
 CAP = 16
 CAP_YZ = 40
-BLK = 256
-SPLIT = 4
+BLK = 512
+SPLIT = 8
 STEP = 1024
-SUB = 512
+SUB = 256
 SHIFTS = (0, 1, 3, 2)
 
 
@@ -211,7 +211,7 @@
     x = lax.axis_index("x")
     classes = lambda v: v.reshape(*sizes, home).transpose(0, 2, 1, 3, 4, 5).reshape(8, queries // 8)
     flat1 = flipped(entity_table, *PARTS[0])
-    got1 = [flat1[0]] + [hopped(p, h) for p, h in zip(flat1[1:5], HOPS[1:5])]
+    got1 = [flat1[0]] + [hopped(p, h) for p, h in zip(flat1[1:7], HOPS[1:7])]
 
     ids = classes(head_ids)
     owner = ids // rows
@@ -230,7 +230,7 @@
     wanted = jnp.sum(jnp.where(hit, local[:, None, :], 0), axis=2).reshape(-1)
     out_rows = jnp.take(entity_table, wanted, axis=0, mode="clip").reshape(8, CAP, width)
     found = exchange(out_rows, ("x", "c")).reshape(-1, width)
-    got1 += [hopped(p, h) for p, h in zip(flat1[5:], HOPS[5:])]
+    got1 += [hopped(p, h) for p, h in zip(flat1[7:], HOPS[7:])]
 
     plane = (owner // 16) % 2 * 8 + owner % 8
     plane_rank = rank_of(plane)
@@ -257,11 +257,11 @@
     query = spread(sent_rows, YZ).reshape(-1, width)
     query = jnp.take(query, back, axis=0, mode="clip")
     query = lax.cond(fits, lambda q: q, every_row, query)
-    got2 = [flat2[0]] + [hopped(p, h) for p, h in zip(flat2[1:5], HOPS[1:5])]
+    got2 = [flat2[0]] + [hopped(p, h) for p, h in zip(flat2[1:4], HOPS[1:4])]
     held = {(0, 0): query}
     for shift in SHIFTS[1:]:
         held[shift, 0] = lax.ppermute(query, "x", [(i, (i + shift) % 4) for i in range(4)])
-    got2 += [hopped(p, h) for p, h in zip(flat2[5:], HOPS[5:])]
+    got2 += [hopped(p, h) for p, h in zip(flat2[4:], HOPS[4:])]
     for shift in SHIFTS:
         held[shift, 1] = lax.ppermute(held[shift, 0], "c", swap)
 

time: 174 us -> 169 us (0.971)
  waiting for transfers between devices: 54.6 us -> 50.9 us
  Pallas kernels: 43 us -> 39.4 us
    ppermute x14, starting transfers between devices: 27 us -> 30 us  [hopped(): return lax.ppermute(part, DIM, way)]
    pallas_call x2, Pallas kernels: 14.9 us -> 12.4 us  [flipped(): pl.pallas_call(flip_kernel, grid=(length // BLK,), in_specs=[pl.BlockSpec...]
    ppermute x3, waiting for transfers between devices: 7.28 us -> 5.3 us  [shards(): lax.ppermute(query, 'x', [(i, (i + shift) % 4) for i in range(4)])]
  transfers between devices with their start and end apart: 24 -> 24, of which waited for: 9 -> 8; matrix products, arithmetic and copies ran while one was open for 4% -> 4% of each run, Pallas kernels for 25% -> 23%
where the time goes in v5:
time: 169 us; the launch traced here: 168 us
  starting transfers between devices  54.3 us (32%)
  waiting for transfers between devices  50.9 us (30%)
  Pallas kernels  39.4 us (23%)
  local copies, waits for them, and re-layouts  16.7 us (10%)
  other arithmetic  4.52 us (3%)
  between operations  2.23 us (1%)
    ppermute x14, waiting for transfers between devices, hopped(): return lax.ppermute(part, DIM, way)  41.5 us
    ppermute x14, starting transfers between devices, hopped(): return lax.ppermute(part, DIM, way)  30 us
    all_to_all x3, starting transfers between devices, exchange(): return lax.all_to_all(value, axis, split_axis=0, concat_axis=0, tiled=True)  20 us
    pallas_call x2, Pallas kernels, soft_counts(): pl.pallas_call(functools.partial(score_kernel, blocks), grid=(rows // STE...  19.6 us
    pallas_call x2, Pallas kernels, flipped(): pl.pallas_call(flip_kernel, grid=(length // BLK,), in_specs=[pl.BlockSpec...  12.4 us
    pallas_call x2, Pallas kernels, placed(): pl.pallas_call(functools.partial(place_kernel, start, rows, hops), in_spe...  7.42 us
    ppermute x3, waiting for transfers between devices, shards(): lax.ppermute(query, 'x', [(i, (i + shift) % 4) for i in range(4)])  5.3 us
    gather x1, local copies, waits for them, and re-layouts, shards(): jnp.take(entity_table, wanted, axis=0, mode='clip').reshape(8, CAP, width)  4.96 us
  transfers between devices with their start and end apart: 24, of which 8 were waited for; matrix products, arithmetic and copies ran while one was open for 4% of the time, Pallas kernels for 23%

profile of v5, /device:TPU:32, one launch (start us, length us, event | category | flops | bytes accessed | tf_op | source)
XLA Modules:
  0.0 168.1 jit_solution(6737625782889483944)
XLA Ops:
  3.3 5.0 %gather_fusion.3 = f32[128,512]{1,0:T(8,128)} fusion(f32[4096,512]{1,0:T(8,128)} %refs_13_.1, s32[1024]{0:T(1024)S(1)} %pad_clamp_fusion.4), kind=kCustom, calls=%fused_computation.3 | custom fusion | bytes 524800 | tf_op jit(solution)/shard_map/jit(_take)/gather | solution.py:231
  8.2 4.3 %all-to-all-start.2 = ((f32[8,16,512]{2,1,0:T(8,128)}), f32[8,16,512]{2,1,0:T(8,128)S(1)}, u32[]{:S(2)}, u32[]{:S(2)}) async-start(f32[8,16,512]{2,1,0:T(8,128)} %bitcast.7), calls=%async_computation.2 | async-start | bytes 524288 | tf_op jit(solution)/shard_map/all_to_all | solution.py:27
  15.9 4.1 %all-to-all-done.2 = f32[8,16,512]{2,1,0:T(8,128)S(1)} async-done(((f32[8,16,512]{2,1,0:T(8,128)}), f32[8,16,512]{2,1,0:T(8,128)S(1)}, u32[]{:S(2)}, u32[]{:S(2)}) %all-to-all-start.2) | async-done | bytes 262176 | tf_op jit(solution)/shard_map/all_to_all | solution.py:27
  21.9 8.1 %all-to-all-start.3 = ((f32[16,40,512]{2,1,0:T(8,128)}), f32[16,40,512]{2,1,0:T(8,128)S(1)}, u32[]{:S(2)}, u32[]{:S(2)}) async-start(f32[16,40,512]{2,1,0:T(8,128)} %broadcast_in_dim.137), calls=%async_computation.3 | async-start | bytes 2621440 | tf_op jit(solution)/shard_map/all_to_all | solution.py:27
  30.0 4.9 %flip.3 = (f32[64,1536]{1,0:T(8,128)}, f32[64,1536]{1,0:T(8,128)}, f32[64,1536]{1,0:T(8,128)}, f32[64,1536]{1,0:T(8,128)}, f32[64,1536]{1,0:T(8,128)}, /*index=5...) custom-call(f32[4096,512]{1,0:T(8,128)} %refs_13_.1), custom_call_target="tpu_custom_call" | custom-call | bytes 6291456 | tf_op jit(solution)/shard_map/flip/pallas_call | solution.py:60
  34.9 3.0 %collective-permute-start.7 = (f32[64,1536]{1,0:T(8,128)}, f32[64,1536]{1,0:T(8,128)S(1)}, u32[]{:S(2)}, u32[]{:S(2)}) collective-permute-start(f32[64,1536]{1,0:T(8,128)} %get-tuple-element.66), channel_id=1, source_target_pairs={{0,4},{1,5},{2,6},{3,7},{4,0},{5,1},{6,2},{7,3},{8,12},{9,13},{10,... | collective-permute-start | bytes 1179656 | tf_op jit(solution)/shard_map/ppermute | solution.py:115
  42.0 3.6 %collective-permute-start.11 = (f32[64,1536]{1,0:T(8,128)}, f32[64,1536]{1,0:T(8,128)}, u32[]{:S(2)}, u32[]{:S(2)}) collective-permute-start(f32[64,1536]{1,0:T(8,128)} %get-tuple-element.70), channel_id=1, source_target_pairs={{0,5},{1,6},{2,7},{3,4},{4,1},{5,2},{6,3},{7,0},{8,13},{9,14},{10,... | collective-permute-start | bytes 1179656 | tf_op jit(solution)/shard_map/ppermute | solution.py:115
  45.6 11.6 %collective-permute-done.7.refs_1_ = f32[64,1536]{1,0:T(8,128)S(1)} collective-permute-done((f32[64,1536]{1,0:T(8,128)}, f32[64,1536]{1,0:T(8,128)S(1)}, u32[]{:S(2)}, u32[]{:S(2)}) %collective-permute-start.7) | collective-permute-done | bytes 393248 | tf_op jit(solution)/shard_map/ppermute | solution.py:115
  57.2 7.4 %flip.2 = (f32[64,2560]{1,0:T(8,128)}, f32[64,2560]{1,0:T(8,128)}, f32[64,2560]{1,0:T(8,128)}, f32[64,2560]{1,0:T(8,128)}, f32[64,2560]{1,0:T(8,128)}, /*index=5...) custom-call(f32[4096,512]{1,0:T(8,128)} %refs_13_.1), custom_call_target="tpu_custom_call" | custom-call | bytes 10485760 | tf_op jit(solution)/shard_map/flip/pallas_call | solution.py:60
  65.4 6.9 %collective-permute-start = (f32[64,2560]{1,0:T(8,128)}, f32[64,2560]{1,0:T(8,128)S(1)}, u32[]{:S(2)}, u32[]{:S(2)}) collective-permute-start(f32[64,2560]{1,0:T(8,128)} %get-tuple-element.58), channel_id=1, source_target_pairs={{0,4},{1,5},{2,6},{3,7},{4,0},{5,1},{6,2},{7,3},{8,12},{9,13},{10,... | collective-permute-start | bytes 1966088 | tf_op jit(solution)/shard_map/ppermute | solution.py:115
  74.8 2.3 %collective-permute-start.13 = (f32[64,1536]{1,0:T(8,128)}, f32[64,1536]{1,0:T(8,128)S(1)}, u32[]{:S(2)}, u32[]{:S(2)}) collective-permute-start(f32[64,1536]{1,0:T(8,128)} %get-tuple-element.72), channel_id=1, source_target_pairs={{0,2},{1,3},{2,0},{3,1},{4,6},{5,7},{6,4},{7,5},{8,10},{9,11},{10,... | collective-permute-start | bytes 1179656 | tf_op jit(solution)/shard_map/ppermute | solution.py:115
  78.9 2.7 %collective-permute-start.15 = (f32[256,512]{1,0:T(8,128)S(1)}, f32[256,512]{1,0:T(8,128)}, u32[]{:S(2)}, u32[]{:S(2)}) collective-permute-start(f32[256,512]{1,0:T(8,128)S(1)} %get-tuple-element.100.refs_0_), channel_id=1, source_target_pairs={{0,96},{32,0},{64,32},{96,64},{1,97},{33,1},{65,33},{97,65},{2,98}... | collective-permute-start | bytes 1572872 | tf_op jit(solution)/shard_map/ppermute | solution.py:263
  81.5 2.6 %collective-permute-done.12.refs_6_ = f32[64,1536]{1,0:T(8,128)} collective-permute-done((f32[64,1536]{1,0:T(8,128)}, f32[64,1536]{1,0:T(8,128)}, u32[]{:S(2)}, u32[]{:S(2)}) %collective-permute-start.12) | collective-permute-done | bytes 393248 | tf_op jit(solution)/shard_map/ppermute | solution.py:115
  84.5 4.0 %collective-permute-done.13.refs_7_ = f32[64,1536]{1,0:T(8,128)S(1)} collective-permute-done((f32[64,1536]{1,0:T(8,128)}, f32[64,1536]{1,0:T(8,128)S(1)}, u32[]{:S(2)}, u32[]{:S(2)}) %collective-permute-start.13) | collective-permute-done | bytes 393248 | tf_op jit(solution)/shard_map/ppermute | solution.py:115
  88.6 6.2 %collective-permute-done.refs_1_ = f32[64,2560]{1,0:T(8,128)S(1)} collective-permute-done((f32[64,2560]{1,0:T(8,128)}, f32[64,2560]{1,0:T(8,128)S(1)}, u32[]{:S(2)}, u32[]{:S(2)}) %collective-permute-start) | collective-permute-done | bytes 655392 | tf_op jit(solution)/shard_map/ppermute | solution.py:115
  94.7 5.3 %collective-permute-done.14.refs_0_ = f32[256,512]{1,0:T(8,128)} collective-permute-done((f32[256,512]{1,0:T(8,128)S(1)}, f32[256,512]{1,0:T(8,128)}, u32[]{:S(2)}, u32[]{:S(2)}) %collective-permute-start.14) | collective-permute-done | bytes 524320 | tf_op jit(solution)/shard_map/ppermute | solution.py:263
  106.9 4.7 %collective-permute-start.4 = (f32[64,2560]{1,0:T(8,128)}, f32[64,2560]{1,0:T(8,128)}, u32[]{:S(2)}, u32[]{:S(2)}) collective-permute-start(f32[64,2560]{1,0:T(8,128)} %get-tuple-element.62), channel_id=1, source_target_pairs={{0,5},{1,6},{2,7},{3,4},{4,1},{5,2},{6,3},{7,0},{8,13},{9,14},{10,... | collective-permute-start | bytes 1966088 | tf_op jit(solution)/shard_map/ppermute | solution.py:115
  111.6 2.6 %collective-permute-start.6 = (f32[64,2560]{1,0:T(8,128)}, f32[64,2560]{1,0:T(8,128)}, u32[]{:S(2)}, u32[]{:S(2)}) collective-permute-start(f32[64,2560]{1,0:T(8,128)} %get-tuple-element.64), channel_id=1, source_target_pairs={{0,2},{1,3},{2,0},{3,1},{4,6},{5,7},{6,4},{7,5},{8,10},{9,11},{10,... | collective-permute-start | bytes 1966088 | tf_op jit(solution)/shard_map/ppermute | solution.py:115
  114.8 7.1 %soft_counts.2.refs_15_ = f32[8,256]{1,0:T(8,128)} custom-call(f32[256,512]{1,0:T(8,128)S(1)} %get-tuple-element.100.refs_0_, f32[256,512]{1,0:T(8,128)} %copy-done.4, f32[4096,512]{1,0:T(8,128)} %refs_13_.1, f32[4096,512]{1,0:T(8,128)} %refs_13_.1, f32[4096,512]{1,0:T(8,128)} %refs_13_.1, f32[4096,512]{1,0:T(8,128)} %refs_13_.1, f32[4096,512]{1,0:T(8,128)} %refs_13_.1, ...), custom_call_target="tpu_custom_call" | custom-call | flops 2147483648 | bytes 9437184 | tf_op jit(solution)/shard_map/soft_counts/pallas_call | solution.py:168
  122.0 12.4 %soft_counts.3 = f32[8,256]{1,0:T(8,128)} custom-call(f32[256,512]{1,0:T(8,128)} %collective-permute-done.14.refs_0_, f32[256,512]{1,0:T(8,128)} %collective-permute-done.15.refs_1_, f32[256,512]{1,0:T(8,128)} %collective-permute-done.16.refs_2_, f32[256,512]{1,0:T(8,128)} %collective-permute-done.17.refs_3_, f32[256,512]{1,0:T(8,128)} %collective-permute-done.18.refs_4_, ...), custom_call_target="tpu_custom_call" | custom-call | flops 6442450944 | bytes 11534336 | tf_op jit(solution)/shard_map/soft_counts/pallas_call | solution.py:168
  135.8 7.6 %all-to-all-start.4 = ((f32[128,1,16]{2,1,0:T(1,128)}), f32[128,1,16]{2,1,0:T(1,128)S(1)}, u32[]{:S(2)}, u32[]{:S(2)}) async-start(f32[128,1,16]{2,1,0:T(1,128)} %bitcast.18), calls=%async_computation.4 | async-start | bytes 131072 | tf_op jit(solution)/shard_map/all_to_all | solution.py:27
  143.5 2.8 %place.2.refs_8_ = f32[64,32768]{1,0:T(8,128)} custom-call(f32[64,1536]{1,0:T(8,128)} %get-tuple-element.65.refs_0_, f32[64,1536]{1,0:T(8,128)} %copy-done.5, f32[64,1536]{1,0:T(8,128)} %copy-done.6, f32[64,1536]{1,0:T(8,128)} %copy-done.7, f32[64,1536]{1,0:T(8,128)} %copy-done.8, f32[64,1536]{1,0:T(8,128)} %collective-permute-done.11.refs_5_, ...), custom_call_target="tpu_custom_call" | custom-call | tf_op jit(solution)/shard_map/place/pallas_call | solution.py:97
  146.3 15.4 %collective-permute-done.2.refs_3_ = f32[64,2560]{1,0:T(8,128)S(1)} collective-permute-done((f32[64,2560]{1,0:T(8,128)}, f32[64,2560]{1,0:T(8,128)S(1)}, u32[]{:S(2)}, u32[]{:S(2)}) %collective-permute-start.2) | collective-permute-done | bytes 655392 | tf_op jit(solution)/shard_map/ppermute | solution.py:115
  162.8 4.6 %place.3 = f32[64,32768]{1,0:T(8,128)} custom-call(f32[64,2560]{1,0:T(8,128)} %get-tuple-element.57.refs_0_, f32[64,2560]{1,0:T(8,128)} %copy-done, f32[64,2560]{1,0:T(8,128)} %copy-done.1, f32[64,2560]{1,0:T(8,128)} %copy-done.2, f32[64,2560]{1,0:T(8,128)} %copy-done.3, f32[64,2560]{1,0:T(8,128)} %collective-permute-done.4.refs_5_, ...), custom_call_target="tpu_custom_call", output_to_operand_aliasing={{}: (8, {})} | custom-call | tf_op jit(solution)/shard_map/place/pallas_call | solution.py:97
  (95 shorter events, 27.5 us)
Async XLA Ops:
  8.2 11.8 %all-to-all-start.2 = ((f32[8,16,512]{2,1,0:T(8,128)}), f32[8,16,512]{2,1,0:T(8,128)S(1)}, u32[]{:S(2)}, u32[]{:S(2)}) async-start(f32[8,16,512]{2,1,0:T(8,128)} %bitcast.7), calls=%async_computation.2 | async-start | bytes 524288 | tf_op jit(solution)/shard_map/all_to_all | solution.py:27
  21.9 55.3 %all-to-all-start.3 = ((f32[16,40,512]{2,1,0:T(8,128)}), f32[16,40,512]{2,1,0:T(8,128)S(1)}, u32[]{:S(2)}, u32[]{:S(2)}) async-start(f32[16,40,512]{2,1,0:T(8,128)} %broadcast_in_dim.137), calls=%async_computation.3 | async-start | bytes 2621440 | tf_op jit(solution)/shard_map/all_to_all | solution.py:27
  34.9 22.2 %collective-permute-start.7 = (f32[64,1536]{1,0:T(8,128)}, f32[64,1536]{1,0:T(8,128)S(1)}, u32[]{:S(2)}, u32[]{:S(2)}) collective-permute-start(f32[64,1536]{1,0:T(8,128)} %get-tuple-element.66), channel_id=1, source_target_pairs={{0,4},{1,5},{2,6},{3,7},{4,0},{5,1},{6,2},{7,3},{8,12},{9,13},{10,... | collective-permute-start | bytes 1179656 | tf_op jit(solution)/shard_map/ppermute | solution.py:115
  37.9 26.7 %collective-permute-start.8 = (f32[64,1536]{1,0:T(8,128)}, f32[64,1536]{1,0:T(8,128)S(1)}, u32[]{:S(2)}, u32[]{:S(2)}) collective-permute-start(f32[64,1536]{1,0:T(8,128)} %get-tuple-element.67), channel_id=1, source_target_pairs={{0,1},{1,2},{2,3},{3,0},{4,5},{5,6},{6,7},{7,4},{8,9},{9,10},{10,1... | collective-permute-start | bytes 1179656 | tf_op jit(solution)/shard_map/ppermute | solution.py:115
  39.4 35.4 %collective-permute-start.9 = (f32[64,1536]{1,0:T(8,128)}, f32[64,1536]{1,0:T(8,128)S(1)}, u32[]{:S(2)}, u32[]{:S(2)}) collective-permute-start(f32[64,1536]{1,0:T(8,128)} %get-tuple-element.68), channel_id=1, source_target_pairs={{0,3},{1,0},{2,1},{3,2},{4,7},{5,4},{6,5},{7,6},{8,11},{9,8},{10,9... | collective-permute-start | bytes 1179656 | tf_op jit(solution)/shard_map/ppermute | solution.py:115
  39.9 38.3 %collective-permute-start.10 = (f32[64,1536]{1,0:T(8,128)}, f32[64,1536]{1,0:T(8,128)S(1)}, u32[]{:S(2)}, u32[]{:S(2)}) collective-permute-start(f32[64,1536]{1,0:T(8,128)} %get-tuple-element.69), channel_id=1, source_target_pairs={{0,6},{1,7},{2,4},{3,5},{4,2},{5,3},{6,0},{7,1},{8,14},{9,15},{10,... | collective-permute-start | bytes 1179656 | tf_op jit(solution)/shard_map/ppermute | solution.py:115
  42.0 36.9 %collective-permute-start.11 = (f32[64,1536]{1,0:T(8,128)}, f32[64,1536]{1,0:T(8,128)}, u32[]{:S(2)}, u32[]{:S(2)}) collective-permute-start(f32[64,1536]{1,0:T(8,128)} %get-tuple-element.70), channel_id=1, source_target_pairs={{0,5},{1,6},{2,7},{3,4},{4,1},{5,2},{6,3},{7,0},{8,13},{9,14},{10,... | collective-permute-start | bytes 1179656 | tf_op jit(solution)/shard_map/ppermute | solution.py:115
  57.1 27.0 %collective-permute-start.12 = (f32[64,1536]{1,0:T(8,128)}, f32[64,1536]{1,0:T(8,128)}, u32[]{:S(2)}, u32[]{:S(2)}) collective-permute-start(f32[64,1536]{1,0:T(8,128)} %get-tuple-element.71), channel_id=1, source_target_pairs={{0,7},{1,4},{2,5},{3,6},{4,3},{5,0},{6,1},{7,2},{8,15},{9,12},{10,... | collective-permute-start | bytes 1179656 | tf_op jit(solution)/shard_map/ppermute | solution.py:115
  65.4 29.3 %collective-permute-start = (f32[64,2560]{1,0:T(8,128)}, f32[64,2560]{1,0:T(8,128)S(1)}, u32[]{:S(2)}, u32[]{:S(2)}) collective-permute-start(f32[64,2560]{1,0:T(8,128)} %get-tuple-element.58), channel_id=1, source_target_pairs={{0,4},{1,5},{2,6},{3,7},{4,0},{5,1},{6,2},{7,3},{8,12},{9,13},{10,... | collective-permute-start | bytes 1966088 | tf_op jit(solution)/shard_map/ppermute | solution.py:115
  74.8 13.7 %collective-permute-start.13 = (f32[64,1536]{1,0:T(8,128)}, f32[64,1536]{1,0:T(8,128)S(1)}, u32[]{:S(2)}, u32[]{:S(2)}) collective-permute-start(f32[64,1536]{1,0:T(8,128)} %get-tuple-element.72), channel_id=1, source_target_pairs={{0,2},{1,3},{2,0},{3,1},{4,6},{5,7},{6,4},{7,5},{8,10},{9,11},{10,... | collective-permute-start | bytes 1179656 | tf_op jit(solution)/shard_map/ppermute | solution.py:115
  78.2 21.8 %collective-permute-start.14 = (f32[256,512]{1,0:T(8,128)S(1)}, f32[256,512]{1,0:T(8,128)}, u32[]{:S(2)}, u32[]{:S(2)}) collective-permute-start(f32[256,512]{1,0:T(8,128)S(1)} %get-tuple-element.100.refs_0_), channel_id=1, source_target_pairs={{0,32},{32,64},{64,96},{96,0},{1,33},{33,65},{65,97},{97,1},{2,34}... | collective-permute-start | bytes 1572872 | tf_op jit(solution)/shard_map/ppermute | solution.py:263
  78.9 21.2 %collective-permute-start.15 = (f32[256,512]{1,0:T(8,128)S(1)}, f32[256,512]{1,0:T(8,128)}, u32[]{:S(2)}, u32[]{:S(2)}) collective-permute-start(f32[256,512]{1,0:T(8,128)S(1)} %get-tuple-element.100.refs_0_), channel_id=1, source_target_pairs={{0,96},{32,0},{64,32},{96,64},{1,97},{33,1},{65,33},{97,65},{2,98}... | collective-permute-start | bytes 1572872 | tf_op jit(solution)/shard_map/ppermute | solution.py:263
  84.1 16.4 %collective-permute-start.16 = (f32[256,512]{1,0:T(8,128)S(1)}, f32[256,512]{1,0:T(8,128)}, u32[]{:S(2)}, u32[]{:S(2)}) collective-permute-start(f32[256,512]{1,0:T(8,128)S(1)} %get-tuple-element.100.refs_0_), channel_id=1, source_target_pairs={{0,64},{32,96},{64,0},{96,32},{1,65},{33,97},{65,1},{97,33},{2,66}... | collective-permute-start | bytes 1572872 | tf_op jit(solution)/shard_map/ppermute | solution.py:263
  88.6 14.7 %collective-permute-start.1 = (f32[64,2560]{1,0:T(8,128)}, f32[64,2560]{1,0:T(8,128)S(1)}, u32[]{:S(2)}, u32[]{:S(2)}) collective-permute-start(f32[64,2560]{1,0:T(8,128)} %get-tuple-element.59), channel_id=1, source_target_pairs={{0,1},{1,2},{2,3},{3,0},{4,5},{5,6},{6,7},{7,4},{8,9},{9,10},{10,1... | collective-permute-start | bytes 1966088 | tf_op jit(solution)/shard_map/ppermute | solution.py:115
  94.7 10.5 %collective-permute-start.20 = (f32[256,512]{1,0:T(8,128)S(1)}, f32[256,512]{1,0:T(8,128)S(1)}, u32[]{:S(2)}, u32[]{:S(2)}) collective-permute-start(f32[256,512]{1,0:T(8,128)S(1)} %get-tuple-element.100.refs_0_), channel_id=1, source_target_pairs={{0,8},{8,0},{1,9},{9,1},{2,10},{10,2},{3,11},{11,3},{4,12},{12,4},... | collective-permute-start | bytes 1572872 | tf_op jit(solution)/shard_map/ppermute | solution.py:266
  100.0 6.9 %collective-permute-start.17 = (f32[256,512]{1,0:T(8,128)}, f32[256,512]{1,0:T(8,128)}, u32[]{:S(2)}, u32[]{:S(2)}) collective-permute-start(f32[256,512]{1,0:T(8,128)} %collective-permute-done.14.refs_0_), channel_id=1, source_target_pairs={{0,8},{8,0},{1,9},{9,1},{2,10},{10,2},{3,11},{11,3},{4,12},{12,4},... | collective-permute-start | bytes 1572872 | tf_op jit(solution)/shard_map/ppermute | solution.py:266
  100.0 11.6 %collective-permute-start.18 = (f32[256,512]{1,0:T(8,128)}, f32[256,512]{1,0:T(8,128)}, u32[]{:S(2)}, u32[]{:S(2)}) collective-permute-start(f32[256,512]{1,0:T(8,128)} %collective-permute-done.15.refs_1_), channel_id=1, source_target_pairs={{0,8},{8,0},{1,9},{9,1},{2,10},{10,2},{3,11},{11,3},{4,12},{12,4},... | collective-permute-start | bytes 1572872 | tf_op jit(solution)/shard_map/ppermute | solution.py:266
  100.5 11.1 %collective-permute-start.19 = (f32[256,512]{1,0:T(8,128)}, f32[256,512]{1,0:T(8,128)}, u32[]{:S(2)}, u32[]{:S(2)}) collective-permute-start(f32[256,512]{1,0:T(8,128)} %collective-permute-done.16.refs_2_), channel_id=1, source_target_pairs={{0,8},{8,0},{1,9},{9,1},{2,10},{10,2},{3,11},{11,3},{4,12},{12,4},... | collective-permute-start | bytes 1572872 | tf_op jit(solution)/shard_map/ppermute | solution.py:266
  103.3 58.4 %collective-permute-start.2 = (f32[64,2560]{1,0:T(8,128)}, f32[64,2560]{1,0:T(8,128)S(1)}, u32[]{:S(2)}, u32[]{:S(2)}) collective-permute-start(f32[64,2560]{1,0:T(8,128)} %get-tuple-element.60), channel_id=1, source_target_pairs={{0,3},{1,0},{2,1},{3,2},{4,7},{5,4},{6,5},{7,6},{8,11},{9,8},{10,9... | collective-permute-start | bytes 1966088 | tf_op jit(solution)/shard_map/ppermute | solution.py:115
  106.0 55.7 %collective-permute-start.3 = (f32[64,2560]{1,0:T(8,128)}, f32[64,2560]{1,0:T(8,128)S(1)}, u32[]{:S(2)}, u32[]{:S(2)}) collective-permute-start(f32[64,2560]{1,0:T(8,128)} %get-tuple-element.61), channel_id=1, source_target_pairs={{0,6},{1,7},{2,4},{3,5},{4,2},{5,3},{6,0},{7,1},{8,14},{9,15},{10,... | collective-permute-start | bytes 1966088 | tf_op jit(solution)/shard_map/ppermute | solution.py:115
  106.9 54.9 %collective-permute-start.4 = (f32[64,2560]{1,0:T(8,128)}, f32[64,2560]{1,0:T(8,128)}, u32[]{:S(2)}, u32[]{:S(2)}) collective-permute-start(f32[64,2560]{1,0:T(8,128)} %get-tuple-element.62), channel_id=1, source_target_pairs={{0,5},{1,6},{2,7},{3,4},{4,1},{5,2},{6,3},{7,0},{8,13},{9,14},{10,... | collective-permute-start | bytes 1966088 | tf_op jit(solution)/shard_map/ppermute | solution.py:115
  111.6 50.1 %collective-permute-start.5 = (f32[64,2560]{1,0:T(8,128)}, f32[64,2560]{1,0:T(8,128)}, u32[]{:S(2)}, u32[]{:S(2)}) collective-permute-start(f32[64,2560]{1,0:T(8,128)} %get-tuple-element.63), channel_id=1, source_target_pairs={{0,7},{1,4},{2,5},{3,6},{4,3},{5,0},{6,1},{7,2},{8,15},{9,12},{10,... | collective-permute-start | bytes 1966088 | tf_op jit(solution)/shard_map/ppermute | solution.py:115
  111.6 50.1 %collective-permute-start.6 = (f32[64,2560]{1,0:T(8,128)}, f32[64,2560]{1,0:T(8,128)}, u32[]{:S(2)}, u32[]{:S(2)}) collective-permute-start(f32[64,2560]{1,0:T(8,128)} %get-tuple-element.64), channel_id=1, source_target_pairs={{0,2},{1,3},{2,0},{3,1},{4,6},{5,7},{6,4},{7,5},{8,10},{9,11},{10,... | collective-permute-start | bytes 1966088 | tf_op jit(solution)/shard_map/ppermute | solution.py:115
  135.8 31.6 %all-to-all-start.4 = ((f32[128,1,16]{2,1,0:T(1,128)}), f32[128,1,16]{2,1,0:T(1,128)S(1)}, u32[]{:S(2)}, u32[]{:S(2)}) async-start(f32[128,1,16]{2,1,0:T(1,128)} %bitcast.18), calls=%async_computation.4 | async-start | bytes 131072 | tf_op jit(solution)/shard_map/all_to_all | solution.py:27
  (13 other events, 170.2 us)

commit v6 on v5

--- a/solution.py
+++ b/solution.py
@@ -15,6 +15,7 @@
 YZ = ("yl", "yh", "z")
 PARTS = ((0, 1536), (1536, 2560))
 CAP = 16
+ORDER = (1, 2, 3, 5, 6, 4, 7)
 CAP_YZ = 40
 BLK = 512
 SPLIT = 8
@@ -69,15 +70,16 @@
     )(table)
 
 
-def place_kernel(start, rows, hops, *refs):
-    count = len(hops)
-    parts, (out, held, sems_in, sems_out) = refs[:count], refs[-4:]
+def place_kernel(spots, rows, *refs):
+    count = len(spots)
+    parts, (out, *rest) = refs[:count], refs[-count - 3 :]
+    held, (sems_in, sems_out) = rest[:count], rest[count:]
     loads, stores = [], []
-    for k, part in enumerate(parts):
-        at = pl.multiple_of(slab_from(HOPS[hops[k]]) * rows + start, 128)
-        loads.append(pltpu.make_async_copy(part, held.at[k], sems_in.at[k]))
+    for k, ((hop, start), part) in enumerate(zip(spots, parts)):
+        at = pl.multiple_of(slab_from(HOPS[hop]) * rows + start, 128)
+        loads.append(pltpu.make_async_copy(part, held[k], sems_in.at[k]))
         stores.append(
-            pltpu.make_async_copy(held.at[k], out.at[:, pl.ds(at, part.shape[1])], sems_out.at[k])
+            pltpu.make_async_copy(held[k], out.at[:, pl.ds(at, part.shape[1])], sems_out.at[k])
         )
     for load in loads:
         load.start()
@@ -88,22 +90,19 @@
         store.wait()
 
 
-def placed(parts, hops, start, rows, held):
-    count = len(hops)
-    cols, length = parts[0].shape
-    args = [parts[k] for k in hops]
+def placed(parts, spots, rows, held):
+    count = len(parts)
+    cols = parts[0].shape[0]
+    args = list(parts)
     if held is not None:
         args.append(held)
     return pl.pallas_call(
-        functools.partial(place_kernel, start, rows, hops),
+        functools.partial(place_kernel, spots, rows),
         in_specs=[pl.BlockSpec(memory_space=pl.ANY)] * len(args),
         out_specs=pl.BlockSpec(memory_space=pl.ANY),
         out_shape=jax.ShapeDtypeStruct((cols, len(HOPS) * rows), parts[0].dtype),
-        scratch_shapes=[
-            pltpu.VMEM((count, cols, length), parts[0].dtype),
-            pltpu.SemaphoreType.DMA((count,)),
-            pltpu.SemaphoreType.DMA((count,)),
-        ],
+        scratch_shapes=[pltpu.VMEM(part.shape, part.dtype) for part in parts]
+        + [pltpu.SemaphoreType.DMA((count,)), pltpu.SemaphoreType.DMA((count,))],
         input_output_aliases={} if held is None else {count: 0},
         name="place",
     )(*args)
@@ -257,11 +256,14 @@
     query = spread(sent_rows, YZ).reshape(-1, width)
     query = jnp.take(query, back, axis=0, mode="clip")
     query = lax.cond(fits, lambda q: q, every_row, query)
-    got2 = [flat2[0]] + [hopped(p, h) for p, h in zip(flat2[1:4], HOPS[1:4])]
+    got2 = [flat2[0]] + [None] * 7
+    for k in ORDER[:3]:
+        got2[k] = hopped(flat2[k], HOPS[k])
     held = {(0, 0): query}
     for shift in SHIFTS[1:]:
         held[shift, 0] = lax.ppermute(query, "x", [(i, (i + shift) % 4) for i in range(4)])
-    got2 += [hopped(p, h) for p, h in zip(flat2[4:], HOPS[4:])]
+    for k in ORDER[3:]:
+        got2[k] = hopped(flat2[k], HOPS[k])
     for shift in SHIFTS:
         held[shift, 1] = lax.ppermute(held[shift, 0], "c", swap)
 
@@ -274,8 +276,10 @@
     got = exchange(sums.reshape(devices, home), ("x", "c", "yl", "yh", "z"))
     fraction = jnp.sum(got, axis=0) * (1.0 / ents)
 
-    table = placed(got1, tuple(range(8)), PARTS[0][0], rows, None)
-    table = placed(got2, tuple(range(8)), PARTS[1][0], rows, table)
+    first, second = PARTS[0][0], PARTS[1][0]
+    spots = tuple((k, first) for k in range(8)) + ((0, second),)
+    table = placed(got1 + got2[:1], spots, rows, None)
+    table = placed(got2[1:], tuple((k, second) for k in range(1, 8)), rows, table)
     return (table.T, fraction)
 
 

time: 169 us -> 168 us (level)
  no operation moved by 1% of the time
where the time goes in v6:
time: 168 us; the launch traced here: 167 us
  starting transfers between devices  54.3 us (32%)
  waiting for transfers between devices  50.4 us (30%)
  Pallas kernels  39.2 us (23%)
  local copies, waits for them, and re-layouts  16.7 us (10%)
  other arithmetic  4.52 us (3%)
  between operations  2.23 us (1%)
    ppermute x14, waiting for transfers between devices, hopped(): return lax.ppermute(part, DIM, way)  40.9 us
    ppermute x14, starting transfers between devices, hopped(): return lax.ppermute(part, DIM, way)  30.1 us
    all_to_all x3, starting transfers between devices, exchange(): return lax.all_to_all(value, axis, split_axis=0, concat_axis=0, tiled=True)  20 us
    pallas_call x2, Pallas kernels, soft_counts(): pl.pallas_call(functools.partial(score_kernel, blocks), grid=(rows // STE...  19.6 us
    pallas_call x2, Pallas kernels, flipped(): pl.pallas_call(flip_kernel, grid=(length // BLK,), in_specs=[pl.BlockSpec...  12.3 us
    pallas_call x2, Pallas kernels, placed(): pl.pallas_call(functools.partial(place_kernel, spots, rows), in_specs=[pl...  7.28 us
    ppermute x3, waiting for transfers between devices, shards(): lax.ppermute(query, 'x', [(i, (i + shift) % 4) for i in range(4)])  5.3 us
    gather x1, local copies, waits for them, and re-layouts, shards(): jnp.take(entity_table, wanted, axis=0, mode='clip').reshape(8, CAP, width)  4.96 us
  transfers between devices with their start and end apart: 24, of which 8 were waited for; matrix products, arithmetic and copies ran while one was open for 4% of the time, Pallas kernels for 23%

profile of v6, /device:TPU:32, one launch (start us, length us, event | category | flops | bytes accessed | tf_op | source)
XLA Modules:
  0.0 167.4 jit_solution(41962481965965589)
XLA Ops:
  3.3 5.0 %gather_fusion.3 = f32[128,512]{1,0:T(8,128)} fusion(f32[4096,512]{1,0:T(8,128)} %refs_13_.1, s32[1024]{0:T(1024)S(1)} %pad_clamp_fusion.4), kind=kCustom, calls=%fused_computation.3 | custom fusion | bytes 524800 | tf_op jit(solution)/shard_map/jit(_take)/gather | solution.py:230
  8.2 4.3 %all-to-all-start.2 = ((f32[8,16,512]{2,1,0:T(8,128)}), f32[8,16,512]{2,1,0:T(8,128)S(1)}, u32[]{:S(2)}, u32[]{:S(2)}) async-start(f32[8,16,512]{2,1,0:T(8,128)} %bitcast.7), calls=%async_computation.2 | async-start | bytes 524288 | tf_op jit(solution)/shard_map/all_to_all | solution.py:28
  15.9 4.1 %all-to-all-done.2 = f32[8,16,512]{2,1,0:T(8,128)S(1)} async-done(((f32[8,16,512]{2,1,0:T(8,128)}), f32[8,16,512]{2,1,0:T(8,128)S(1)}, u32[]{:S(2)}, u32[]{:S(2)}) %all-to-all-start.2) | async-done | bytes 262176 | tf_op jit(solution)/shard_map/all_to_all | solution.py:28
  21.9 8.1 %all-to-all-start.3 = ((f32[16,40,512]{2,1,0:T(8,128)}), f32[16,40,512]{2,1,0:T(8,128)S(1)}, u32[]{:S(2)}, u32[]{:S(2)}) async-start(f32[16,40,512]{2,1,0:T(8,128)} %broadcast_in_dim.137), calls=%async_computation.3 | async-start | bytes 2621440 | tf_op jit(solution)/shard_map/all_to_all | solution.py:28
  30.0 4.9 %flip.3 = (f32[64,1536]{1,0:T(8,128)}, f32[64,1536]{1,0:T(8,128)}, f32[64,1536]{1,0:T(8,128)}, f32[64,1536]{1,0:T(8,128)}, f32[64,1536]{1,0:T(8,128)}, /*index=5...) custom-call(f32[4096,512]{1,0:T(8,128)} %refs_13_.1), custom_call_target="tpu_custom_call" | custom-call | bytes 6291456 | tf_op jit(solution)/shard_map/flip/pallas_call | solution.py:61
  34.9 3.0 %collective-permute-start.7 = (f32[64,1536]{1,0:T(8,128)}, f32[64,1536]{1,0:T(8,128)S(1)}, u32[]{:S(2)}, u32[]{:S(2)}) collective-permute-start(f32[64,1536]{1,0:T(8,128)} %get-tuple-element.65), channel_id=1, source_target_pairs={{0,4},{1,5},{2,6},{3,7},{4,0},{5,1},{6,2},{7,3},{8,12},{9,13},{10,... | collective-permute-start | bytes 1179656 | tf_op jit(solution)/shard_map/ppermute | solution.py:114
  42.0 3.6 %collective-permute-start.11 = (f32[64,1536]{1,0:T(8,128)}, f32[64,1536]{1,0:T(8,128)}, u32[]{:S(2)}, u32[]{:S(2)}) collective-permute-start(f32[64,1536]{1,0:T(8,128)} %get-tuple-element.69), channel_id=1, source_target_pairs={{0,5},{1,6},{2,7},{3,4},{4,1},{5,2},{6,3},{7,0},{8,13},{9,14},{10,... | collective-permute-start | bytes 1179656 | tf_op jit(solution)/shard_map/ppermute | solution.py:114
  45.6 11.6 %collective-permute-done.7.refs_1_ = f32[64,1536]{1,0:T(8,128)S(1)} collective-permute-done((f32[64,1536]{1,0:T(8,128)}, f32[64,1536]{1,0:T(8,128)S(1)}, u32[]{:S(2)}, u32[]{:S(2)}) %collective-permute-start.7) | collective-permute-done | bytes 393248 | tf_op jit(solution)/shard_map/ppermute | solution.py:114
  57.2 7.4 %flip.2 = (f32[64,2560]{1,0:T(8,128)}, f32[64,2560]{1,0:T(8,128)}, f32[64,2560]{1,0:T(8,128)}, f32[64,2560]{1,0:T(8,128)}, f32[64,2560]{1,0:T(8,128)}, /*index=5...) custom-call(f32[4096,512]{1,0:T(8,128)} %refs_13_.1), custom_call_target="tpu_custom_call" | custom-call | bytes 10485760 | tf_op jit(solution)/shard_map/flip/pallas_call | solution.py:61
  65.4 6.9 %collective-permute-start = (f32[64,2560]{1,0:T(8,128)}, f32[64,2560]{1,0:T(8,128)S(1)}, u32[]{:S(2)}, u32[]{:S(2)}) collective-permute-start(f32[64,2560]{1,0:T(8,128)} %get-tuple-element.57), channel_id=1, source_target_pairs={{0,4},{1,5},{2,6},{3,7},{4,0},{5,1},{6,2},{7,3},{8,12},{9,13},{10,... | collective-permute-start | bytes 1966088 | tf_op jit(solution)/shard_map/ppermute | solution.py:114
  74.8 2.3 %collective-permute-start.13 = (f32[64,1536]{1,0:T(8,128)}, f32[64,1536]{1,0:T(8,128)S(1)}, u32[]{:S(2)}, u32[]{:S(2)}) collective-permute-start(f32[64,1536]{1,0:T(8,128)} %get-tuple-element.71), channel_id=1, source_target_pairs={{0,2},{1,3},{2,0},{3,1},{4,6},{5,7},{6,4},{7,5},{8,10},{9,11},{10,... | collective-permute-start | bytes 1179656 | tf_op jit(solution)/shard_map/ppermute | solution.py:114
  78.9 2.7 %collective-permute-start.15 = (f32[256,512]{1,0:T(8,128)S(1)}, f32[256,512]{1,0:T(8,128)}, u32[]{:S(2)}, u32[]{:S(2)}) collective-permute-start(f32[256,512]{1,0:T(8,128)S(1)} %get-tuple-element.100.refs_0_), channel_id=1, source_target_pairs={{0,96},{32,0},{64,32},{96,64},{1,97},{33,1},{65,33},{97,65},{2,98}... | collective-permute-start | bytes 1572872 | tf_op jit(solution)/shard_map/ppermute | solution.py:264
  81.5 2.6 %collective-permute-done.12.refs_6_ = f32[64,1536]{1,0:T(8,128)} collective-permute-done((f32[64,1536]{1,0:T(8,128)}, f32[64,1536]{1,0:T(8,128)}, u32[]{:S(2)}, u32[]{:S(2)}) %collective-permute-start.12) | collective-permute-done | bytes 393248 | tf_op jit(solution)/shard_map/ppermute | solution.py:114
  84.5 4.0 %collective-permute-done.13.refs_7_ = f32[64,1536]{1,0:T(8,128)S(1)} collective-permute-done((f32[64,1536]{1,0:T(8,128)}, f32[64,1536]{1,0:T(8,128)S(1)}, u32[]{:S(2)}, u32[]{:S(2)}) %collective-permute-start.13) | collective-permute-done | bytes 393248 | tf_op jit(solution)/shard_map/ppermute | solution.py:114
  88.6 6.2 %collective-permute-done.refs_0_ = f32[64,2560]{1,0:T(8,128)S(1)} collective-permute-done((f32[64,2560]{1,0:T(8,128)}, f32[64,2560]{1,0:T(8,128)S(1)}, u32[]{:S(2)}, u32[]{:S(2)}) %collective-permute-start) | collective-permute-done | bytes 655392 | tf_op jit(solution)/shard_map/ppermute | solution.py:114
  94.7 5.3 %collective-permute-done.14.refs_0_ = f32[256,512]{1,0:T(8,128)} collective-permute-done((f32[256,512]{1,0:T(8,128)S(1)}, f32[256,512]{1,0:T(8,128)}, u32[]{:S(2)}, u32[]{:S(2)}) %collective-permute-start.14) | collective-permute-done | bytes 524320 | tf_op jit(solution)/shard_map/ppermute | solution.py:264
  106.9 4.7 %collective-permute-start.4 = (f32[64,2560]{1,0:T(8,128)}, f32[64,2560]{1,0:T(8,128)}, u32[]{:S(2)}, u32[]{:S(2)}) collective-permute-start(f32[64,2560]{1,0:T(8,128)} %get-tuple-element.61), channel_id=1, source_target_pairs={{0,5},{1,6},{2,7},{3,4},{4,1},{5,2},{6,3},{7,0},{8,13},{9,14},{10,... | collective-permute-start | bytes 1966088 | tf_op jit(solution)/shard_map/ppermute | solution.py:114
  111.6 2.6 %collective-permute-start.6 = (f32[64,2560]{1,0:T(8,128)}, f32[64,2560]{1,0:T(8,128)}, u32[]{:S(2)}, u32[]{:S(2)}) collective-permute-start(f32[64,2560]{1,0:T(8,128)} %get-tuple-element.63), channel_id=1, source_target_pairs={{0,2},{1,3},{2,0},{3,1},{4,6},{5,7},{6,4},{7,5},{8,10},{9,11},{10,... | collective-permute-start | bytes 1966088 | tf_op jit(solution)/shard_map/ppermute | solution.py:114
  114.8 7.2 %soft_counts.2.refs_15_ = f32[8,256]{1,0:T(8,128)} custom-call(f32[256,512]{1,0:T(8,128)S(1)} %get-tuple-element.100.refs_0_, f32[256,512]{1,0:T(8,128)} %copy-done.4, f32[4096,512]{1,0:T(8,128)} %refs_13_.1, f32[4096,512]{1,0:T(8,128)} %refs_13_.1, f32[4096,512]{1,0:T(8,128)} %refs_13_.1, f32[4096,512]{1,0:T(8,128)} %refs_13_.1, f32[4096,512]{1,0:T(8,128)} %refs_13_.1, ...), custom_call_target="tpu_custom_call" | custom-call | flops 2147483648 | bytes 9437184 | tf_op jit(solution)/shard_map/soft_counts/pallas_call | solution.py:167
  122.0 12.4 %soft_counts.3 = f32[8,256]{1,0:T(8,128)} custom-call(f32[256,512]{1,0:T(8,128)} %collective-permute-done.14.refs_0_, f32[256,512]{1,0:T(8,128)} %collective-permute-done.15.refs_1_, f32[256,512]{1,0:T(8,128)} %collective-permute-done.16.refs_2_, f32[256,512]{1,0:T(8,128)} %collective-permute-done.17.refs_3_, f32[256,512]{1,0:T(8,128)} %collective-permute-done.18.refs_4_, ...), custom_call_target="tpu_custom_call" | custom-call | flops 6442450944 | bytes 11534336 | tf_op jit(solution)/shard_map/soft_counts/pallas_call | solution.py:167
  135.8 7.6 %all-to-all-start.4 = ((f32[128,1,16]{2,1,0:T(1,128)}), f32[128,1,16]{2,1,0:T(1,128)S(1)}, u32[]{:S(2)}, u32[]{:S(2)}) async-start(f32[128,1,16]{2,1,0:T(1,128)} %bitcast.18), calls=%async_computation.4 | async-start | bytes 131072 | tf_op jit(solution)/shard_map/all_to_all | solution.py:28
  143.4 3.4 %place.2.refs_7_ = f32[64,32768]{1,0:T(8,128)} custom-call(f32[64,1536]{1,0:T(8,128)} %get-tuple-element.64.refs_0_, f32[64,1536]{1,0:T(8,128)} %copy-done.5, f32[64,1536]{1,0:T(8,128)} %copy-done.6, f32[64,1536]{1,0:T(8,128)} %copy-done.7, f32[64,1536]{1,0:T(8,128)} %copy-done.8, f32[64,1536]{1,0:T(8,128)} %collective-permute-done.11.refs_5_, ...), custom_call_target="tpu_custom_call" | custom-call | tf_op jit(solution)/shard_map/place/pallas_call | solution.py:99
  146.8 14.9 %collective-permute-done.2.refs_2_ = f32[64,2560]{1,0:T(8,128)S(1)} collective-permute-done((f32[64,2560]{1,0:T(8,128)}, f32[64,2560]{1,0:T(8,128)S(1)}, u32[]{:S(2)}, u32[]{:S(2)}) %collective-permute-start.2) | collective-permute-done | bytes 655392 | tf_op jit(solution)/shard_map/ppermute | solution.py:114
  162.8 3.9 %place.3 = f32[64,32768]{1,0:T(8,128)} custom-call(f32[64,2560]{1,0:T(8,128)} %copy-done, f32[64,2560]{1,0:T(8,128)} %copy-done.1, f32[64,2560]{1,0:T(8,128)} %copy-done.2, f32[64,2560]{1,0:T(8,128)} %copy-done.3, f32[64,2560]{1,0:T(8,128)} %collective-permute-done.4.refs_4_, ...), custom_call_target="tpu_custom_call", output_to_operand_aliasing={{}: (7, {})} | custom-call | tf_op jit(solution)/shard_map/place/pallas_call | solution.py:99
  (95 shorter events, 27.5 us)
Async XLA Ops:
  8.2 11.8 %all-to-all-start.2 = ((f32[8,16,512]{2,1,0:T(8,128)}), f32[8,16,512]{2,1,0:T(8,128)S(1)}, u32[]{:S(2)}, u32[]{:S(2)}) async-start(f32[8,16,512]{2,1,0:T(8,128)} %bitcast.7), calls=%async_computation.2 | async-start | bytes 524288 | tf_op jit(solution)/shard_map/all_to_all | solution.py:28
  21.9 55.3 %all-to-all-start.3 = ((f32[16,40,512]{2,1,0:T(8,128)}), f32[16,40,512]{2,1,0:T(8,128)S(1)}, u32[]{:S(2)}, u32[]{:S(2)}) async-start(f32[16,40,512]{2,1,0:T(8,128)} %broadcast_in_dim.137), calls=%async_computation.3 | async-start | bytes 2621440 | tf_op jit(solution)/shard_map/all_to_all | solution.py:28
  34.9 22.2 %collective-permute-start.7 = (f32[64,1536]{1,0:T(8,128)}, f32[64,1536]{1,0:T(8,128)S(1)}, u32[]{:S(2)}, u32[]{:S(2)}) collective-permute-start(f32[64,1536]{1,0:T(8,128)} %get-tuple-element.65), channel_id=1, source_target_pairs={{0,4},{1,5},{2,6},{3,7},{4,0},{5,1},{6,2},{7,3},{8,12},{9,13},{10,... | collective-permute-start | bytes 1179656 | tf_op jit(solution)/shard_map/ppermute | solution.py:114
  37.9 26.7 %collective-permute-start.8 = (f32[64,1536]{1,0:T(8,128)}, f32[64,1536]{1,0:T(8,128)S(1)}, u32[]{:S(2)}, u32[]{:S(2)}) collective-permute-start(f32[64,1536]{1,0:T(8,128)} %get-tuple-element.66), channel_id=1, source_target_pairs={{0,1},{1,2},{2,3},{3,0},{4,5},{5,6},{6,7},{7,4},{8,9},{9,10},{10,1... | collective-permute-start | bytes 1179656 | tf_op jit(solution)/shard_map/ppermute | solution.py:114
  39.4 35.4 %collective-permute-start.9 = (f32[64,1536]{1,0:T(8,128)}, f32[64,1536]{1,0:T(8,128)S(1)}, u32[]{:S(2)}, u32[]{:S(2)}) collective-permute-start(f32[64,1536]{1,0:T(8,128)} %get-tuple-element.67), channel_id=1, source_target_pairs={{0,3},{1,0},{2,1},{3,2},{4,7},{5,4},{6,5},{7,6},{8,11},{9,8},{10,9... | collective-permute-start | bytes 1179656 | tf_op jit(solution)/shard_map/ppermute | solution.py:114
  39.9 38.3 %collective-permute-start.10 = (f32[64,1536]{1,0:T(8,128)}, f32[64,1536]{1,0:T(8,128)S(1)}, u32[]{:S(2)}, u32[]{:S(2)}) collective-permute-start(f32[64,1536]{1,0:T(8,128)} %get-tuple-element.68), channel_id=1, source_target_pairs={{0,6},{1,7},{2,4},{3,5},{4,2},{5,3},{6,0},{7,1},{8,14},{9,15},{10,... | collective-permute-start | bytes 1179656 | tf_op jit(solution)/shard_map/ppermute | solution.py:114
  42.0 36.9 %collective-permute-start.11 = (f32[64,1536]{1,0:T(8,128)}, f32[64,1536]{1,0:T(8,128)}, u32[]{:S(2)}, u32[]{:S(2)}) collective-permute-start(f32[64,1536]{1,0:T(8,128)} %get-tuple-element.69), channel_id=1, source_target_pairs={{0,5},{1,6},{2,7},{3,4},{4,1},{5,2},{6,3},{7,0},{8,13},{9,14},{10,... | collective-permute-start | bytes 1179656 | tf_op jit(solution)/shard_map/ppermute | solution.py:114
  57.1 27.0 %collective-permute-start.12 = (f32[64,1536]{1,0:T(8,128)}, f32[64,1536]{1,0:T(8,128)}, u32[]{:S(2)}, u32[]{:S(2)}) collective-permute-start(f32[64,1536]{1,0:T(8,128)} %get-tuple-element.70), channel_id=1, source_target_pairs={{0,7},{1,4},{2,5},{3,6},{4,3},{5,0},{6,1},{7,2},{8,15},{9,12},{10,... | collective-permute-start | bytes 1179656 | tf_op jit(solution)/shard_map/ppermute | solution.py:114
  65.4 29.4 %collective-permute-start = (f32[64,2560]{1,0:T(8,128)}, f32[64,2560]{1,0:T(8,128)S(1)}, u32[]{:S(2)}, u32[]{:S(2)}) collective-permute-start(f32[64,2560]{1,0:T(8,128)} %get-tuple-element.57), channel_id=1, source_target_pairs={{0,4},{1,5},{2,6},{3,7},{4,0},{5,1},{6,2},{7,3},{8,12},{9,13},{10,... | collective-permute-start | bytes 1966088 | tf_op jit(solution)/shard_map/ppermute | solution.py:114
  74.8 13.7 %collective-permute-start.13 = (f32[64,1536]{1,0:T(8,128)}, f32[64,1536]{1,0:T(8,128)S(1)}, u32[]{:S(2)}, u32[]{:S(2)}) collective-permute-start(f32[64,1536]{1,0:T(8,128)} %get-tuple-element.71), channel_id=1, source_target_pairs={{0,2},{1,3},{2,0},{3,1},{4,6},{5,7},{6,4},{7,5},{8,10},{9,11},{10,... | collective-permute-start | bytes 1179656 | tf_op jit(solution)/shard_map/ppermute | solution.py:114
  78.2 21.8 %collective-permute-start.14 = (f32[256,512]{1,0:T(8,128)S(1)}, f32[256,512]{1,0:T(8,128)}, u32[]{:S(2)}, u32[]{:S(2)}) collective-permute-start(f32[256,512]{1,0:T(8,128)S(1)} %get-tuple-element.100.refs_0_), channel_id=1, source_target_pairs={{0,32},{32,64},{64,96},{96,0},{1,33},{33,65},{65,97},{97,1},{2,34}... | collective-permute-start | bytes 1572872 | tf_op jit(solution)/shard_map/ppermute | solution.py:264
  78.9 21.2 %collective-permute-start.15 = (f32[256,512]{1,0:T(8,128)S(1)}, f32[256,512]{1,0:T(8,128)}, u32[]{:S(2)}, u32[]{:S(2)}) collective-permute-start(f32[256,512]{1,0:T(8,128)S(1)} %get-tuple-element.100.refs_0_), channel_id=1, source_target_pairs={{0,96},{32,0},{64,32},{96,64},{1,97},{33,1},{65,33},{97,65},{2,98}... | collective-permute-start | bytes 1572872 | tf_op jit(solution)/shard_map/ppermute | solution.py:264
  84.1 16.4 %collective-permute-start.16 = (f32[256,512]{1,0:T(8,128)S(1)}, f32[256,512]{1,0:T(8,128)}, u32[]{:S(2)}, u32[]{:S(2)}) collective-permute-start(f32[256,512]{1,0:T(8,128)S(1)} %get-tuple-element.100.refs_0_), channel_id=1, source_target_pairs={{0,64},{32,96},{64,0},{96,32},{1,65},{33,97},{65,1},{97,33},{2,66}... | collective-permute-start | bytes 1572872 | tf_op jit(solution)/shard_map/ppermute | solution.py:264
  88.5 14.7 %collective-permute-start.1 = (f32[64,2560]{1,0:T(8,128)}, f32[64,2560]{1,0:T(8,128)S(1)}, u32[]{:S(2)}, u32[]{:S(2)}) collective-permute-start(f32[64,2560]{1,0:T(8,128)} %get-tuple-element.58), channel_id=1, source_target_pairs={{0,1},{1,2},{2,3},{3,0},{4,5},{5,6},{6,7},{7,4},{8,9},{9,10},{10,1... | collective-permute-start | bytes 1966088 | tf_op jit(solution)/shard_map/ppermute | solution.py:114
  94.7 10.5 %collective-permute-start.20 = (f32[256,512]{1,0:T(8,128)S(1)}, f32[256,512]{1,0:T(8,128)S(1)}, u32[]{:S(2)}, u32[]{:S(2)}) collective-permute-start(f32[256,512]{1,0:T(8,128)S(1)} %get-tuple-element.100.refs_0_), channel_id=1, source_target_pairs={{0,8},{8,0},{1,9},{9,1},{2,10},{10,2},{3,11},{11,3},{4,12},{12,4},... | collective-permute-start | bytes 1572872 | tf_op jit(solution)/shard_map/ppermute | solution.py:268
  100.0 6.8 %collective-permute-start.17 = (f32[256,512]{1,0:T(8,128)}, f32[256,512]{1,0:T(8,128)}, u32[]{:S(2)}, u32[]{:S(2)}) collective-permute-start(f32[256,512]{1,0:T(8,128)} %collective-permute-done.14.refs_0_), channel_id=1, source_target_pairs={{0,8},{8,0},{1,9},{9,1},{2,10},{10,2},{3,11},{11,3},{4,12},{12,4},... | collective-permute-start | bytes 1572872 | tf_op jit(solution)/shard_map/ppermute | solution.py:268
  100.0 11.6 %collective-permute-start.18 = (f32[256,512]{1,0:T(8,128)}, f32[256,512]{1,0:T(8,128)}, u32[]{:S(2)}, u32[]{:S(2)}) collective-permute-start(f32[256,512]{1,0:T(8,128)} %collective-permute-done.15.refs_1_), channel_id=1, source_target_pairs={{0,8},{8,0},{1,9},{9,1},{2,10},{10,2},{3,11},{11,3},{4,12},{12,4},... | collective-permute-start | bytes 1572872 | tf_op jit(solution)/shard_map/ppermute | solution.py:268
  100.5 11.1 %collective-permute-start.19 = (f32[256,512]{1,0:T(8,128)}, f32[256,512]{1,0:T(8,128)}, u32[]{:S(2)}, u32[]{:S(2)}) collective-permute-start(f32[256,512]{1,0:T(8,128)} %collective-permute-done.16.refs_2_), channel_id=1, source_target_pairs={{0,8},{8,0},{1,9},{9,1},{2,10},{10,2},{3,11},{11,3},{4,12},{12,4},... | collective-permute-start | bytes 1572872 | tf_op jit(solution)/shard_map/ppermute | solution.py:268
  103.2 58.5 %collective-permute-start.2 = (f32[64,2560]{1,0:T(8,128)}, f32[64,2560]{1,0:T(8,128)S(1)}, u32[]{:S(2)}, u32[]{:S(2)}) collective-permute-start(f32[64,2560]{1,0:T(8,128)} %get-tuple-element.59), channel_id=1, source_target_pairs={{0,3},{1,0},{2,1},{3,2},{4,7},{5,4},{6,5},{7,6},{8,11},{9,8},{10,9... | collective-permute-start | bytes 1966088 | tf_op jit(solution)/shard_map/ppermute | solution.py:114
  106.0 55.7 %collective-permute-start.3 = (f32[64,2560]{1,0:T(8,128)}, f32[64,2560]{1,0:T(8,128)S(1)}, u32[]{:S(2)}, u32[]{:S(2)}) collective-permute-start(f32[64,2560]{1,0:T(8,128)} %get-tuple-element.60), channel_id=1, source_target_pairs={{0,6},{1,7},{2,4},{3,5},{4,2},{5,3},{6,0},{7,1},{8,14},{9,15},{10,... | collective-permute-start | bytes 1966088 | tf_op jit(solution)/shard_map/ppermute | solution.py:114
  106.9 54.9 %collective-permute-start.4 = (f32[64,2560]{1,0:T(8,128)}, f32[64,2560]{1,0:T(8,128)}, u32[]{:S(2)}, u32[]{:S(2)}) collective-permute-start(f32[64,2560]{1,0:T(8,128)} %get-tuple-element.61), channel_id=1, source_target_pairs={{0,5},{1,6},{2,7},{3,4},{4,1},{5,2},{6,3},{7,0},{8,13},{9,14},{10,... | collective-permute-start | bytes 1966088 | tf_op jit(solution)/shard_map/ppermute | solution.py:114
  111.6 50.1 %collective-permute-start.5 = (f32[64,2560]{1,0:T(8,128)}, f32[64,2560]{1,0:T(8,128)}, u32[]{:S(2)}, u32[]{:S(2)}) collective-permute-start(f32[64,2560]{1,0:T(8,128)} %get-tuple-element.62), channel_id=1, source_target_pairs={{0,7},{1,4},{2,5},{3,6},{4,3},{5,0},{6,1},{7,2},{8,15},{9,12},{10,... | collective-permute-start | bytes 1966088 | tf_op jit(solution)/shard_map/ppermute | solution.py:114
  111.6 50.1 %collective-permute-start.6 = (f32[64,2560]{1,0:T(8,128)}, f32[64,2560]{1,0:T(8,128)}, u32[]{:S(2)}, u32[]{:S(2)}) collective-permute-start(f32[64,2560]{1,0:T(8,128)} %get-tuple-element.63), channel_id=1, source_target_pairs={{0,2},{1,3},{2,0},{3,1},{4,6},{5,7},{6,4},{7,5},{8,10},{9,11},{10,... | collective-permute-start | bytes 1966088 | tf_op jit(solution)/shard_map/ppermute | solution.py:114
  135.8 30.9 %all-to-all-start.4 = ((f32[128,1,16]{2,1,0:T(1,128)}), f32[128,1,16]{2,1,0:T(1,128)S(1)}, u32[]{:S(2)}, u32[]{:S(2)}) async-start(f32[128,1,16]{2,1,0:T(1,128)} %bitcast.18), calls=%async_computation.4 | async-start | bytes 131072 | tf_op jit(solution)/shard_map/all_to_all | solution.py:28
  (13 other events, 170.2 us)

commit v7 on v6

--- a/solution.py
+++ b/solution.py
@@ -119,7 +119,7 @@
     return lax.rem(lax.axis_index("x") + 4 - shift, 4) * 2 + (lax.axis_index("c") ^ side)
 
 
-def score_kernel(blocks, *refs):
+def score_kernel(blocks, weight, *refs):
     count = len(blocks)
     q_refs, e_refs, (lvl_ref, old_ref, o_ref, ql_ref, row_ref, acc_ref, ent_ref) = (
         refs[:count],
@@ -155,17 +155,17 @@
         o_ref[...] = old_ref[...]
         for k, block in enumerate(blocks):
             total = jnp.sum(acc_ref[:, k * piece : (k + 1) * piece], axis=0, keepdims=True)
-            o_ref[pl.ds(block_class(block), 1), :] = total
-
-
-def soft_counts(blocks, pieces, table, level, old):
+            o_ref[pl.ds(block_class(block), 1), :] = total * weight
+
+
+def soft_counts(blocks, weight, pieces, table, level, old):
     piece, width = pieces[0].shape
     queries = piece * len(pieces)
     rows = table.shape[0]
     eb = STEP // SPLIT
     whole = pl.BlockSpec(level.shape, lambda i: (0, 0))
     return pl.pallas_call(
-        functools.partial(score_kernel, blocks),
+        functools.partial(score_kernel, blocks, weight),
         grid=(rows // STEP,),
         in_specs=[pl.BlockSpec((piece, width), lambda i: (0, 0))] * len(pieces)
         + [pl.BlockSpec((eb, width), lambda i, j=j: (i * SPLIT + j, 0)) for j in range(SPLIT)]
@@ -272,9 +272,9 @@
     sums = jnp.zeros_like(level)
     for shifts in (SHIFTS[:1], SHIFTS[1:]):
         blocks = tuple((shift, side) for side in (0, 1) for shift in shifts)
-        sums = soft_counts(blocks, [held[b] for b in blocks], entity_table, level, sums)
+        sums = soft_counts(blocks, 1.0 / ents, [held[b] for b in blocks], entity_table, level, sums)
     got = exchange(sums.reshape(devices, home), ("x", "c", "yl", "yh", "z"))
-    fraction = jnp.sum(got, axis=0) * (1.0 / ents)
+    fraction = jnp.sum(got, axis=0)
 
     first, second = PARTS[0][0], PARTS[1][0]
     spots = tuple((k, first) for k in range(8)) + ((0, second),)

time: 168 us -> 168 us (level)
  no operation moved by 1% of the time
where the time goes in v7:
time: 168 us; the launch traced here: 167 us
  starting transfers between devices  54.3 us (32%)
  waiting for transfers between devices  50.4 us (30%)
  Pallas kernels  39.2 us (23%)
  local copies, waits for them, and re-layouts  16.7 us (10%)
  other arithmetic  4.51 us (3%)
  between operations  2.23 us (1%)
    ppermute x14, waiting for transfers between devices, hopped(): return lax.ppermute(part, DIM, way)  41 us
    ppermute x14, starting transfers between devices, hopped(): return lax.ppermute(part, DIM, way)  30.1 us
    all_to_all x3, starting transfers between devices, exchange(): return lax.all_to_all(value, axis, split_axis=0, concat_axis=0, tiled=True)  20 us
    pallas_call x2, Pallas kernels, soft_counts(): pl.pallas_call(functools.partial(score_kernel, blocks, weight), grid=(row...  19.6 us
    pallas_call x2, Pallas kernels, flipped(): pl.pallas_call(flip_kernel, grid=(length // BLK,), in_specs=[pl.BlockSpec...  12.3 us
    pallas_call x2, Pallas kernels, placed(): pl.pallas_call(functools.partial(place_kernel, spots, rows), in_specs=[pl...  7.28 us
    ppermute x3, waiting for transfers between devices, shards(): lax.ppermute(query, 'x', [(i, (i + shift) % 4) for i in range(4)])  5.3 us
    gather x1, local copies, waits for them, and re-layouts, shards(): jnp.take(entity_table, wanted, axis=0, mode='clip').reshape(8, CAP, width)  4.96 us
  transfers between devices with their start and end apart: 24, of which 8 were waited for; matrix products, arithmetic and copies ran while one was open for 4% of the time, Pallas kernels for 23%

profile of v7, /device:TPU:32, one launch (start us, length us, event | category | flops | bytes accessed | tf_op | source)
XLA Modules:
  0.0 167.4 jit_solution(13921527676127127327)
XLA Ops:
  3.3 5.0 %gather_fusion.3 = f32[128,512]{1,0:T(8,128)} fusion(f32[4096,512]{1,0:T(8,128)} %refs_13_.1, s32[1024]{0:T(1024)S(1)} %pad_clamp_fusion.4), kind=kCustom, calls=%fused_computation.3 | custom fusion | bytes 524800 | tf_op jit(solution)/shard_map/jit(_take)/gather | solution.py:230
  8.2 4.3 %all-to-all-start.2 = ((f32[8,16,512]{2,1,0:T(8,128)}), f32[8,16,512]{2,1,0:T(8,128)S(1)}, u32[]{:S(2)}, u32[]{:S(2)}) async-start(f32[8,16,512]{2,1,0:T(8,128)} %bitcast.7), calls=%async_computation.2 | async-start | bytes 524288 | tf_op jit(solution)/shard_map/all_to_all | solution.py:28
  15.9 4.1 %all-to-all-done.2 = f32[8,16,512]{2,1,0:T(8,128)S(1)} async-done(((f32[8,16,512]{2,1,0:T(8,128)}), f32[8,16,512]{2,1,0:T(8,128)S(1)}, u32[]{:S(2)}, u32[]{:S(2)}) %all-to-all-start.2) | async-done | bytes 262176 | tf_op jit(solution)/shard_map/all_to_all | solution.py:28
  21.9 8.1 %all-to-all-start.3 = ((f32[16,40,512]{2,1,0:T(8,128)}), f32[16,40,512]{2,1,0:T(8,128)S(1)}, u32[]{:S(2)}, u32[]{:S(2)}) async-start(f32[16,40,512]{2,1,0:T(8,128)} %broadcast_in_dim.137), calls=%async_computation.3 | async-start | bytes 2621440 | tf_op jit(solution)/shard_map/all_to_all | solution.py:28
  30.0 4.9 %flip.3 = (f32[64,1536]{1,0:T(8,128)}, f32[64,1536]{1,0:T(8,128)}, f32[64,1536]{1,0:T(8,128)}, f32[64,1536]{1,0:T(8,128)}, f32[64,1536]{1,0:T(8,128)}, /*index=5...) custom-call(f32[4096,512]{1,0:T(8,128)} %refs_13_.1), custom_call_target="tpu_custom_call" | custom-call | bytes 6291456 | tf_op jit(solution)/shard_map/flip/pallas_call | solution.py:61
  34.9 3.0 %collective-permute-start.7 = (f32[64,1536]{1,0:T(8,128)}, f32[64,1536]{1,0:T(8,128)S(1)}, u32[]{:S(2)}, u32[]{:S(2)}) collective-permute-start(f32[64,1536]{1,0:T(8,128)} %get-tuple-element.65), channel_id=1, source_target_pairs={{0,4},{1,5},{2,6},{3,7},{4,0},{5,1},{6,2},{7,3},{8,12},{9,13},{10,... | collective-permute-start | bytes 1179656 | tf_op jit(solution)/shard_map/ppermute | solution.py:114
  42.0 3.6 %collective-permute-start.11 = (f32[64,1536]{1,0:T(8,128)}, f32[64,1536]{1,0:T(8,128)}, u32[]{:S(2)}, u32[]{:S(2)}) collective-permute-start(f32[64,1536]{1,0:T(8,128)} %get-tuple-element.69), channel_id=1, source_target_pairs={{0,5},{1,6},{2,7},{3,4},{4,1},{5,2},{6,3},{7,0},{8,13},{9,14},{10,... | collective-permute-start | bytes 1179656 | tf_op jit(solution)/shard_map/ppermute | solution.py:114
  45.6 11.6 %collective-permute-done.7.refs_1_ = f32[64,1536]{1,0:T(8,128)S(1)} collective-permute-done((f32[64,1536]{1,0:T(8,128)}, f32[64,1536]{1,0:T(8,128)S(1)}, u32[]{:S(2)}, u32[]{:S(2)}) %collective-permute-start.7) | collective-permute-done | bytes 393248 | tf_op jit(solution)/shard_map/ppermute | solution.py:114
  57.2 7.4 %flip.2 = (f32[64,2560]{1,0:T(8,128)}, f32[64,2560]{1,0:T(8,128)}, f32[64,2560]{1,0:T(8,128)}, f32[64,2560]{1,0:T(8,128)}, f32[64,2560]{1,0:T(8,128)}, /*index=5...) custom-call(f32[4096,512]{1,0:T(8,128)} %refs_13_.1), custom_call_target="tpu_custom_call" | custom-call | bytes 10485760 | tf_op jit(solution)/shard_map/flip/pallas_call | solution.py:61
  65.4 6.9 %collective-permute-start = (f32[64,2560]{1,0:T(8,128)}, f32[64,2560]{1,0:T(8,128)S(1)}, u32[]{:S(2)}, u32[]{:S(2)}) collective-permute-start(f32[64,2560]{1,0:T(8,128)} %get-tuple-element.57), channel_id=1, source_target_pairs={{0,4},{1,5},{2,6},{3,7},{4,0},{5,1},{6,2},{7,3},{8,12},{9,13},{10,... | collective-permute-start | bytes 1966088 | tf_op jit(solution)/shard_map/ppermute | solution.py:114
  74.8 2.3 %collective-permute-start.13 = (f32[64,1536]{1,0:T(8,128)}, f32[64,1536]{1,0:T(8,128)S(1)}, u32[]{:S(2)}, u32[]{:S(2)}) collective-permute-start(f32[64,1536]{1,0:T(8,128)} %get-tuple-element.71), channel_id=1, source_target_pairs={{0,2},{1,3},{2,0},{3,1},{4,6},{5,7},{6,4},{7,5},{8,10},{9,11},{10,... | collective-permute-start | bytes 1179656 | tf_op jit(solution)/shard_map/ppermute | solution.py:114
  78.9 2.7 %collective-permute-start.15 = (f32[256,512]{1,0:T(8,128)S(1)}, f32[256,512]{1,0:T(8,128)}, u32[]{:S(2)}, u32[]{:S(2)}) collective-permute-start(f32[256,512]{1,0:T(8,128)S(1)} %get-tuple-element.100.refs_0_), channel_id=1, source_target_pairs={{0,96},{32,0},{64,32},{96,64},{1,97},{33,1},{65,33},{97,65},{2,98}... | collective-permute-start | bytes 1572872 | tf_op jit(solution)/shard_map/ppermute | solution.py:264
  81.5 2.6 %collective-permute-done.12.refs_6_ = f32[64,1536]{1,0:T(8,128)} collective-permute-done((f32[64,1536]{1,0:T(8,128)}, f32[64,1536]{1,0:T(8,128)}, u32[]{:S(2)}, u32[]{:S(2)}) %collective-permute-start.12) | collective-permute-done | bytes 393248 | tf_op jit(solution)/shard_map/ppermute | solution.py:114
  84.5 4.0 %collective-permute-done.13.refs_7_ = f32[64,1536]{1,0:T(8,128)S(1)} collective-permute-done((f32[64,1536]{1,0:T(8,128)}, f32[64,1536]{1,0:T(8,128)S(1)}, u32[]{:S(2)}, u32[]{:S(2)}) %collective-permute-start.13) | collective-permute-done | bytes 393248 | tf_op jit(solution)/shard_map/ppermute | solution.py:114
  88.6 6.2 %collective-permute-done.refs_0_ = f32[64,2560]{1,0:T(8,128)S(1)} collective-permute-done((f32[64,2560]{1,0:T(8,128)}, f32[64,2560]{1,0:T(8,128)S(1)}, u32[]{:S(2)}, u32[]{:S(2)}) %collective-permute-start) | collective-permute-done | bytes 655392 | tf_op jit(solution)/shard_map/ppermute | solution.py:114
  94.7 5.3 %collective-permute-done.14.refs_0_ = f32[256,512]{1,0:T(8,128)} collective-permute-done((f32[256,512]{1,0:T(8,128)S(1)}, f32[256,512]{1,0:T(8,128)}, u32[]{:S(2)}, u32[]{:S(2)}) %collective-permute-start.14) | collective-permute-done | bytes 524320 | tf_op jit(solution)/shard_map/ppermute | solution.py:264
  106.9 4.7 %collective-permute-start.4 = (f32[64,2560]{1,0:T(8,128)}, f32[64,2560]{1,0:T(8,128)}, u32[]{:S(2)}, u32[]{:S(2)}) collective-permute-start(f32[64,2560]{1,0:T(8,128)} %get-tuple-element.61), channel_id=1, source_target_pairs={{0,5},{1,6},{2,7},{3,4},{4,1},{5,2},{6,3},{7,0},{8,13},{9,14},{10,... | collective-permute-start | bytes 1966088 | tf_op jit(solution)/shard_map/ppermute | solution.py:114
  111.6 2.6 %collective-permute-start.6 = (f32[64,2560]{1,0:T(8,128)}, f32[64,2560]{1,0:T(8,128)}, u32[]{:S(2)}, u32[]{:S(2)}) collective-permute-start(f32[64,2560]{1,0:T(8,128)} %get-tuple-element.63), channel_id=1, source_target_pairs={{0,2},{1,3},{2,0},{3,1},{4,6},{5,7},{6,4},{7,5},{8,10},{9,11},{10,... | collective-permute-start | bytes 1966088 | tf_op jit(solution)/shard_map/ppermute | solution.py:114
  114.8 7.2 %soft_counts.2.refs_15_ = f32[8,256]{1,0:T(8,128)} custom-call(f32[256,512]{1,0:T(8,128)S(1)} %get-tuple-element.100.refs_0_, f32[256,512]{1,0:T(8,128)} %copy-done.4, f32[4096,512]{1,0:T(8,128)} %refs_13_.1, f32[4096,512]{1,0:T(8,128)} %refs_13_.1, f32[4096,512]{1,0:T(8,128)} %refs_13_.1, f32[4096,512]{1,0:T(8,128)} %refs_13_.1, f32[4096,512]{1,0:T(8,128)} %refs_13_.1, ...), custom_call_target="tpu_custom_call" | custom-call | flops 2147483648 | bytes 9437184 | tf_op jit(solution)/shard_map/soft_counts/pallas_call | solution.py:167
  122.0 12.4 %soft_counts.3 = f32[8,256]{1,0:T(8,128)} custom-call(f32[256,512]{1,0:T(8,128)} %collective-permute-done.14.refs_0_, f32[256,512]{1,0:T(8,128)} %collective-permute-done.15.refs_1_, f32[256,512]{1,0:T(8,128)} %collective-permute-done.16.refs_2_, f32[256,512]{1,0:T(8,128)} %collective-permute-done.17.refs_3_, f32[256,512]{1,0:T(8,128)} %collective-permute-done.18.refs_4_, ...), custom_call_target="tpu_custom_call" | custom-call | flops 6442450944 | bytes 11534336 | tf_op jit(solution)/shard_map/soft_counts/pallas_call | solution.py:167
  135.8 7.6 %all-to-all-start.4 = ((f32[128,1,16]{2,1,0:T(1,128)}), f32[128,1,16]{2,1,0:T(1,128)S(1)}, u32[]{:S(2)}, u32[]{:S(2)}) async-start(f32[128,1,16]{2,1,0:T(1,128)} %bitcast.18), calls=%async_computation.4 | async-start | bytes 131072 | tf_op jit(solution)/shard_map/all_to_all | solution.py:28
  143.4 3.4 %place.2.refs_7_ = f32[64,32768]{1,0:T(8,128)} custom-call(f32[64,1536]{1,0:T(8,128)} %get-tuple-element.64.refs_0_, f32[64,1536]{1,0:T(8,128)} %copy-done.5, f32[64,1536]{1,0:T(8,128)} %copy-done.6, f32[64,1536]{1,0:T(8,128)} %copy-done.7, f32[64,1536]{1,0:T(8,128)} %copy-done.8, f32[64,1536]{1,0:T(8,128)} %collective-permute-done.11.refs_5_, ...), custom_call_target="tpu_custom_call" | custom-call | tf_op jit(solution)/shard_map/place/pallas_call | solution.py:99
  146.8 15.0 %collective-permute-done.2.refs_2_ = f32[64,2560]{1,0:T(8,128)S(1)} collective-permute-done((f32[64,2560]{1,0:T(8,128)}, f32[64,2560]{1,0:T(8,128)S(1)}, u32[]{:S(2)}, u32[]{:S(2)}) %collective-permute-start.2) | collective-permute-done | bytes 655392 | tf_op jit(solution)/shard_map/ppermute | solution.py:114
  162.8 3.9 %place.3 = f32[64,32768]{1,0:T(8,128)} custom-call(f32[64,2560]{1,0:T(8,128)} %copy-done, f32[64,2560]{1,0:T(8,128)} %copy-done.1, f32[64,2560]{1,0:T(8,128)} %copy-done.2, f32[64,2560]{1,0:T(8,128)} %copy-done.3, f32[64,2560]{1,0:T(8,128)} %collective-permute-done.4.refs_4_, ...), custom_call_target="tpu_custom_call", output_to_operand_aliasing={{}: (7, {})} | custom-call | tf_op jit(solution)/shard_map/place/pallas_call | solution.py:99
  (94 shorter events, 27.5 us)
Async XLA Ops:
  8.2 11.8 %all-to-all-start.2 = ((f32[8,16,512]{2,1,0:T(8,128)}), f32[8,16,512]{2,1,0:T(8,128)S(1)}, u32[]{:S(2)}, u32[]{:S(2)}) async-start(f32[8,16,512]{2,1,0:T(8,128)} %bitcast.7), calls=%async_computation.2 | async-start | bytes 524288 | tf_op jit(solution)/shard_map/all_to_all | solution.py:28
  21.9 55.3 %all-to-all-start.3 = ((f32[16,40,512]{2,1,0:T(8,128)}), f32[16,40,512]{2,1,0:T(8,128)S(1)}, u32[]{:S(2)}, u32[]{:S(2)}) async-start(f32[16,40,512]{2,1,0:T(8,128)} %broadcast_in_dim.137), calls=%async_computation.3 | async-start | bytes 2621440 | tf_op jit(solution)/shard_map/all_to_all | solution.py:28
  34.9 22.2 %collective-permute-start.7 = (f32[64,1536]{1,0:T(8,128)}, f32[64,1536]{1,0:T(8,128)S(1)}, u32[]{:S(2)}, u32[]{:S(2)}) collective-permute-start(f32[64,1536]{1,0:T(8,128)} %get-tuple-element.65), channel_id=1, source_target_pairs={{0,4},{1,5},{2,6},{3,7},{4,0},{5,1},{6,2},{7,3},{8,12},{9,13},{10,... | collective-permute-start | bytes 1179656 | tf_op jit(solution)/shard_map/ppermute | solution.py:114
  37.9 26.7 %collective-permute-start.8 = (f32[64,1536]{1,0:T(8,128)}, f32[64,1536]{1,0:T(8,128)S(1)}, u32[]{:S(2)}, u32[]{:S(2)}) collective-permute-start(f32[64,1536]{1,0:T(8,128)} %get-tuple-element.66), channel_id=1, source_target_pairs={{0,1},{1,2},{2,3},{3,0},{4,5},{5,6},{6,7},{7,4},{8,9},{9,10},{10,1... | collective-permute-start | bytes 1179656 | tf_op jit(solution)/shard_map/ppermute | solution.py:114
  39.4 35.4 %collective-permute-start.9 = (f32[64,1536]{1,0:T(8,128)}, f32[64,1536]{1,0:T(8,128)S(1)}, u32[]{:S(2)}, u32[]{:S(2)}) collective-permute-start(f32[64,1536]{1,0:T(8,128)} %get-tuple-element.67), channel_id=1, source_target_pairs={{0,3},{1,0},{2,1},{3,2},{4,7},{5,4},{6,5},{7,6},{8,11},{9,8},{10,9... | collective-permute-start | bytes 1179656 | tf_op jit(solution)/shard_map/ppermute | solution.py:114
  39.9 38.3 %collective-permute-start.10 = (f32[64,1536]{1,0:T(8,128)}, f32[64,1536]{1,0:T(8,128)S(1)}, u32[]{:S(2)}, u32[]{:S(2)}) collective-permute-start(f32[64,1536]{1,0:T(8,128)} %get-tuple-element.68), channel_id=1, source_target_pairs={{0,6},{1,7},{2,4},{3,5},{4,2},{5,3},{6,0},{7,1},{8,14},{9,15},{10,... | collective-permute-start | bytes 1179656 | tf_op jit(solution)/shard_map/ppermute | solution.py:114
  42.0 36.9 %collective-permute-start.11 = (f32[64,1536]{1,0:T(8,128)}, f32[64,1536]{1,0:T(8,128)}, u32[]{:S(2)}, u32[]{:S(2)}) collective-permute-start(f32[64,1536]{1,0:T(8,128)} %get-tuple-element.69), channel_id=1, source_target_pairs={{0,5},{1,6},{2,7},{3,4},{4,1},{5,2},{6,3},{7,0},{8,13},{9,14},{10,... | collective-permute-start | bytes 1179656 | tf_op jit(solution)/shard_map/ppermute | solution.py:114
  57.1 27.0 %collective-permute-start.12 = (f32[64,1536]{1,0:T(8,128)}, f32[64,1536]{1,0:T(8,128)}, u32[]{:S(2)}, u32[]{:S(2)}) collective-permute-start(f32[64,1536]{1,0:T(8,128)} %get-tuple-element.70), channel_id=1, source_target_pairs={{0,7},{1,4},{2,5},{3,6},{4,3},{5,0},{6,1},{7,2},{8,15},{9,12},{10,... | collective-permute-start | bytes 1179656 | tf_op jit(solution)/shard_map/ppermute | solution.py:114
  65.4 29.4 %collective-permute-start = (f32[64,2560]{1,0:T(8,128)}, f32[64,2560]{1,0:T(8,128)S(1)}, u32[]{:S(2)}, u32[]{:S(2)}) collective-permute-start(f32[64,2560]{1,0:T(8,128)} %get-tuple-element.57), channel_id=1, source_target_pairs={{0,4},{1,5},{2,6},{3,7},{4,0},{5,1},{6,2},{7,3},{8,12},{9,13},{10,... | collective-permute-start | bytes 1966088 | tf_op jit(solution)/shard_map/ppermute | solution.py:114
  74.8 13.7 %collective-permute-start.13 = (f32[64,1536]{1,0:T(8,128)}, f32[64,1536]{1,0:T(8,128)S(1)}, u32[]{:S(2)}, u32[]{:S(2)}) collective-permute-start(f32[64,1536]{1,0:T(8,128)} %get-tuple-element.71), channel_id=1, source_target_pairs={{0,2},{1,3},{2,0},{3,1},{4,6},{5,7},{6,4},{7,5},{8,10},{9,11},{10,... | collective-permute-start | bytes 1179656 | tf_op jit(solution)/shard_map/ppermute | solution.py:114
  78.2 21.8 %collective-permute-start.14 = (f32[256,512]{1,0:T(8,128)S(1)}, f32[256,512]{1,0:T(8,128)}, u32[]{:S(2)}, u32[]{:S(2)}) collective-permute-start(f32[256,512]{1,0:T(8,128)S(1)} %get-tuple-element.100.refs_0_), channel_id=1, source_target_pairs={{0,32},{32,64},{64,96},{96,0},{1,33},{33,65},{65,97},{97,1},{2,34}... | collective-permute-start | bytes 1572872 | tf_op jit(solution)/shard_map/ppermute | solution.py:264
  78.9 21.2 %collective-permute-start.15 = (f32[256,512]{1,0:T(8,128)S(1)}, f32[256,512]{1,0:T(8,128)}, u32[]{:S(2)}, u32[]{:S(2)}) collective-permute-start(f32[256,512]{1,0:T(8,128)S(1)} %get-tuple-element.100.refs_0_), channel_id=1, source_target_pairs={{0,96},{32,0},{64,32},{96,64},{1,97},{33,1},{65,33},{97,65},{2,98}... | collective-permute-start | bytes 1572872 | tf_op jit(solution)/shard_map/ppermute | solution.py:264
  84.1 16.4 %collective-permute-start.16 = (f32[256,512]{1,0:T(8,128)S(1)}, f32[256,512]{1,0:T(8,128)}, u32[]{:S(2)}, u32[]{:S(2)}) collective-permute-start(f32[256,512]{1,0:T(8,128)S(1)} %get-tuple-element.100.refs_0_), channel_id=1, source_target_pairs={{0,64},{32,96},{64,0},{96,32},{1,65},{33,97},{65,1},{97,33},{2,66}... | collective-permute-start | bytes 1572872 | tf_op jit(solution)/shard_map/ppermute | solution.py:264
  88.5 14.7 %collective-permute-start.1 = (f32[64,2560]{1,0:T(8,128)}, f32[64,2560]{1,0:T(8,128)S(1)}, u32[]{:S(2)}, u32[]{:S(2)}) collective-permute-start(f32[64,2560]{1,0:T(8,128)} %get-tuple-element.58), channel_id=1, source_target_pairs={{0,1},{1,2},{2,3},{3,0},{4,5},{5,6},{6,7},{7,4},{8,9},{9,10},{10,1... | collective-permute-start | bytes 1966088 | tf_op jit(solution)/shard_map/ppermute | solution.py:114
  94.7 10.5 %collective-permute-start.20 = (f32[256,512]{1,0:T(8,128)S(1)}, f32[256,512]{1,0:T(8,128)S(1)}, u32[]{:S(2)}, u32[]{:S(2)}) collective-permute-start(f32[256,512]{1,0:T(8,128)S(1)} %get-tuple-element.100.refs_0_), channel_id=1, source_target_pairs={{0,8},{8,0},{1,9},{9,1},{2,10},{10,2},{3,11},{11,3},{4,12},{12,4},... | collective-permute-start | bytes 1572872 | tf_op jit(solution)/shard_map/ppermute | solution.py:268
  100.0 6.8 %collective-permute-start.17 = (f32[256,512]{1,0:T(8,128)}, f32[256,512]{1,0:T(8,128)}, u32[]{:S(2)}, u32[]{:S(2)}) collective-permute-start(f32[256,512]{1,0:T(8,128)} %collective-permute-done.14.refs_0_), channel_id=1, source_target_pairs={{0,8},{8,0},{1,9},{9,1},{2,10},{10,2},{3,11},{11,3},{4,12},{12,4},... | collective-permute-start | bytes 1572872 | tf_op jit(solution)/shard_map/ppermute | solution.py:268
  100.0 11.6 %collective-permute-start.18 = (f32[256,512]{1,0:T(8,128)}, f32[256,512]{1,0:T(8,128)}, u32[]{:S(2)}, u32[]{:S(2)}) collective-permute-start(f32[256,512]{1,0:T(8,128)} %collective-permute-done.15.refs_1_), channel_id=1, source_target_pairs={{0,8},{8,0},{1,9},{9,1},{2,10},{10,2},{3,11},{11,3},{4,12},{12,4},... | collective-permute-start | bytes 1572872 | tf_op jit(solution)/shard_map/ppermute | solution.py:268
  100.5 11.1 %collective-permute-start.19 = (f32[256,512]{1,0:T(8,128)}, f32[256,512]{1,0:T(8,128)}, u32[]{:S(2)}, u32[]{:S(2)}) collective-permute-start(f32[256,512]{1,0:T(8,128)} %collective-permute-done.16.refs_2_), channel_id=1, source_target_pairs={{0,8},{8,0},{1,9},{9,1},{2,10},{10,2},{3,11},{11,3},{4,12},{12,4},... | collective-permute-start | bytes 1572872 | tf_op jit(solution)/shard_map/ppermute | solution.py:268
  103.2 58.5 %collective-permute-start.2 = (f32[64,2560]{1,0:T(8,128)}, f32[64,2560]{1,0:T(8,128)S(1)}, u32[]{:S(2)}, u32[]{:S(2)}) collective-permute-start(f32[64,2560]{1,0:T(8,128)} %get-tuple-element.59), channel_id=1, source_target_pairs={{0,3},{1,0},{2,1},{3,2},{4,7},{5,4},{6,5},{7,6},{8,11},{9,8},{10,9... | collective-permute-start | bytes 1966088 | tf_op jit(solution)/shard_map/ppermute | solution.py:114
  106.0 55.7 %collective-permute-start.3 = (f32[64,2560]{1,0:T(8,128)}, f32[64,2560]{1,0:T(8,128)S(1)}, u32[]{:S(2)}, u32[]{:S(2)}) collective-permute-start(f32[64,2560]{1,0:T(8,128)} %get-tuple-element.60), channel_id=1, source_target_pairs={{0,6},{1,7},{2,4},{3,5},{4,2},{5,3},{6,0},{7,1},{8,14},{9,15},{10,... | collective-permute-start | bytes 1966088 | tf_op jit(solution)/shard_map/ppermute | solution.py:114
  106.9 54.9 %collective-permute-start.4 = (f32[64,2560]{1,0:T(8,128)}, f32[64,2560]{1,0:T(8,128)}, u32[]{:S(2)}, u32[]{:S(2)}) collective-permute-start(f32[64,2560]{1,0:T(8,128)} %get-tuple-element.61), channel_id=1, source_target_pairs={{0,5},{1,6},{2,7},{3,4},{4,1},{5,2},{6,3},{7,0},{8,13},{9,14},{10,... | collective-permute-start | bytes 1966088 | tf_op jit(solution)/shard_map/ppermute | solution.py:114
  111.6 50.1 %collective-permute-start.5 = (f32[64,2560]{1,0:T(8,128)}, f32[64,2560]{1,0:T(8,128)}, u32[]{:S(2)}, u32[]{:S(2)}) collective-permute-start(f32[64,2560]{1,0:T(8,128)} %get-tuple-element.62), channel_id=1, source_target_pairs={{0,7},{1,4},{2,5},{3,6},{4,3},{5,0},{6,1},{7,2},{8,15},{9,12},{10,... | collective-permute-start | bytes 1966088 | tf_op jit(solution)/shard_map/ppermute | solution.py:114
  111.6 50.1 %collective-permute-start.6 = (f32[64,2560]{1,0:T(8,128)}, f32[64,2560]{1,0:T(8,128)}, u32[]{:S(2)}, u32[]{:S(2)}) collective-permute-start(f32[64,2560]{1,0:T(8,128)} %get-tuple-element.63), channel_id=1, source_target_pairs={{0,2},{1,3},{2,0},{3,1},{4,6},{5,7},{6,4},{7,5},{8,10},{9,11},{10,... | collective-permute-start | bytes 1966088 | tf_op jit(solution)/shard_map/ppermute | solution.py:114
  135.8 30.9 %all-to-all-start.4 = ((f32[128,1,16]{2,1,0:T(1,128)}), f32[128,1,16]{2,1,0:T(1,128)S(1)}, u32[]{:S(2)}, u32[]{:S(2)}) async-start(f32[128,1,16]{2,1,0:T(1,128)} %bitcast.18), calls=%async_computation.4 | async-start | bytes 131072 | tf_op jit(solution)/shard_map/all_to_all | solution.py:28
  (13 other events, 170.2 us)
